TPU v7x, 32 devices: a whole 2x2x4 slice. The times are simulated.
32 devices in a mesh: fsdp: 8 (over y, x, core), model: 4 (over z).
Axes of the slice: x: 2, y: 2, z: 4, core: 2. Of those that a mesh axis runs over, the one named last changes fastest.
Arguments:
- w_query: float32 [4096, 4096], P('fsdp', 'model'), may hold values from -0.125 to 0.125
- first_query: float32 [4096, 4096], P('fsdp', 'model'), may hold values from -0.09375 to 0.09375
- second_query: float32 [4096, 4096], P('fsdp', 'model'), may hold values from -0.09375 to 0.09375
- w_key: float32 [4096, 4096], P('fsdp', 'model'), may hold values from -0.125 to 0.125
- first_key: float32 [4096, 4096], P('fsdp', 'model'), may hold values from -0.09375 to 0.09375
- second_key: float32 [4096, 4096], P('fsdp', 'model'), may hold values from -0.09375 to 0.09375
- w_value: float32 [4096, 4096], P('fsdp', 'model'), may hold values from -0.125 to 0.125
- first_value: float32 [4096, 4096], P('fsdp', 'model'), may hold values from -0.09375 to 0.09375
- second_value: float32 [4096, 4096], P('fsdp', 'model'), may hold values from -0.09375 to 0.09375
- norm_gain: float32 [4096], P('fsdp'), may hold values from 0.25 to 1.75
Outputs:
- ready_query: bfloat16 [4096, 4096], P(None, 'model')
- ready_key: bfloat16 [4096, 4096], P(None, 'model')
- ready_value: bfloat16 [4096, 4096], P(None, 'model')
- factor_query: float32 [4096], P('model')
- factor_key: float32 [4096], P('model')
- factor_value: float32 [4096], P('model')
All inputs are finite; a program needn't handle non-finite values. Where the computation divides by a largest or mean magnitude, that divisor is 1e-20 or more.
Results may differ from a plain program's by a relative error of at most 0.001.
Values may be sent and summed in bfloat16 or wider, within the bound.
No kernel may reach another device: no remote copies, remote signals or barrier semaphores. Data moves between devices by JAX's collectives and lax.ppermute only.
A program may use at most 128 MiB of HBM per device.

v0:
```python
import functools
import math

import jax
import jax.numpy as jnp
from jax import lax
from jax.experimental import pallas as pl
from jax.experimental.pallas import tpu as pltpu
from jax.sharding import PartitionSpec as P


learn_rate = 0.2
hold_rate = 0.9

VMEM_LIMIT = 16 * 1024 * 1024
LANES = 128


def swap(value, mask, n):
    return lax.ppermute(value, "fsdp", [(i, i ^ mask) for i in range(n)])


def hbm(value):
    return pltpu.with_memory_space_constraint(value, pltpu.HBM)


def step_rows(rows):
    return math.gcd(rows, 64)


def gain_columns(gain_ref, start, rows, slab):
    at = start // LANES
    row = jnp.broadcast_to(gain_ref[:, pl.ds(pl.multiple_of(at * LANES, LANES), LANES)], (slab, LANES))
    lane = lax.broadcasted_iota(jnp.int32, (slab, LANES), 1)
    place_of = lax.broadcasted_iota(jnp.int32, (slab, LANES), 0) + (start - at * LANES)
    return [
        jnp.sum(jnp.where(lane == place_of + r, row, 0.0), axis=1, keepdims=True)
        for r in range(0, rows, slab)
    ]


def lane_groups(cols):
    return [slice(at, at + LANES) for at in range(0, cols, LANES)]


def update_kernel(count, chunk, gain_ref, *refs):
    ins, kept, sums = refs[: 3 * count], refs[3 * count : 4 * count], refs[4 * count]
    held, (acc_ref, column_ref, sems) = refs[4 * count + 1 : -3], refs[-3:]
    rows, cols = kept[0].shape
    chunks = rows // chunk

    def copy(c, j):
        at = pl.ds(pl.multiple_of(c * chunk, 8), chunk)
        return pltpu.make_async_copy(ins[j].at[at], held[j].at[at], sems.at[c, j])

    for c in range(chunks):
        for j in range(3 * count):
            copy(c, j).start()
    acc_ref[...] = jnp.zeros_like(acc_ref)
    for start in range(0, rows, chunk):
        for i, column in enumerate(gain_columns(gain_ref, start, chunk, 8)):
            column_ref[start + 8 * i : start + 8 * i + 8, :] = jnp.broadcast_to(column, (8, LANES))

    def work(c, _):
        spots = [pl.ds(pl.multiple_of(c * chunk + r, 8), 8) for r in range(0, chunk, 8)]
        columns = [column_ref[at, :] for at in spots]
        for t in range(count):
            w, first, second = held[3 * t : 3 * t + 3]
            for j in range(3 * t, 3 * t + 3):
                copy(c, j).wait()
            for lanes in lane_groups(cols):
                acc = acc_ref[t, :, lanes]
                for at, column in zip(spots, columns):
                    hold = hold_rate * first[at, lanes] + second[at, lanes]
                    gained = (w[at, lanes] - learn_rate * hold) * column
                    kept[t][at, lanes] = gained
                    acc += jnp.abs(gained)
                acc_ref[t, :, lanes] = acc
        return _

    lax.fori_loop(0, chunks, work, 0)
    for t in range(count):
        sums[t : t + 1, :] = jnp.sum(acc_ref[t], axis=0, keepdims=True)


def update(triples, gain_row):
    rows, cols = triples[0][0].shape
    chunk = step_rows(rows)
    count = len(triples)
    size = rows * cols * count
    *gained, sums = pl.pallas_call(
        functools.partial(update_kernel, count, chunk),
        in_specs=[pl.BlockSpec(memory_space=pltpu.VMEM)]
        + [pl.BlockSpec(memory_space=pltpu.HBM)] * (3 * count),
        out_specs=[pl.BlockSpec(memory_space=pltpu.VMEM)] * (count + 1),
        out_shape=[jax.ShapeDtypeStruct((rows, cols), jnp.float32)] * count
        + [jax.ShapeDtypeStruct((count, cols), jnp.float32)],
        scratch_shapes=[pltpu.VMEM((rows, cols), jnp.float32)] * (3 * count)
        + [
            pltpu.VMEM((count, 8, cols), jnp.float32),
            pltpu.VMEM((rows, LANES), jnp.float32),
            pltpu.SemaphoreType.DMA((rows // chunk, 3 * count)),
        ],
        compiler_params=pltpu.CompilerParams(vmem_limit_bytes=VMEM_LIMIT),
        cost_estimate=pl.CostEstimate(flops=8 * size, bytes_accessed=12 * size, transcendentals=0),
        name="update",
    )(gain_row, *[hbm(a) for triple in triples for a in triple])
    return gained, sums


def mean_of(index, rows_all, me_ref, totals, roles):
    values = [r[index : index + 1, :] for r in totals]
    even = (me_ref[0] & 1) == 0
    if roles == "fast":
        own, got, other, across = values
        values = [own, jnp.where(even, got, other), across, jnp.where(even, other, got)]
    if roles == "aside":
        own, got, other, both, passed = values
        values = [
            own,
            jnp.where(even, got, other),
            jnp.where(even, other, got),
            jnp.where(even, passed, both),
        ]
    while len(values) > 1:
        values = [a + b for a, b in zip(values[::2], values[1::2])]
    return values[0] / rows_all


def narrow_kernel(index, count, rows_all, edges, roles, me_ref, *refs):
    totals, block, pieces = refs[:count], refs[count], refs[count + 1 : -2]
    factor, scale = refs[-2:]
    rows, cols = block.shape
    step = pl.program_id(0)

    @pl.when(step == 0)
    def _():
        mean = mean_of(index, rows_all, me_ref, totals, roles)
        factor[...] = mean
        scale[...] = 1.0 / mean

    def write(piece):
        for lanes in lane_groups(cols):
            by = scale[:, lanes]
            for r in range(0, rows, 16):
                piece[r : r + 16, lanes] = (block[r : r + 16, lanes] * by).astype(jnp.bfloat16)

    for p, piece in enumerate(pieces):
        pl.when((step >= edges[p]) & (step < edges[p + 1]))(functools.partial(write, piece))


def narrow(gained, totals, roles, index, me, n, sizes):
    rows, cols = gained.shape
    br = math.gcd(step_rows(rows), *sizes)
    edges = [sum(sizes[:p]) // br for p in range(len(sizes) + 1)]
    size = rows * cols

    def piece_spec(p):
        return pl.BlockSpec((br, cols), lambda i: (jnp.clip(i - edges[p], 0, edges[p + 1] - edges[p] - 1), 0))

    *pieces, factor = pl.pallas_call(
        functools.partial(narrow_kernel, index, len(totals), float(n * rows), edges, roles),
        grid=(rows // br,),
        in_specs=[pl.BlockSpec(memory_space=pltpu.SMEM)]
        + [pl.BlockSpec(t.shape, lambda i: (0, 0)) for t in totals]
        + [pl.BlockSpec((br, cols), lambda i: (i, 0))],
        out_specs=[piece_spec(p) for p in range(len(sizes))] + [pl.BlockSpec((1, cols), lambda i: (0, 0))],
        out_shape=[jax.ShapeDtypeStruct((s, cols), jnp.bfloat16) for s in sizes]
        + [jax.ShapeDtypeStruct((1, cols), jnp.float32)],
        scratch_shapes=[pltpu.VMEM((1, cols), jnp.float32)],
        compiler_params=pltpu.CompilerParams(vmem_limit_bytes=VMEM_LIMIT),
        cost_estimate=pl.CostEstimate(flops=8 * size, bytes_accessed=6 * size, transcendentals=0),
        name="narrow",
    )(me, *totals, gained)
    return pieces, factor.reshape(cols)


def place_kernel(spots, rows, held, me_ref, *refs):
    pieces, out, sems = refs[held : held + len(spots)], refs[-2], refs[-1]
    copies = []
    for i, (offset, start) in enumerate(spots):
        at = pl.multiple_of((me_ref[0] ^ offset) * rows + start, 16)
        copies.append(
            pltpu.make_async_copy(pieces[i], out.at[pl.ds(at, pieces[i].shape[0])], sems.at[i])
        )
        copies[-1].start()
    for copy in copies:
        copy.wait()


def place(out, me, n, rows, items):
    spots = tuple((offset, start) for offset, start, _ in items)
    pieces = [piece for _, _, piece in items]
    size = sum(piece.size for piece in pieces)
    held = [] if out is None else [out]
    return pl.pallas_call(
        functools.partial(place_kernel, spots, rows, len(held)),
        in_specs=[pl.BlockSpec(memory_space=pltpu.SMEM)]
        + [pl.BlockSpec(memory_space=pltpu.HBM)] * len(held)
        + [pl.BlockSpec(memory_space=pltpu.VMEM)] * len(pieces),
        out_specs=pl.BlockSpec(memory_space=pltpu.HBM),
        out_shape=jax.ShapeDtypeStruct((n * rows, pieces[0].shape[1]), pieces[0].dtype),
        input_output_aliases={1: 0} if held else {},
        scratch_shapes=[pltpu.SemaphoreType.DMA((len(pieces),))],
        compiler_params=pltpu.CompilerParams(vmem_limit_bytes=VMEM_LIMIT),
        cost_estimate=pl.CostEstimate(flops=size, bytes_accessed=4 * size, transcendentals=0),
        name="place",
    )(me, *held, *pieces)


def send(mask, piece, n):
    return swap(piece, mask, n)


def send_first(pieces, plan, masks, n):
    sent = []
    for p, (_, turn) in enumerate(plan):
        for s in range(len(masks)):
            mask = masks[(turn + s) % len(masks)]
            sent.append((mask, p, s, send(mask, pieces[p], n)))
    return sent


def send_onward(first, plan, masks, n):
    later, level = [], first
    while level:
        following = []
        for offset, p, at, piece in level:
            for step in range(at + 1, len(masks)):
                mask = masks[(plan[p][1] + step) % len(masks)]
                following.append((offset ^ mask, p, step, send(mask, piece, n)))
        level = following
        later += level
    return later


def assemble(pieces, first, later, plan, me, n):
    starts = [sum(size for size, _ in plan[:p]) for p in range(len(plan) + 1)]
    stages = [
        [(0, starts[p], x) for p, x in enumerate(pieces)] + [(o, starts[p], x) for o, p, _, x in first],
        [(1, starts[p], send(1, x, n)) for p, x in enumerate(pieces)]
        + [(o ^ 1, starts[p], send(1, x, n)) for o, p, _, x in first],
        [(o, starts[p], x) for o, p, _, x in later],
        [(o ^ 1, starts[p], send(1, x, n)) for o, p, _, x in later],
    ]
    out = None
    for items in stages:
        if items:
            out = place(out, me, n, starts[-1], items)
    return out


def chip_totals(sums, n, aside):
    chip = sums + swap(sums, 1, n)
    if n.bit_length() != 4:
        return [chip] + [swap(chip, 2 * o, n) for o in range(1, n // 2)], "all"
    if aside:
        got = lax.ppermute(chip, "fsdp", [(i, i ^ (4 if i & 1 else 2)) for i in range(n)])
        both = lax.ppermute(chip, "fsdp", [(i, i ^ 6) for i in range(n) if i & 1])
    else:
        got = lax.ppermute(chip, "fsdp", [(i, i ^ (6 if i & 1 else 2)) for i in range(n)])
        across = swap(chip, 4, n)
    other = send(1, got, n)
    if aside:
        return [chip, got, other, both, send(1, both, n)], "aside"
    return [chip, got, other, across], "fast"


def plans_for(rows, links, count):
    if links == 2 and rows % 128 == 0:
        long, half = rows * 5 // 8, rows // 2
        return [[(long, 0), (rows - long, 1)], [(long, 1), (rows - long, 0)], [(half, 0), (half, 1)]]
    return [[(rows // links, p) for p in range(links)]] * count


def solution(mesh):
    n = mesh.shape["fsdp"]
    links = n.bit_length() - 2
    masks = [2 << j for j in range(links)]

    def on_device(wq, fq, sq, wk, fk, sk, wv, fv, sv, norm_gain):
        me = lax.axis_index("fsdp").astype(jnp.int32).reshape(1)
        gain_row = hbm(norm_gain[None, :])
        plans = plans_for(wq.shape[0], links, 3)
        sizes = [[size for size, _ in plan] for plan in plans]
        gained, sums = update([(wq, fq, sq)], gain_row)
        totals, roles = chip_totals(sums, n, False)
        pieces, factor = narrow(gained[0], totals, roles, 0, me, n, sizes[0])
        gained, sums = update([(wk, fk, sk), (wv, fv, sv)], gain_row)
        totals, roles = chip_totals(sums, n, True)
        narrowed = [
            narrow(g, totals, roles, t, me, n, sizes[t + 1]) for t, g in enumerate(gained)
        ]
        pieces = [pieces, narrowed[0][0], narrowed[1][0]]
        outs = []
        for t, plan in enumerate(plans):
            first = send_first(pieces[t], plan, masks, n)
            later = send_onward(first, plan, masks, n)
            outs.append(assemble(pieces[t], first, later, plan, me, n))
        return (*outs, factor, narrowed[0][1], narrowed[1][1])

    return jax.shard_map(
        on_device,
        mesh=mesh,
        in_specs=(P("fsdp", "model"),) * 9 + (P("fsdp"),),
        out_specs=(P(None, "model"),) * 3 + (P("model"),) * 3,
        check_vma=False,
    )
```

profile of v0, /device:TPU:0, one launch (start us, length us, event | category | flops | bytes accessed | tf_op | source)
XLA Modules:
  0.0 156.4 jit_solution(1505301798281687456)
XLA Ops:
  0.6 3.7 %update.2 = (f32[512,1024]{1,0:T(8,128)S(1)}, f32[1,1024]{1,0:T(1,128)S(1)}) custom-call(f32[1,512]{1,0:T(1,128)} %bitcast.5, f32[512,1024]{1,0:T(8,128)} %refs_0_.2, f32[512,1024]{1,0:T(8,128)} %refs_1_.2, f32[512,1024]{1,0:T(8,128)} %refs_2_.2), custom_call_target="tpu_custom_call" | custom-call | flops 4194304 | bytes 6291456 | tf_op jit(solution)/shard_map/update/pallas_call | solution.py:91
  4.4 0.6 collective-permute-start
  4.9 0.8 collective-permute-done
  5.8 2.8 %collective-permute-start.1 = (f32[1,1024]{1,0:T(1,128)S(1)}, f32[1,1024]{1,0:T(1,128)S(1)}, u32[]{:S(2)}, u32[]{:S(2)}) collective-permute-start(f32[1,1024]{1,0:T(1,128)S(1)} %add.6.refs_0_), channel_id=1, source_target_pairs={{0,8},{4,28},{8,0},{12,20},{16,24},{20,12},{24,16},{28,4},{1,9},{5... | collective-permute-start | bytes 12296 | tf_op jit(solution)/shard_map/ppermute | solution.py:261
  8.6 1.5 collective-permute-start.3
  10.4 1.8 %collective-permute-done.3.refs_3_ = f32[1,1024]{1,0:T(1,128)S(1)} collective-permute-done((f32[1,1024]{1,0:T(1,128)S(1)}, f32[1,1024]{1,0:T(1,128)S(1)}, u32[]{:S(2)}, u32[]{:S(2)}) %collective-permute-start.3) | collective-permute-done | bytes 4128 | tf_op jit(solution)/shard_map/ppermute | solution.py:20
  12.2 1.0 narrow.3
  13.2 1.5 collective-permute-start.6
  14.7 1.2 collective-permute-start.7
  15.9 5.7 %update.3 = (f32[512,1024]{1,0:T(8,128)S(1)}, f32[512,1024]{1,0:T(8,128)S(1)}, f32[2,1024]{1,0:T(2,128)S(1)}) custom-call(f32[1,512]{1,0:T(1,128)} %bitcast.6, f32[512,1024]{1,0:T(8,128)} %refs_0_.3, f32[512,1024]{1,0:T(8,128)} %refs_1_.3, f32[512,1024]{1,0:T(8,128)} %refs_2_.3, f32[512,1024]{1,0:T(8,128)} %refs_3_.1, f32[512,1024]{1,0:T(8,128)} %refs_4_.1, ...), custom_call_target="tpu_custom_call" | custom-call | flops 8388608 | bytes 12582912 | tf_op jit(solution)/shard_map/update/pallas_call | solution.py:91
  21.6 0.6 collective-permute-start.18
  22.2 0.8 collective-permute-done.18
  23.0 0.9 collective-permute-start.19
  23.9 0.6 collective-permute-start.21
  24.6 2.1 %collective-permute-done.19.refs_1_ = f32[2,1024]{1,0:T(2,128)S(1)} collective-permute-done((f32[2,1024]{1,0:T(2,128)S(1)}, f32[2,1024]{1,0:T(2,128)S(1)}, u32[]{:S(2)}, u32[]{:S(2)}) %collective-permute-start.19) | collective-permute-done | bytes 8224 | tf_op jit(solution)/shard_map/ppermute | solution.py:258
  27.1 1.8 %collective-permute-start.22 = (f32[2,1024]{1,0:T(2,128)S(1)}, f32[2,1024]{1,0:T(2,128)S(1)}, u32[]{:S(2)}, u32[]{:S(2)}) collective-permute-start(f32[2,1024]{1,0:T(2,128)S(1)} %collective-permute-done.21.refs_3_), channel_id=1, source_target_pairs={{0,4},{4,0},{8,12},{12,8},{16,20},{20,16},{24,28},{28,24},{1,5},{5... | collective-permute-start | bytes 24584 | tf_op jit(solution)/shard_map/ppermute | solution.py:20
  28.9 0.8 collective-permute-done.22.refs_4_
  29.7 1.0 narrow.4
  30.7 0.9 collective-permute-start.25
  31.6 1.5 collective-permute-start.26
  33.1 1.0 narrow.5
  34.1 1.2 collective-permute-start.37
  35.3 0.5 collective-permute-start.39
  35.8 6.9 %collective-permute-done.25.refs_4_ = bf16[192,1024]{1,0:T(8,128)(2,1)S(1)} collective-permute-done((bf16[192,1024]{1,0:T(8,128)(2,1)S(1)}, bf16[192,1024]{1,0:T(8,128)(2,1)S(1)}, u32[]{:S(2)}, u32[]{:S(2)}) %collective-permute-start.25) | collective-permute-done | bytes 393248 | tf_op jit(solution)/shard_map/ppermute | solution.py:20
  42.7 1.5 collective-permute-start.38
  44.2 0.9 collective-permute-start.40
  45.1 8.8 %collective-permute-done.37.refs_2_ = bf16[256,1024]{1,0:T(8,128)(2,1)S(1)} collective-permute-done((bf16[256,1024]{1,0:T(8,128)(2,1)S(1)}, bf16[256,1024]{1,0:T(8,128)(2,1)S(1)}, u32[]{:S(2)}, u32[]{:S(2)}) %collective-permute-start.37) | collective-permute-done | bytes 524320 | tf_op jit(solution)/shard_map/ppermute | solution.py:20
  53.9 0.9 collective-permute-done.39.refs_4_
  54.8 1.2 collective-permute-start.4
  56.0 9.2 %collective-permute-done.38.refs_3_ = bf16[256,1024]{1,0:T(8,128)(2,1)S(1)} collective-permute-done((bf16[256,1024]{1,0:T(8,128)(2,1)S(1)}, bf16[256,1024]{1,0:T(8,128)(2,1)S(1)}, u32[]{:S(2)}, u32[]{:S(2)}) %collective-permute-start.38) | collective-permute-done | bytes 524320 | tf_op jit(solution)/shard_map/ppermute | solution.py:20
  65.1 1.5 collective-permute-start.5
  66.7 0.6 collective-permute-start.23
  67.2 1.2 collective-permute-start.24
  68.4 10.8 %collective-permute-done.4.refs_2_ = bf16[320,1024]{1,0:T(8,128)(2,1)S(1)} collective-permute-done((bf16[320,1024]{1,0:T(8,128)(2,1)S(1)}, bf16[320,1024]{1,0:T(8,128)(2,1)S(1)}, u32[]{:S(2)}, u32[]{:S(2)}) %collective-permute-start.4) | collective-permute-done | bytes 655392 | tf_op jit(solution)/shard_map/ppermute | solution.py:20
  79.2 3.5 %collective-permute-done.5.refs_3_ = bf16[320,1024]{1,0:T(8,128)(2,1)S(1)} collective-permute-done((bf16[320,1024]{1,0:T(8,128)(2,1)S(1)}, bf16[320,1024]{1,0:T(8,128)(2,1)S(1)}, u32[]{:S(2)}, u32[]{:S(2)}) %collective-permute-start.5) | collective-permute-done | bytes 655392 | tf_op jit(solution)/shard_map/ppermute | solution.py:20
  82.7 0.5 collective-permute-start.13
  83.2 11.8 %collective-permute-done.23.refs_2_ = bf16[320,1024]{1,0:T(8,128)(2,1)S(1)} collective-permute-done((bf16[320,1024]{1,0:T(8,128)(2,1)S(1)}, bf16[320,1024]{1,0:T(8,128)(2,1)S(1)}, u32[]{:S(2)}, u32[]{:S(2)}) %collective-permute-start.23) | collective-permute-done | bytes 655392 | tf_op jit(solution)/shard_map/ppermute | solution.py:20
  95.0 1.2 collective-permute-start.15
  96.2 0.5 collective-permute-start.43
  97.2 7.2 %collective-permute-done.15.refs_2_ = bf16[192,1024]{1,0:T(8,128)(2,1)S(1)} collective-permute-done((bf16[192,1024]{1,0:T(8,128)(2,1)S(1)}, bf16[192,1024]{1,0:T(8,128)(2,1)S(1)}, u32[]{:S(2)}, u32[]{:S(2)}) %collective-permute-start.15) | collective-permute-done | bytes 393248 | tf_op jit(solution)/shard_map/ppermute | solution.py:20
  104.4 1.5 collective-permute-start.34
  105.9 0.5 collective-permute-start.46
  106.4 7.2 %collective-permute-done.34.refs_2_ = bf16[192,1024]{1,0:T(8,128)(2,1)S(1)} collective-permute-done((bf16[192,1024]{1,0:T(8,128)(2,1)S(1)}, bf16[192,1024]{1,0:T(8,128)(2,1)S(1)}, u32[]{:S(2)}, u32[]{:S(2)}) %collective-permute-start.34) | collective-permute-done | bytes 393248 | tf_op jit(solution)/shard_map/ppermute | solution.py:20
  113.7 1.5 collective-permute-start.47
  115.2 1.2 collective-permute-start.48
  116.4 0.5 collective-permute-start.11
  116.9 0.5 collective-permute-start.14
  117.4 11.1 %collective-permute-done.47.refs_1_ = bf16[256,1024]{1,0:T(8,128)(2,1)S(1)} collective-permute-done((bf16[256,1024]{1,0:T(8,128)(2,1)S(1)}, bf16[256,1024]{1,0:T(8,128)(2,1)S(1)}, u32[]{:S(2)}, u32[]{:S(2)}) %collective-permute-start.47) | collective-permute-done | bytes 524320 | tf_op jit(solution)/shard_map/ppermute | solution.py:20
  128.5 1.2 collective-permute-start.33
  130.2 8.0 %collective-permute-done.14.refs_1_ = bf16[320,1024]{1,0:T(8,128)(2,1)S(1)} collective-permute-done((bf16[320,1024]{1,0:T(8,128)(2,1)S(1)}, bf16[320,1024]{1,0:T(8,128)(2,1)S(1)}, u32[]{:S(2)}, u32[]{:S(2)}) %collective-permute-start.14) | collective-permute-done | bytes 655392 | tf_op jit(solution)/shard_map/ppermute | solution.py:20
  138.2 0.9 collective-permute-done.33.refs_1_
  139.0 0.5 collective-permute-start.50
  140.1 1.7 %place.20.refs_0_ = bf16[4096,1024]{1,0:T(8,128)(2,1)} custom-call(s32[1]{0:T(128)} %bitcast.me_ref, bf16[256,1024]{1,0:T(8,128)(2,1)S(1)} %get-tuple-element.29.refs_0_, bf16[256,1024]{1,0:T(8,128)(2,1)S(1)} %get-tuple-element.30.refs_1_, bf16[256,1024]{1,0:T(8,128)(2,1)S(1)} %collective-permute-done.37.refs_2_, ...), custom_call_target="tpu_custom_call" | custom-call | flops 1572864 | bytes 6291456 | tf_op jit(solution)/shard_map/place/pallas_call | solution.py:196
  141.8 1.7 %place.12.refs_0_ = bf16[4096,1024]{1,0:T(8,128)(2,1)} custom-call(s32[1]{0:T(128)} %bitcast.me_ref, bf16[320,1024]{1,0:T(8,128)(2,1)S(1)} %get-tuple-element.22.refs_0_, bf16[192,1024]{1,0:T(8,128)(2,1)S(1)} %get-tuple-element.23.refs_1_, bf16[320,1024]{1,0:T(8,128)(2,1)S(1)} %collective-permute-done.4.refs_2_, ...), custom_call_target="tpu_custom_call" | custom-call | flops 1572864 | bytes 6291456 | tf_op jit(solution)/shard_map/place/pallas_call | solution.py:196
  143.5 1.7 %place.16.refs_0_ = bf16[4096,1024]{1,0:T(8,128)(2,1)} custom-call(s32[1]{0:T(128)} %bitcast.me_ref, bf16[320,1024]{1,0:T(8,128)(2,1)S(1)} %get-tuple-element.26.refs_0_, bf16[192,1024]{1,0:T(8,128)(2,1)S(1)} %get-tuple-element.27.refs_1_, bf16[320,1024]{1,0:T(8,128)(2,1)S(1)} %collective-permute-done.23.refs_2_, ...), custom_call_target="tpu_custom_call" | custom-call | flops 1572864 | bytes 6291456 | tf_op jit(solution)/shard_map/place/pallas_call | solution.py:196
  145.2 1.7 %place.21.refs_0_ = bf16[4096,1024]{1,0:T(8,128)(2,1)} custom-call(s32[1]{0:T(128)} %bitcast.me_ref, bf16[4096,1024]{1,0:T(8,128)(2,1)} %place.20.refs_0_, bf16[256,1024]{1,0:T(8,128)(2,1)S(1)} %collective-permute-done.41.refs_1_, bf16[256,1024]{1,0:T(8,128)(2,1)S(1)} %collective-permute-done.42.refs_2_, ...), custom_call_target="tpu_custom_call", output_to_operand_aliasing={{}: (1, {})} | custom-call | flops 1572864 | bytes 6291456 | tf_op jit(solution)/shard_map/place/pallas_call | solution.py:196
  146.9 1.0 place.22.refs_0_
  147.9 1.7 %place.13.refs_0_ = bf16[4096,1024]{1,0:T(8,128)(2,1)} custom-call(s32[1]{0:T(128)} %bitcast.me_ref, bf16[4096,1024]{1,0:T(8,128)(2,1)} %place.12.refs_0_, bf16[320,1024]{1,0:T(8,128)(2,1)S(1)} %collective-permute-done.8.refs_1_, bf16[192,1024]{1,0:T(8,128)(2,1)S(1)} %collective-permute-done.9.refs_2_, ...), custom_call_target="tpu_custom_call", output_to_operand_aliasing={{}: (1, {})} | custom-call | flops 1572864 | bytes 6291456 | tf_op jit(solution)/shard_map/place/pallas_call | solution.py:196
  149.7 1.0 place.14.refs_0_
  150.6 1.7 %place.17.refs_0_ = bf16[4096,1024]{1,0:T(8,128)(2,1)} custom-call(s32[1]{0:T(128)} %bitcast.me_ref, bf16[4096,1024]{1,0:T(8,128)(2,1)} %place.16.refs_0_, bf16[320,1024]{1,0:T(8,128)(2,1)S(1)} %collective-permute-done.27.refs_1_, bf16[192,1024]{1,0:T(8,128)(2,1)S(1)} %collective-permute-done.28.refs_2_, ...), custom_call_target="tpu_custom_call", output_to_operand_aliasing={{}: (1, {})} | custom-call | flops 1572864 | bytes 6291456 | tf_op jit(solution)/shard_map/place/pallas_call | solution.py:196
  152.4 1.0 place.18.refs_0_
  153.4 1.0 place.23
  154.4 1.0 place.15
  155.4 1.0 place.19
  (57 shorter events, 2.5 us)
Async XLA Ops:
  4.4 1.4 collective-permute-start
  5.8 4.4 %collective-permute-start.1 = (f32[1,1024]{1,0:T(1,128)S(1)}, f32[1,1024]{1,0:T(1,128)S(1)}, u32[]{:S(2)}, u32[]{:S(2)}) collective-permute-start(f32[1,1024]{1,0:T(1,128)S(1)} %add.6.refs_0_), channel_id=1, source_target_pairs={{0,8},{4,28},{8,0},{12,20},{16,24},{20,12},{24,16},{28,4},{1,9},{5... | collective-permute-start | bytes 12296 | tf_op jit(solution)/shard_map/ppermute | solution.py:261
  8.6 3.6 %collective-permute-start.3 = (f32[1,1024]{1,0:T(1,128)S(1)}, f32[1,1024]{1,0:T(1,128)S(1)}, u32[]{:S(2)}, u32[]{:S(2)}) collective-permute-start(f32[1,1024]{1,0:T(1,128)S(1)} %add.6.refs_0_), channel_id=1, source_target_pairs={{0,16},{4,20},{8,24},{12,28},{16,0},{20,4},{24,8},{28,12},{1,17},{... | collective-permute-start | bytes 12296 | tf_op jit(solution)/shard_map/ppermute | solution.py:20
  10.2 2.0 %collective-permute-start.2 = (f32[1,1024]{1,0:T(1,128)S(1)}, f32[1,1024]{1,0:T(1,128)S(1)}, u32[]{:S(2)}, u32[]{:S(2)}) collective-permute-start(f32[1,1024]{1,0:T(1,128)S(1)} %collective-permute-done.1.refs_1_), channel_id=1, source_target_pairs={{0,4},{4,0},{8,12},{12,8},{16,20},{20,16},{24,28},{28,24},{1,5},{5... | collective-permute-start | bytes 12296 | tf_op jit(solution)/shard_map/ppermute | solution.py:20
  13.2 20.9 %collective-permute-start.6 = (bf16[192,1024]{1,0:T(8,128)(2,1)S(1)}, bf16[192,1024]{1,0:T(8,128)(2,1)S(1)}, u32[]{:S(2)}, u32[]{:S(2)}) collective-permute-start(bf16[192,1024]{1,0:T(8,128)(2,1)S(1)} %get-tuple-element.23.refs_1_), channel_id=1, source_target_pairs={{0,16},{4,20},{8,24},{12,28},{16,0},{20,4},{24,8},{28,12},{1,17},{... | collective-permute-start | bytes 1179656 | tf_op jit(solution)/shard_map/ppermute | solution.py:20
  14.7 19.4 %collective-permute-start.7 = (bf16[192,1024]{1,0:T(8,128)(2,1)S(1)}, bf16[192,1024]{1,0:T(8,128)(2,1)S(1)}, u32[]{:S(2)}, u32[]{:S(2)}) collective-permute-start(bf16[192,1024]{1,0:T(8,128)(2,1)S(1)} %get-tuple-element.23.refs_1_), channel_id=1, source_target_pairs={{0,8},{4,12},{8,0},{12,4},{16,24},{20,28},{24,16},{28,20},{1,9},{5... | collective-permute-start | bytes 1179656 | tf_op jit(solution)/shard_map/ppermute | solution.py:20
  15.9 19.4 %collective-permute-start.9 = (bf16[192,1024]{1,0:T(8,128)(2,1)S(1)}, bf16[192,1024]{1,0:T(8,128)(2,1)S(1)}, u32[]{:S(2)}, u32[]{:S(2)}) collective-permute-start(bf16[192,1024]{1,0:T(8,128)(2,1)S(1)} %get-tuple-element.23.refs_1_), channel_id=1, source_target_pairs={{0,4},{4,0},{8,12},{12,8},{16,20},{20,16},{24,28},{28,24},{1,5},{5... | collective-permute-start | bytes 1179656 | tf_op jit(solution)/shard_map/ppermute | solution.py:20
  21.6 1.4 collective-permute-start.18
  23.0 3.7 %collective-permute-start.19 = (f32[2,1024]{1,0:T(2,128)S(1)}, f32[2,1024]{1,0:T(2,128)S(1)}, u32[]{:S(2)}, u32[]{:S(2)}) collective-permute-start(f32[2,1024]{1,0:T(2,128)S(1)} %add.7.refs_0_), channel_id=1, source_target_pairs={{0,8},{4,20},{8,0},{12,28},{16,24},{20,4},{24,16},{28,12},{1,9},{5... | collective-permute-start | bytes 24584 | tf_op jit(solution)/shard_map/ppermute | solution.py:258
  23.9 3.2 %collective-permute-start.21 = (f32[2,1024]{1,0:T(2,128)S(1)}, f32[2,1024]{1,0:T(2,128)S(1)}, u32[]{:S(2)}, u32[]{:S(2)}) collective-permute-start(f32[2,1024]{1,0:T(2,128)S(1)} %add.7.refs_0_), channel_id=1, source_target_pairs={{4,28},{12,20},{20,12},{28,4},{5,29},{13,21},{21,13},{29,5},{6,30}... | collective-permute-start | bytes 24584 | tf_op jit(solution)/shard_map/ppermute | solution.py:259
  26.7 2.2 %collective-permute-start.20 = (f32[2,1024]{1,0:T(2,128)S(1)}, f32[2,1024]{1,0:T(2,128)S(1)}, u32[]{:S(2)}, u32[]{:S(2)}) collective-permute-start(f32[2,1024]{1,0:T(2,128)S(1)} %collective-permute-done.19.refs_1_), channel_id=1, source_target_pairs={{0,4},{4,0},{8,12},{12,8},{16,20},{20,16},{24,28},{28,24},{1,5},{5... | collective-permute-start | bytes 24584 | tf_op jit(solution)/shard_map/ppermute | solution.py:20
  27.1 2.6 %collective-permute-start.22 = (f32[2,1024]{1,0:T(2,128)S(1)}, f32[2,1024]{1,0:T(2,128)S(1)}, u32[]{:S(2)}, u32[]{:S(2)}) collective-permute-start(f32[2,1024]{1,0:T(2,128)S(1)} %collective-permute-done.21.refs_3_), channel_id=1, source_target_pairs={{0,4},{4,0},{8,12},{12,8},{16,20},{20,16},{24,28},{28,24},{1,5},{5... | collective-permute-start | bytes 24584 | tf_op jit(solution)/shard_map/ppermute | solution.py:20
  30.7 12.0 %collective-permute-start.25 = (bf16[192,1024]{1,0:T(8,128)(2,1)S(1)}, bf16[192,1024]{1,0:T(8,128)(2,1)S(1)}, u32[]{:S(2)}, u32[]{:S(2)}) collective-permute-start(bf16[192,1024]{1,0:T(8,128)(2,1)S(1)} %get-tuple-element.27.refs_1_), channel_id=1, source_target_pairs={{0,8},{4,12},{8,0},{12,4},{16,24},{20,28},{24,16},{28,20},{1,9},{5... | collective-permute-start | bytes 1179656 | tf_op jit(solution)/shard_map/ppermute | solution.py:20
  31.6 12.6 %collective-permute-start.26 = (bf16[192,1024]{1,0:T(8,128)(2,1)S(1)}, bf16[192,1024]{1,0:T(8,128)(2,1)S(1)}, u32[]{:S(2)}, u32[]{:S(2)}) collective-permute-start(bf16[192,1024]{1,0:T(8,128)(2,1)S(1)} %get-tuple-element.27.refs_1_), channel_id=1, source_target_pairs={{0,16},{4,20},{8,24},{12,28},{16,0},{20,4},{24,8},{28,12},{1,17},{... | collective-permute-start | bytes 1179656 | tf_op jit(solution)/shard_map/ppermute | solution.py:20
  34.1 11.0 %collective-permute-start.28 = (bf16[192,1024]{1,0:T(8,128)(2,1)S(1)}, bf16[192,1024]{1,0:T(8,128)(2,1)S(1)}, u32[]{:S(2)}, u32[]{:S(2)}) collective-permute-start(bf16[192,1024]{1,0:T(8,128)(2,1)S(1)} %get-tuple-element.27.refs_1_), channel_id=1, source_target_pairs={{0,4},{4,0},{8,12},{12,8},{16,20},{20,16},{24,28},{28,24},{1,5},{5... | collective-permute-start | bytes 1179656 | tf_op jit(solution)/shard_map/ppermute | solution.py:20
  34.1 19.8 %collective-permute-start.37 = (bf16[256,1024]{1,0:T(8,128)(2,1)S(1)}, bf16[256,1024]{1,0:T(8,128)(2,1)S(1)}, u32[]{:S(2)}, u32[]{:S(2)}) collective-permute-start(bf16[256,1024]{1,0:T(8,128)(2,1)S(1)} %get-tuple-element.29.refs_0_), channel_id=1, source_target_pairs={{0,8},{4,12},{8,0},{12,4},{16,24},{20,28},{24,16},{28,20},{1,9},{5... | collective-permute-start | bytes 1572872 | tf_op jit(solution)/shard_map/ppermute | solution.py:20
  35.3 19.5 %collective-permute-start.39 = (bf16[256,1024]{1,0:T(8,128)(2,1)S(1)}, bf16[256,1024]{1,0:T(8,128)(2,1)S(1)}, u32[]{:S(2)}, u32[]{:S(2)}) collective-permute-start(bf16[256,1024]{1,0:T(8,128)(2,1)S(1)} %get-tuple-element.30.refs_1_), channel_id=1, source_target_pairs={{0,16},{4,20},{8,24},{12,28},{16,0},{20,4},{24,8},{28,12},{1,17},{... | collective-permute-start | bytes 1572872 | tf_op jit(solution)/shard_map/ppermute | solution.py:20
  42.7 22.4 %collective-permute-start.38 = (bf16[256,1024]{1,0:T(8,128)(2,1)S(1)}, bf16[256,1024]{1,0:T(8,128)(2,1)S(1)}, u32[]{:S(2)}, u32[]{:S(2)}) collective-permute-start(bf16[256,1024]{1,0:T(8,128)(2,1)S(1)} %get-tuple-element.29.refs_0_), channel_id=1, source_target_pairs={{0,16},{4,20},{8,24},{12,28},{16,0},{20,4},{24,8},{28,12},{1,17},{... | collective-permute-start | bytes 1572872 | tf_op jit(solution)/shard_map/ppermute | solution.py:20
  44.2 22.4 %collective-permute-start.40 = (bf16[256,1024]{1,0:T(8,128)(2,1)S(1)}, bf16[256,1024]{1,0:T(8,128)(2,1)S(1)}, u32[]{:S(2)}, u32[]{:S(2)}) collective-permute-start(bf16[256,1024]{1,0:T(8,128)(2,1)S(1)} %get-tuple-element.30.refs_1_), channel_id=1, source_target_pairs={{0,8},{4,12},{8,0},{12,4},{16,24},{20,28},{24,16},{28,20},{1,9},{5... | collective-permute-start | bytes 1572872 | tf_op jit(solution)/shard_map/ppermute | solution.py:20
  45.1 21.6 %collective-permute-start.41 = (bf16[256,1024]{1,0:T(8,128)(2,1)S(1)}, bf16[256,1024]{1,0:T(8,128)(2,1)S(1)}, u32[]{:S(2)}, u32[]{:S(2)}) collective-permute-start(bf16[256,1024]{1,0:T(8,128)(2,1)S(1)} %get-tuple-element.29.refs_0_), channel_id=1, source_target_pairs={{0,4},{4,0},{8,12},{12,8},{16,20},{20,16},{24,28},{28,24},{1,5},{5... | collective-permute-start | bytes 1572872 | tf_op jit(solution)/shard_map/ppermute | solution.py:20
  53.9 13.3 %collective-permute-start.42 = (bf16[256,1024]{1,0:T(8,128)(2,1)S(1)}, bf16[256,1024]{1,0:T(8,128)(2,1)S(1)}, u32[]{:S(2)}, u32[]{:S(2)}) collective-permute-start(bf16[256,1024]{1,0:T(8,128)(2,1)S(1)} %get-tuple-element.30.refs_1_), channel_id=1, source_target_pairs={{0,4},{4,0},{8,12},{12,8},{16,20},{20,16},{24,28},{28,24},{1,5},{5... | collective-permute-start | bytes 1572872 | tf_op jit(solution)/shard_map/ppermute | solution.py:20
  54.8 24.4 %collective-permute-start.4 = (bf16[320,1024]{1,0:T(8,128)(2,1)S(1)}, bf16[320,1024]{1,0:T(8,128)(2,1)S(1)}, u32[]{:S(2)}, u32[]{:S(2)}) collective-permute-start(bf16[320,1024]{1,0:T(8,128)(2,1)S(1)} %get-tuple-element.22.refs_0_), channel_id=1, source_target_pairs={{0,8},{4,12},{8,0},{12,4},{16,24},{20,28},{24,16},{28,20},{1,9},{5... | collective-permute-start | bytes 1966088 | tf_op jit(solution)/shard_map/ppermute | solution.py:20
  65.1 17.6 %collective-permute-start.5 = (bf16[320,1024]{1,0:T(8,128)(2,1)S(1)}, bf16[320,1024]{1,0:T(8,128)(2,1)S(1)}, u32[]{:S(2)}, u32[]{:S(2)}) collective-permute-start(bf16[320,1024]{1,0:T(8,128)(2,1)S(1)} %get-tuple-element.22.refs_0_), channel_id=1, source_target_pairs={{0,16},{4,20},{8,24},{12,28},{16,0},{20,4},{24,8},{28,12},{1,17},{... | collective-permute-start | bytes 1966088 | tf_op jit(solution)/shard_map/ppermute | solution.py:20
  66.6 16.1 %collective-permute-start.8 = (bf16[320,1024]{1,0:T(8,128)(2,1)S(1)}, bf16[320,1024]{1,0:T(8,128)(2,1)S(1)}, u32[]{:S(2)}, u32[]{:S(2)}) collective-permute-start(bf16[320,1024]{1,0:T(8,128)(2,1)S(1)} %get-tuple-element.22.refs_0_), channel_id=1, source_target_pairs={{0,4},{4,0},{8,12},{12,8},{16,20},{20,16},{24,28},{28,24},{1,5},{5... | collective-permute-start | bytes 1966088 | tf_op jit(solution)/shard_map/ppermute | solution.py:20
  66.7 28.4 %collective-permute-start.23 = (bf16[320,1024]{1,0:T(8,128)(2,1)S(1)}, bf16[320,1024]{1,0:T(8,128)(2,1)S(1)}, u32[]{:S(2)}, u32[]{:S(2)}) collective-permute-start(bf16[320,1024]{1,0:T(8,128)(2,1)S(1)} %get-tuple-element.26.refs_0_), channel_id=1, source_target_pairs={{0,16},{4,20},{8,24},{12,28},{16,0},{20,4},{24,8},{28,12},{1,17},{... | collective-permute-start | bytes 1966088 | tf_op jit(solution)/shard_map/ppermute | solution.py:20
  67.2 28.9 %collective-permute-start.24 = (bf16[320,1024]{1,0:T(8,128)(2,1)S(1)}, bf16[320,1024]{1,0:T(8,128)(2,1)S(1)}, u32[]{:S(2)}, u32[]{:S(2)}) collective-permute-start(bf16[320,1024]{1,0:T(8,128)(2,1)S(1)} %get-tuple-element.26.refs_0_), channel_id=1, source_target_pairs={{0,8},{4,12},{8,0},{12,4},{16,24},{20,28},{24,16},{28,20},{1,9},{5... | collective-permute-start | bytes 1966088 | tf_op jit(solution)/shard_map/ppermute | solution.py:20
  79.2 17.0 %collective-permute-start.27 = (bf16[320,1024]{1,0:T(8,128)(2,1)S(1)}, bf16[320,1024]{1,0:T(8,128)(2,1)S(1)}, u32[]{:S(2)}, u32[]{:S(2)}) collective-permute-start(bf16[320,1024]{1,0:T(8,128)(2,1)S(1)} %get-tuple-element.26.refs_0_), channel_id=1, source_target_pairs={{0,4},{4,0},{8,12},{12,8},{16,20},{20,16},{24,28},{28,24},{1,5},{5... | collective-permute-start | bytes 1966088 | tf_op jit(solution)/shard_map/ppermute | solution.py:20
  82.7 14.0 %collective-permute-start.12 = (bf16[192,1024]{1,0:T(8,128)(2,1)S(1)}, bf16[192,1024]{1,0:T(8,128)(2,1)S(1)}, u32[]{:S(2)}, u32[]{:S(2)}) collective-permute-start(bf16[192,1024]{1,0:T(8,128)(2,1)S(1)} %collective-permute-done.6.refs_4_), channel_id=1, source_target_pairs={{0,4},{4,0},{8,12},{12,8},{16,20},{20,16},{24,28},{28,24},{1,5},{5... | collective-permute-start | bytes 1179656 | tf_op jit(solution)/shard_map/ppermute | solution.py:20
  82.7 14.0 %collective-permute-start.13 = (bf16[192,1024]{1,0:T(8,128)(2,1)S(1)}, bf16[192,1024]{1,0:T(8,128)(2,1)S(1)}, u32[]{:S(2)}, u32[]{:S(2)}) collective-permute-start(bf16[192,1024]{1,0:T(8,128)(2,1)S(1)} %collective-permute-done.7.refs_5_), channel_id=1, source_target_pairs={{0,4},{4,0},{8,12},{12,8},{16,20},{20,16},{24,28},{28,24},{1,5},{5... | collective-permute-start | bytes 1179656 | tf_op jit(solution)/shard_map/ppermute | solution.py:20
  95.0 9.4 %collective-permute-start.15 = (bf16[192,1024]{1,0:T(8,128)(2,1)S(1)}, bf16[192,1024]{1,0:T(8,128)(2,1)S(1)}, u32[]{:S(2)}, u32[]{:S(2)}) collective-permute-start(bf16[192,1024]{1,0:T(8,128)(2,1)S(1)} %collective-permute-done.6.refs_4_), channel_id=1, source_target_pairs={{0,8},{4,12},{8,0},{12,4},{16,24},{20,28},{24,16},{28,20},{1,9},{5... | collective-permute-start | bytes 1179656 | tf_op jit(solution)/shard_map/ppermute | solution.py:20
  96.2 9.7 %collective-permute-start.31 = (bf16[192,1024]{1,0:T(8,128)(2,1)S(1)}, bf16[192,1024]{1,0:T(8,128)(2,1)S(1)}, u32[]{:S(2)}, u32[]{:S(2)}) collective-permute-start(bf16[192,1024]{1,0:T(8,128)(2,1)S(1)} %collective-permute-done.25.refs_4_), channel_id=1, source_target_pairs={{0,4},{4,0},{8,12},{12,8},{16,20},{20,16},{24,28},{28,24},{1,5},{5... | collective-permute-start | bytes 1179656 | tf_op jit(solution)/shard_map/ppermute | solution.py:20
  96.2 19.0 %collective-permute-start.43 = (bf16[256,1024]{1,0:T(8,128)(2,1)S(1)}, bf16[256,1024]{1,0:T(8,128)(2,1)S(1)}, u32[]{:S(2)}, u32[]{:S(2)}) collective-permute-start(bf16[256,1024]{1,0:T(8,128)(2,1)S(1)} %collective-permute-done.37.refs_2_), channel_id=1, source_target_pairs={{0,4},{4,0},{8,12},{12,8},{16,20},{20,16},{24,28},{28,24},{1,5},{5... | collective-permute-start | bytes 1572872 | tf_op jit(solution)/shard_map/ppermute | solution.py:20
  96.7 19.7 %collective-permute-start.45 = (bf16[256,1024]{1,0:T(8,128)(2,1)S(1)}, bf16[256,1024]{1,0:T(8,128)(2,1)S(1)}, u32[]{:S(2)}, u32[]{:S(2)}) collective-permute-start(bf16[256,1024]{1,0:T(8,128)(2,1)S(1)} %collective-permute-done.39.refs_4_), channel_id=1, source_target_pairs={{0,4},{4,0},{8,12},{12,8},{16,20},{20,16},{24,28},{28,24},{1,5},{5... | collective-permute-start | bytes 1572872 | tf_op jit(solution)/shard_map/ppermute | solution.py:20
  96.8 9.1 %collective-permute-start.32 = (bf16[192,1024]{1,0:T(8,128)(2,1)S(1)}, bf16[192,1024]{1,0:T(8,128)(2,1)S(1)}, u32[]{:S(2)}, u32[]{:S(2)}) collective-permute-start(bf16[192,1024]{1,0:T(8,128)(2,1)S(1)} %collective-permute-done.26.refs_5_), channel_id=1, source_target_pairs={{0,4},{4,0},{8,12},{12,8},{16,20},{20,16},{24,28},{28,24},{1,5},{5... | collective-permute-start | bytes 1179656 | tf_op jit(solution)/shard_map/ppermute | solution.py:20
  104.4 9.3 %collective-permute-start.34 = (bf16[192,1024]{1,0:T(8,128)(2,1)S(1)}, bf16[192,1024]{1,0:T(8,128)(2,1)S(1)}, u32[]{:S(2)}, u32[]{:S(2)}) collective-permute-start(bf16[192,1024]{1,0:T(8,128)(2,1)S(1)} %collective-permute-done.25.refs_4_), channel_id=1, source_target_pairs={{0,16},{4,20},{8,24},{12,28},{16,0},{20,4},{24,8},{28,12},{1,17},{... | collective-permute-start | bytes 1179656 | tf_op jit(solution)/shard_map/ppermute | solution.py:20
  105.9 10.5 %collective-permute-start.44 = (bf16[256,1024]{1,0:T(8,128)(2,1)S(1)}, bf16[256,1024]{1,0:T(8,128)(2,1)S(1)}, u32[]{:S(2)}, u32[]{:S(2)}) collective-permute-start(bf16[256,1024]{1,0:T(8,128)(2,1)S(1)} %collective-permute-done.38.refs_3_), channel_id=1, source_target_pairs={{0,4},{4,0},{8,12},{12,8},{16,20},{20,16},{24,28},{28,24},{1,5},{5... | collective-permute-start | bytes 1572872 | tf_op jit(solution)/shard_map/ppermute | solution.py:20
  105.9 11.0 %collective-permute-start.46 = (bf16[256,1024]{1,0:T(8,128)(2,1)S(1)}, bf16[256,1024]{1,0:T(8,128)(2,1)S(1)}, u32[]{:S(2)}, u32[]{:S(2)}) collective-permute-start(bf16[256,1024]{1,0:T(8,128)(2,1)S(1)} %collective-permute-done.40.refs_5_), channel_id=1, source_target_pairs={{0,4},{4,0},{8,12},{12,8},{16,20},{20,16},{24,28},{28,24},{1,5},{5... | collective-permute-start | bytes 1572872 | tf_op jit(solution)/shard_map/ppermute | solution.py:20
  113.7 14.8 %collective-permute-start.47 = (bf16[256,1024]{1,0:T(8,128)(2,1)S(1)}, bf16[256,1024]{1,0:T(8,128)(2,1)S(1)}, u32[]{:S(2)}, u32[]{:S(2)}) collective-permute-start(bf16[256,1024]{1,0:T(8,128)(2,1)S(1)} %collective-permute-done.37.refs_2_), channel_id=1, source_target_pairs={{0,16},{4,20},{8,24},{12,28},{16,0},{20,4},{24,8},{28,12},{1,17},{... | collective-permute-start | bytes 1572872 | tf_op jit(solution)/shard_map/ppermute | solution.py:20
  115.2 14.4 %collective-permute-start.48 = (bf16[256,1024]{1,0:T(8,128)(2,1)S(1)}, bf16[256,1024]{1,0:T(8,128)(2,1)S(1)}, u32[]{:S(2)}, u32[]{:S(2)}) collective-permute-start(bf16[256,1024]{1,0:T(8,128)(2,1)S(1)} %collective-permute-done.39.refs_4_), channel_id=1, source_target_pairs={{0,8},{4,12},{8,0},{12,4},{16,24},{20,28},{24,16},{28,20},{1,9},{5... | collective-permute-start | bytes 1572872 | tf_op jit(solution)/shard_map/ppermute | solution.py:20
  116.3 13.3 %collective-permute-start.10 = (bf16[320,1024]{1,0:T(8,128)(2,1)S(1)}, bf16[320,1024]{1,0:T(8,128)(2,1)S(1)}, u32[]{:S(2)}, u32[]{:S(2)}) collective-permute-start(bf16[320,1024]{1,0:T(8,128)(2,1)S(1)} %collective-permute-done.4.refs_2_), channel_id=1, source_target_pairs={{0,4},{4,0},{8,12},{12,8},{16,20},{20,16},{24,28},{28,24},{1,5},{5... | collective-permute-start | bytes 1966088 | tf_op jit(solution)/shard_map/ppermute | solution.py:20
  116.4 13.8 %collective-permute-start.11 = (bf16[320,1024]{1,0:T(8,128)(2,1)S(1)}, bf16[320,1024]{1,0:T(8,128)(2,1)S(1)}, u32[]{:S(2)}, u32[]{:S(2)}) collective-permute-start(bf16[320,1024]{1,0:T(8,128)(2,1)S(1)} %collective-permute-done.5.refs_3_), channel_id=1, source_target_pairs={{0,4},{4,0},{8,12},{12,8},{16,20},{20,16},{24,28},{28,24},{1,5},{5... | collective-permute-start | bytes 1966088 | tf_op jit(solution)/shard_map/ppermute | solution.py:20
  116.9 21.3 %collective-permute-start.14 = (bf16[320,1024]{1,0:T(8,128)(2,1)S(1)}, bf16[320,1024]{1,0:T(8,128)(2,1)S(1)}, u32[]{:S(2)}, u32[]{:S(2)}) collective-permute-start(bf16[320,1024]{1,0:T(8,128)(2,1)S(1)} %collective-permute-done.4.refs_2_), channel_id=1, source_target_pairs={{0,16},{4,20},{8,24},{12,28},{16,0},{20,4},{24,8},{28,12},{1,17},{... | collective-permute-start | bytes 1966088 | tf_op jit(solution)/shard_map/ppermute | solution.py:20
  128.5 10.6 %collective-permute-start.33 = (bf16[320,1024]{1,0:T(8,128)(2,1)S(1)}, bf16[320,1024]{1,0:T(8,128)(2,1)S(1)}, u32[]{:S(2)}, u32[]{:S(2)}) collective-permute-start(bf16[320,1024]{1,0:T(8,128)(2,1)S(1)} %collective-permute-done.23.refs_2_), channel_id=1, source_target_pairs={{0,8},{4,12},{8,0},{12,4},{16,24},{20,28},{24,16},{28,20},{1,9},{5... | collective-permute-start | bytes 1966088 | tf_op jit(solution)/shard_map/ppermute | solution.py:20
  129.6 9.4 %collective-permute-start.29 = (bf16[320,1024]{1,0:T(8,128)(2,1)S(1)}, bf16[320,1024]{1,0:T(8,128)(2,1)S(1)}, u32[]{:S(2)}, u32[]{:S(2)}) collective-permute-start(bf16[320,1024]{1,0:T(8,128)(2,1)S(1)} %collective-permute-done.23.refs_2_), channel_id=1, source_target_pairs={{0,4},{4,0},{8,12},{12,8},{16,20},{20,16},{24,28},{28,24},{1,5},{5... | collective-permute-start | bytes 1966088 | tf_op jit(solution)/shard_map/ppermute | solution.py:20
  129.6 9.9 %collective-permute-start.30 = (bf16[320,1024]{1,0:T(8,128)(2,1)S(1)}, bf16[320,1024]{1,0:T(8,128)(2,1)S(1)}, u32[]{:S(2)}, u32[]{:S(2)}) collective-permute-start(bf16[320,1024]{1,0:T(8,128)(2,1)S(1)} %collective-permute-done.24.refs_3_), channel_id=1, source_target_pairs={{0,4},{4,0},{8,12},{12,8},{16,20},{20,16},{24,28},{28,24},{1,5},{5... | collective-permute-start | bytes 1966088 | tf_op jit(solution)/shard_map/ppermute | solution.py:20
  130.1 9.5 %collective-permute-start.49 = (bf16[256,1024]{1,0:T(8,128)(2,1)S(1)}, bf16[256,1024]{1,0:T(8,128)(2,1)S(1)}, u32[]{:S(2)}, u32[]{:S(2)}) collective-permute-start(bf16[256,1024]{1,0:T(8,128)(2,1)S(1)} %collective-permute-done.47.refs_1_), channel_id=1, source_target_pairs={{0,4},{4,0},{8,12},{12,8},{16,20},{20,16},{24,28},{28,24},{1,5},{5... | collective-permute-start | bytes 1572872 | tf_op jit(solution)/shard_map/ppermute | solution.py:20
  138.2 16.2 %collective-permute-start.16 = (bf16[320,1024]{1,0:T(8,128)(2,1)S(1)}, bf16[320,1024]{1,0:T(8,128)(2,1)S(1)}, u32[]{:S(2)}, u32[]{:S(2)}) collective-permute-start(bf16[320,1024]{1,0:T(8,128)(2,1)S(1)} %collective-permute-done.14.refs_1_), channel_id=1, source_target_pairs={{0,4},{4,0},{8,12},{12,8},{16,20},{20,16},{24,28},{28,24},{1,5},{5... | collective-permute-start | bytes 1966088 | tf_op jit(solution)/shard_map/ppermute | solution.py:20
  139.0 16.4 %collective-permute-start.35 = (bf16[320,1024]{1,0:T(8,128)(2,1)S(1)}, bf16[320,1024]{1,0:T(8,128)(2,1)S(1)}, u32[]{:S(2)}, u32[]{:S(2)}) collective-permute-start(bf16[320,1024]{1,0:T(8,128)(2,1)S(1)} %collective-permute-done.33.refs_1_), channel_id=1, source_target_pairs={{0,4},{4,0},{8,12},{12,8},{16,20},{20,16},{24,28},{28,24},{1,5},{5... | collective-permute-start | bytes 1966088 | tf_op jit(solution)/shard_map/ppermute | solution.py:20
  139.0 14.3 %collective-permute-start.50 = (bf16[256,1024]{1,0:T(8,128)(2,1)S(1)}, bf16[256,1024]{1,0:T(8,128)(2,1)S(1)}, u32[]{:S(2)}, u32[]{:S(2)}) collective-permute-start(bf16[256,1024]{1,0:T(8,128)(2,1)S(1)} %collective-permute-done.48.refs_2_), channel_id=1, source_target_pairs={{0,4},{4,0},{8,12},{12,8},{16,20},{20,16},{24,28},{28,24},{1,5},{5... | collective-permute-start | bytes 1572872 | tf_op jit(solution)/shard_map/ppermute | solution.py:20
  139.6 14.8 %collective-permute-start.17 = (bf16[192,1024]{1,0:T(8,128)(2,1)S(1)}, bf16[192,1024]{1,0:T(8,128)(2,1)S(1)}, u32[]{:S(2)}, u32[]{:S(2)}) collective-permute-start(bf16[192,1024]{1,0:T(8,128)(2,1)S(1)} %collective-permute-done.15.refs_2_), channel_id=1, source_target_pairs={{0,4},{4,0},{8,12},{12,8},{16,20},{20,16},{24,28},{28,24},{1,5},{5... | collective-permute-start | bytes 1179656 | tf_op jit(solution)/shard_map/ppermute | solution.py:20
  139.6 15.8 %collective-permute-start.36 = (bf16[192,1024]{1,0:T(8,128)(2,1)S(1)}, bf16[192,1024]{1,0:T(8,128)(2,1)S(1)}, u32[]{:S(2)}, u32[]{:S(2)}) collective-permute-start(bf16[192,1024]{1,0:T(8,128)(2,1)S(1)} %collective-permute-done.34.refs_2_), channel_id=1, source_target_pairs={{0,4},{4,0},{8,12},{12,8},{16,20},{20,16},{24,28},{28,24},{1,5},{5... | collective-permute-start | bytes 1179656 | tf_op jit(solution)/shard_map/ppermute | solution.py:20
where the time goes:
time: 157 us; the launch traced here: 156 us
  waiting for transfers between devices  92.7 us (59%)
  starting transfers between devices  34.2 us (22%)
  Pallas kernels  28.6 us (18%)
    ppermute x48, waiting for transfers between devices, swap(): return lax.ppermute(value, 'fsdp', [(i, i ^ mask) for i in range(n)])  90.5 us
    ppermute x48, starting transfers between devices, swap(): return lax.ppermute(value, 'fsdp', [(i, i ^ mask) for i in range(n)])  29.9 us
    pallas_call x12, Pallas kernels, place(): pl.pallas_call(functools.partial(place_kernel, spots, rows, len(held)), i...  16.2 us
    pallas_call x2, Pallas kernels, update(): pl.pallas_call(functools.partial(update_kernel, count, chunk), in_specs=[...  9.49 us
  transfers between devices with their start and end apart: 51, of which 18 were waited for; matrix products, arithmetic and copies ran while one was open for 0% of the time, Pallas kernels for 15%

commit v1 on v0

--- a/solution.py
+++ b/solution.py
@@ -127,47 +127,34 @@
     return values[0] / rows_all
 
 
-def narrow_kernel(index, count, rows_all, edges, roles, me_ref, *refs):
-    totals, block, pieces = refs[:count], refs[count], refs[count + 1 : -2]
-    factor, scale = refs[-2:]
-    rows, cols = block.shape
-    step = pl.program_id(0)
-
-    @pl.when(step == 0)
-    def _():
-        mean = mean_of(index, rows_all, me_ref, totals, roles)
-        factor[...] = mean
-        scale[...] = 1.0 / mean
-
-    def write(piece):
-        for lanes in lane_groups(cols):
-            by = scale[:, lanes]
-            for r in range(0, rows, 16):
-                piece[r : r + 16, lanes] = (block[r : r + 16, lanes] * by).astype(jnp.bfloat16)
-
-    for p, piece in enumerate(pieces):
-        pl.when((step >= edges[p]) & (step < edges[p + 1]))(functools.partial(write, piece))
-
-
-def narrow(gained, totals, roles, index, me, n, sizes):
+def narrow_kernel(index, count, rows_all, start, roles, me_ref, *refs):
+    totals, block, pieces, factor = refs[:count], refs[count], refs[count + 1 : -1], refs[-1]
+    mean = mean_of(index, rows_all, me_ref, totals, roles)
+    factor[...] = mean
+    scale = 1.0 / mean
+    for piece in pieces:
+        rows, cols = piece.shape
+
+        def work(i, _, piece=piece, start=start, cols=cols):
+            for lanes in lane_groups(cols):
+                x = block[pl.ds(pl.multiple_of(start + i * 16, 16), 16), lanes]
+                piece[pl.ds(pl.multiple_of(i * 16, 16), 16), lanes] = (x * scale[:, lanes]).astype(jnp.bfloat16)
+            return _
+
+        lax.fori_loop(0, rows // 16, work, 0, unroll=2 if rows % 32 == 0 else 1)
+        start += rows
+
+
+def narrow(gained, totals, roles, index, me, n, start, sizes):
     rows, cols = gained.shape
-    br = math.gcd(step_rows(rows), *sizes)
-    edges = [sum(sizes[:p]) // br for p in range(len(sizes) + 1)]
-    size = rows * cols
-
-    def piece_spec(p):
-        return pl.BlockSpec((br, cols), lambda i: (jnp.clip(i - edges[p], 0, edges[p + 1] - edges[p] - 1), 0))
-
+    size = sum(sizes) * cols
     *pieces, factor = pl.pallas_call(
-        functools.partial(narrow_kernel, index, len(totals), float(n * rows), edges, roles),
-        grid=(rows // br,),
+        functools.partial(narrow_kernel, index, len(totals), float(n * rows), start, roles),
         in_specs=[pl.BlockSpec(memory_space=pltpu.SMEM)]
-        + [pl.BlockSpec(t.shape, lambda i: (0, 0)) for t in totals]
-        + [pl.BlockSpec((br, cols), lambda i: (i, 0))],
-        out_specs=[piece_spec(p) for p in range(len(sizes))] + [pl.BlockSpec((1, cols), lambda i: (0, 0))],
+        + [pl.BlockSpec(memory_space=pltpu.VMEM)] * (len(totals) + 1),
+        out_specs=[pl.BlockSpec(memory_space=pltpu.VMEM)] * (len(sizes) + 1),
         out_shape=[jax.ShapeDtypeStruct((s, cols), jnp.bfloat16) for s in sizes]
         + [jax.ShapeDtypeStruct((1, cols), jnp.float32)],
-        scratch_shapes=[pltpu.VMEM((1, cols), jnp.float32)],
         compiler_params=pltpu.CompilerParams(vmem_limit_bytes=VMEM_LIMIT),
         cost_estimate=pl.CostEstimate(flops=8 * size, bytes_accessed=6 * size, transcendentals=0),
         name="narrow",
@@ -175,11 +162,17 @@
     return pieces, factor.reshape(cols)
 
 
+def mask_of(link, core, links):
+    return 2 << ((link + core) % links)
+
+
 def place_kernel(spots, rows, held, me_ref, *refs):
     pieces, out, sems = refs[held : held + len(spots)], refs[-2], refs[-1]
+    me = me_ref[0]
     copies = []
-    for i, (offset, start) in enumerate(spots):
-        at = pl.multiple_of((me_ref[0] ^ offset) * rows + start, 16)
+    for i, (even, odd, start) in enumerate(spots):
+        device = me ^ jnp.where((me & 1) == 0, even, odd)
+        at = pl.multiple_of(device * rows + start, 16)
         copies.append(
             pltpu.make_async_copy(pieces[i], out.at[pl.ds(at, pieces[i].shape[0])], sems.at[i])
         )
@@ -189,8 +182,8 @@
 
 
 def place(out, me, n, rows, items):
-    spots = tuple((offset, start) for offset, start, _ in items)
-    pieces = [piece for _, _, piece in items]
+    spots = tuple(item[:3] for item in items)
+    pieces = [item[3] for item in items]
     size = sum(piece.size for piece in pieces)
     held = [] if out is None else [out]
     return pl.pallas_call(
@@ -208,41 +201,62 @@
     )(me, *held, *pieces)
 
 
-def send(mask, piece, n):
-    return swap(piece, mask, n)
-
-
-def send_first(pieces, plan, masks, n):
+def over_link(link, piece, n, links):
+    pairs = [(i, i ^ mask_of(link, i & 1, links)) for i in range(n)]
+    return lax.ppermute(piece, "fsdp", pairs)
+
+
+def to_core(piece, n):
+    return swap(piece, 1, n)
+
+
+def send_first(pieces, plan, n, links):
     sent = []
     for p, (_, turn) in enumerate(plan):
-        for s in range(len(masks)):
-            mask = masks[(turn + s) % len(masks)]
-            sent.append((mask, p, s, send(mask, pieces[p], n)))
+        for s in range(links):
+            link = (turn + s) % links
+            sent.append(((link,), p, s, over_link(link, pieces[p], n, links)))
     return sent
 
 
-def send_onward(first, plan, masks, n):
+def send_onward(first, plan, n, links):
     later, level = [], first
     while level:
         following = []
-        for offset, p, at, piece in level:
-            for step in range(at + 1, len(masks)):
-                mask = masks[(plan[p][1] + step) % len(masks)]
-                following.append((offset ^ mask, p, step, send(mask, piece, n)))
+        for crossed, p, at, piece in level:
+            for step in range(at + 1, links):
+                link = (plan[p][1] + step) % links
+                got = over_link(link, piece, n, links)
+                following.append((crossed + (link,), p, step, got))
         level = following
         later += level
     return later
 
 
-def assemble(pieces, first, later, plan, me, n):
+def assemble(pieces, first, later, plan, me, n, links, last):
     starts = [sum(size for size, _ in plan[:p]) for p in range(len(plan) + 1)]
+
+    def own(crossed, p, piece):
+        even, odd = (sum(mask_of(link, core, links) for link in crossed) for core in (0, 1))
+        return even, odd, starts[p], piece
+
+    def near(crossed, p, piece):
+        even, odd, start, _ = own(crossed, p, piece)
+        return odd ^ 1, even ^ 1, start, to_core(piece, n)
+
     stages = [
-        [(0, starts[p], x) for p, x in enumerate(pieces)] + [(o, starts[p], x) for o, p, _, x in first],
-        [(1, starts[p], send(1, x, n)) for p, x in enumerate(pieces)]
-        + [(o ^ 1, starts[p], send(1, x, n)) for o, p, _, x in first],
-        [(o, starts[p], x) for o, p, _, x in later],
-        [(o ^ 1, starts[p], send(1, x, n)) for o, p, _, x in later],
+        [own((), p, x) for p, x in enumerate(pieces)] + [own(c, p, x) for c, p, _, x in first],
+        [near((), p, x) for p, x in enumerate(pieces)]
+        + [near(c, p, x) for c, p, _, x in first],
     ]
+    batches = [later]
+    if len(plan) > links:
+        split = len(plan) - links
+        batches = [[x for x in later if x[1] < split], [x for x in later if x[1] >= split]]
+    for b, batch in enumerate(batches):
+        mine = [own(c, p, x) for c, p, _, x in batch]
+        others = [near(c, p, x) for c, p, _, x in batch]
+        stages += [mine, others] if last and b == len(batches) - 1 else [mine + others]
     out = None
     for items in stages:
         if items:
@@ -260,23 +274,26 @@
     else:
         got = lax.ppermute(chip, "fsdp", [(i, i ^ (6 if i & 1 else 2)) for i in range(n)])
         across = swap(chip, 4, n)
-    other = send(1, got, n)
+    other = to_core(got, n)
     if aside:
-        return [chip, got, other, both, send(1, both, n)], "aside"
+        return [chip, got, other, both, to_core(both, n)], "aside"
     return [chip, got, other, across], "fast"
 
 
 def plans_for(rows, links, count):
-    if links == 2 and rows % 128 == 0:
-        long, half = rows * 5 // 8, rows // 2
-        return [[(long, 0), (rows - long, 1)], [(long, 1), (rows - long, 0)], [(half, 0), (half, 1)]]
+    if links == 2 and count == 3 and rows % 256 == 0:
+        unit = rows // 16
+        return [
+            [(10 * unit, 0), (6 * unit, 1)],
+            [(10 * unit, 1), (6 * unit, 0)],
+            [(5 * unit, 0), (5 * unit, 1), (3 * unit, 0), (3 * unit, 1)],
+        ]
     return [[(rows // links, p) for p in range(links)]] * count
 
 
 def solution(mesh):
     n = mesh.shape["fsdp"]
     links = n.bit_length() - 2
-    masks = [2 << j for j in range(links)]
 
     def on_device(wq, fq, sq, wk, fk, sk, wv, fv, sv, norm_gain):
         me = lax.axis_index("fsdp").astype(jnp.int32).reshape(1)
@@ -285,18 +302,19 @@
         sizes = [[size for size, _ in plan] for plan in plans]
         gained, sums = update([(wq, fq, sq)], gain_row)
         totals, roles = chip_totals(sums, n, False)
-        pieces, factor = narrow(gained[0], totals, roles, 0, me, n, sizes[0])
+        head, factor = narrow(gained[0], totals, roles, 0, me, n, 0, sizes[0][:1])
+        rest, _ = narrow(gained[0], totals, roles, 0, me, n, sizes[0][0], sizes[0][1:])
         gained, sums = update([(wk, fk, sk), (wv, fv, sv)], gain_row)
         totals, roles = chip_totals(sums, n, True)
         narrowed = [
-            narrow(g, totals, roles, t, me, n, sizes[t + 1]) for t, g in enumerate(gained)
+            narrow(g, totals, roles, t, me, n, 0, sizes[t + 1]) for t, g in enumerate(gained)
         ]
-        pieces = [pieces, narrowed[0][0], narrowed[1][0]]
+        pieces = [head + rest, narrowed[0][0], narrowed[1][0]]
         outs = []
         for t, plan in enumerate(plans):
-            first = send_first(pieces[t], plan, masks, n)
-            later = send_onward(first, plan, masks, n)
-            outs.append(assemble(pieces[t], first, later, plan, me, n))
+            first = send_first(pieces[t], plan, n, links)
+            later = send_onward(first, plan, n, links)
+            outs.append(assemble(pieces[t], first, later, plan, me, n, links, t == 2))
         return (*outs, factor, narrowed[0][1], narrowed[1][1])
 
     return jax.shard_map(

time: 157 us -> 166 us (1.057)
  waiting for transfers between devices: 92.7 us -> 96.5 us
  starting transfers between devices: 34.2 us -> 37.2 us
  local copies, waits for them, and re-layouts: 0 us -> 2.9 us
    ppermute x0 -> x24, waiting for transfers between devices: none -> 85.8 us  [over_link(): return lax.ppermute(piece, 'fsdp', pairs)]
    ppermute x48 -> x38, waiting for transfers between devices: 90.5 us -> 7.87 us  [swap(): return lax.ppermute(value, 'fsdp', [(i, i ^ mask) for i in range(n)])]
    ppermute x0 -> x24, starting transfers between devices: none -> 23 us  [over_link(): return lax.ppermute(piece, 'fsdp', pairs)]
    ppermute x48 -> x38, starting transfers between devices: 29.9 us -> 10.3 us  [swap(): return lax.ppermute(value, 'fsdp', [(i, i ^ mask) for i in range(n)])]
    unnamed x0 -> x4, local copies, waits for them, and re-layouts: none -> 2.9 us
    ppermute x1, starting transfers between devices: 2.82 us -> 0.53 us  [chip_totals(): lax.ppermute(chip, 'fsdp', [(i, i ^ (6 if i & 1 else 2)) for i in range(n)])]
    ppermute x1, starting transfers between devices: 0.86 us -> 2.82 us  [chip_totals(): lax.ppermute(chip, 'fsdp', [(i, i ^ (4 if i & 1 else 2)) for i in range(n)])]
    ppermute x1, waiting for transfers between devices: 0.06 us -> 1.86 us  [chip_totals(): lax.ppermute(chip, 'fsdp', [(i, i ^ (6 if i & 1 else 2)) for i in range(n)])]
  transfers between devices with their start and end apart: 51 -> 65, of which waited for: 18 -> 23; matrix products, arithmetic and copies ran while one was open for 0% -> 0% of each run, Pallas kernels for 15% -> 12%
where the time goes in v1:
time: 166 us
  waiting for transfers between devices  96.5 us (58%)
  starting transfers between devices  37.2 us (22%)
  Pallas kernels  28.4 us (17%)
  local copies, waits for them, and re-layouts  2.9 us (2%)
    ppermute x24, waiting for transfers between devices, over_link(): return lax.ppermute(piece, 'fsdp', pairs)  85.8 us
    ppermute x24, starting transfers between devices, over_link(): return lax.ppermute(piece, 'fsdp', pairs)  23 us
    pallas_call x11, Pallas kernels, place(): pl.pallas_call(functools.partial(place_kernel, spots, rows, len(held)), i...  15.7 us
    ppermute x38, starting transfers between devices, swap(): return lax.ppermute(value, 'fsdp', [(i, i ^ mask) for i in range(n)])  10.3 us
    pallas_call x2, Pallas kernels, update(): pl.pallas_call(functools.partial(update_kernel, count, chunk), in_specs=[...  9.49 us
    ppermute x38, waiting for transfers between devices, swap(): return lax.ppermute(value, 'fsdp', [(i, i ^ mask) for i in range(n)])  7.87 us
  transfers between devices with their start and end apart: 65, of which 23 were waited for; matrix products, arithmetic and copies ran while one was open for 0% of the time, Pallas kernels for 12%

profile of v1, /device:TPU:0, one launch (start us, length us, event | category | flops | bytes accessed | tf_op | source)
XLA Modules:
  0.0 165.9 jit_solution(9345083881600432260)
XLA Ops:
  0.6 5.8 %update.3 = (f32[512,1024]{1,0:T(8,128)S(1)}, f32[512,1024]{1,0:T(8,128)S(1)}, f32[2,1024]{1,0:T(2,128)S(1)}) custom-call(f32[1,512]{1,0:T(1,128)} %bitcast.5, f32[512,1024]{1,0:T(8,128)} %refs_0_.3, f32[512,1024]{1,0:T(8,128)} %refs_1_.3, f32[512,1024]{1,0:T(8,128)} %refs_2_.3, f32[512,1024]{1,0:T(8,128)} %refs_3_.1, f32[512,1024]{1,0:T(8,128)} %refs_4_.1, ...), custom_call_target="tpu_custom_call" | custom-call | flops 8388608 | bytes 12582912 | tf_op jit(solution)/shard_map/update/pallas_call | solution.py:91
  6.4 1.3 copy-done
  8.2 0.8 collective-permute-done.18
  9.0 2.8 %collective-permute-start.19 = (f32[2,1024]{1,0:T(2,128)S(1)}, f32[2,1024]{1,0:T(2,128)S(1)}, u32[]{:S(2)}, u32[]{:S(2)}) collective-permute-start(f32[2,1024]{1,0:T(2,128)S(1)} %add.7.refs_0_), channel_id=1, source_target_pairs={{0,8},{4,20},{8,0},{12,28},{16,24},{20,4},{24,16},{28,12},{1,9},{5... | collective-permute-start | bytes 24584 | tf_op jit(solution)/shard_map/ppermute | solution.py:272
  11.9 0.6 collective-permute-start.21
  12.5 1.0 collective-permute-done.19.refs_1_
  13.5 1.4 collective-permute-start.20
  14.9 2.1 %collective-permute-start.22 = (f32[2,1024]{1,0:T(2,128)S(1)}, f32[2,1024]{1,0:T(2,128)S(1)}, u32[]{:S(2)}, u32[]{:S(2)}) collective-permute-start(f32[2,1024]{1,0:T(2,128)S(1)} %collective-permute-done.21.refs_3_), channel_id=1, source_target_pairs={{0,4},{4,0},{8,12},{12,8},{16,20},{20,16},{24,28},{28,24},{1,5},{5... | collective-permute-start | bytes 24584 | tf_op jit(solution)/shard_map/ppermute | solution.py:20
  17.1 0.8 collective-permute-done.22.refs_4_
  17.9 1.6 copy-done.1
  19.5 0.9 narrow.7
  20.4 1.5 collective-permute-start.41
  21.9 3.7 %update.2 = (f32[512,1024]{1,0:T(8,128)S(1)}, f32[1,1024]{1,0:T(1,128)S(1)}) custom-call(f32[1,512]{1,0:T(1,128)} %bitcast.6, f32[512,1024]{1,0:T(8,128)} %refs_0_.2, f32[512,1024]{1,0:T(8,128)} %refs_1_.2, f32[512,1024]{1,0:T(8,128)} %refs_2_.2), custom_call_target="tpu_custom_call" | custom-call | flops 4194304 | bytes 6291456 | tf_op jit(solution)/shard_map/update/pallas_call | solution.py:91
  25.7 1.2 collective-permute-done
  26.8 0.5 collective-permute-start.1
  27.4 1.2 collective-permute-start.3
  28.6 1.9 %collective-permute-done.1.refs_1_ = f32[1,1024]{1,0:T(1,128)S(1)} collective-permute-done((f32[1,1024]{1,0:T(1,128)S(1)}, f32[1,1024]{1,0:T(1,128)S(1)}, u32[]{:S(2)}, u32[]{:S(2)}) %collective-permute-start.1) | collective-permute-done | bytes 4128 | tf_op jit(solution)/shard_map/ppermute | solution.py:275
  31.0 1.5 collective-permute-start.42
  32.5 0.6 collective-permute-start.44
  33.1 1.5 collective-permute-start.37
  34.6 2.6 %collective-permute-done.43.refs_10_ = bf16[96,1024]{1,0:T(8,128)(2,1)S(1)} collective-permute-done((bf16[96,1024]{1,0:T(8,128)(2,1)S(1)}, bf16[96,1024]{1,0:T(8,128)(2,1)S(1)}, u32[]{:S(2)}, u32[]{:S(2)}) %collective-permute-start.43) | collective-permute-done | bytes 196640 | tf_op jit(solution)/shard_map/ppermute | solution.py:206
  37.7 3.7 %collective-permute-done.42.refs_9_ = bf16[96,1024]{1,0:T(8,128)(2,1)S(1)} collective-permute-done((bf16[96,1024]{1,0:T(8,128)(2,1)S(1)}, bf16[96,1024]{1,0:T(8,128)(2,1)S(1)}, u32[]{:S(2)}, u32[]{:S(2)}) %collective-permute-start.42) | collective-permute-done | bytes 196640 | tf_op jit(solution)/shard_map/ppermute | solution.py:206
  41.9 1.5 collective-permute-start.40
  43.4 1.4 collective-permute-done.48.refs_4_
  45.0 0.7 narrow.5
  45.7 1.6 collective-permute-done.37.refs_4_
  47.8 0.7 collective-permute-done.39.refs_6_
  48.5 0.7 collective-permute-start.7
  49.1 6.3 %collective-permute-done.38.refs_5_ = bf16[160,1024]{1,0:T(8,128)(2,1)S(1)} collective-permute-done((bf16[160,1024]{1,0:T(8,128)(2,1)S(1)}, bf16[160,1024]{1,0:T(8,128)(2,1)S(1)}, u32[]{:S(2)}, u32[]{:S(2)}) %collective-permute-start.38) | collective-permute-done | bytes 327712 | tf_op jit(solution)/shard_map/ppermute | solution.py:206
  56.1 1.6 collective-permute-done.46.refs_2_
  57.8 5.0 %collective-permute-done.6.refs_4_ = bf16[192,1024]{1,0:T(8,128)(2,1)S(1)} collective-permute-done((bf16[192,1024]{1,0:T(8,128)(2,1)S(1)}, bf16[192,1024]{1,0:T(8,128)(2,1)S(1)}, u32[]{:S(2)}, u32[]{:S(2)}) %collective-permute-start.6) | collective-permute-done | bytes 393248 | tf_op jit(solution)/shard_map/ppermute | solution.py:206
  62.8 0.5 collective-permute-start.61
  63.6 0.9 narrow.6
  64.5 1.5 collective-permute-start.25
  66.0 0.8 narrow.4
  66.7 0.6 collective-permute-start.4
  67.3 1.3 collective-permute-start.26
  68.6 1.1 collective-permute-done.61.refs_1_
  69.7 15.9 %collective-permute-done.62.refs_2_ = bf16[96,1024]{1,0:T(8,128)(2,1)S(1)} collective-permute-done((bf16[96,1024]{1,0:T(8,128)(2,1)S(1)}, bf16[96,1024]{1,0:T(8,128)(2,1)S(1)}, u32[]{:S(2)}, u32[]{:S(2)}) %collective-permute-start.62) | collective-permute-done | bytes 196640 | tf_op jit(solution)/shard_map/ppermute | solution.py:206
  85.6 1.3 collective-permute-start.5
  87.5 1.8 %collective-permute-done.63.refs_1_ = bf16[96,1024]{1,0:T(8,128)(2,1)S(1)} collective-permute-done((bf16[96,1024]{1,0:T(8,128)(2,1)S(1)}, bf16[96,1024]{1,0:T(8,128)(2,1)S(1)}, u32[]{:S(2)}, u32[]{:S(2)}) %collective-permute-start.63) | collective-permute-done | bytes 196640 | tf_op jit(solution)/shard_map/ppermute | solution.py:20
  90.1 6.1 %collective-permute-done.5.refs_3_ = bf16[320,1024]{1,0:T(8,128)(2,1)S(1)} collective-permute-done((bf16[320,1024]{1,0:T(8,128)(2,1)S(1)}, bf16[320,1024]{1,0:T(8,128)(2,1)S(1)}, u32[]{:S(2)}, u32[]{:S(2)}) %collective-permute-start.5) | collective-permute-done | bytes 655392 | tf_op jit(solution)/shard_map/ppermute | solution.py:206
  96.2 1.3 collective-permute-start.23
  97.5 0.7 collective-permute-start.57
  98.2 1.5 collective-permute-start.24
  99.7 0.6 collective-permute-start.58
  100.3 19.5 %collective-permute-done.57.refs_1_ = bf16[160,1024]{1,0:T(8,128)(2,1)S(1)} collective-permute-done((bf16[160,1024]{1,0:T(8,128)(2,1)S(1)}, bf16[160,1024]{1,0:T(8,128)(2,1)S(1)}, u32[]{:S(2)}, u32[]{:S(2)}) %collective-permute-start.57) | collective-permute-done | bytes 327712 | tf_op jit(solution)/shard_map/ppermute | solution.py:206
  119.8 0.5 collective-permute-done.58.refs_2_
  120.7 1.5 collective-permute-start.15
  123.2 8.4 %collective-permute-done.15.refs_2_ = bf16[192,1024]{1,0:T(8,128)(2,1)S(1)} collective-permute-done((bf16[192,1024]{1,0:T(8,128)(2,1)S(1)}, bf16[192,1024]{1,0:T(8,128)(2,1)S(1)}, u32[]{:S(2)}, u32[]{:S(2)}) %collective-permute-start.15) | collective-permute-done | bytes 393248 | tf_op jit(solution)/shard_map/ppermute | solution.py:206
  132.1 2.1 %collective-permute-start.14 = (bf16[320,1024]{1,0:T(8,128)(2,1)S(1)}, bf16[320,1024]{1,0:T(8,128)(2,1)S(1)}, u32[]{:S(2)}, u32[]{:S(2)}) collective-permute-start(bf16[320,1024]{1,0:T(8,128)(2,1)S(1)} %collective-permute-done.4.refs_2_), channel_id=1, source_target_pairs={{0,16},{4,12},{8,24},{12,4},{16,0},{20,28},{24,8},{28,20},{1,17},{... | collective-permute-start | bytes 1966088 | tf_op jit(solution)/shard_map/ppermute | solution.py:206
  135.1 13.6 %collective-permute-done.14.refs_1_ = bf16[320,1024]{1,0:T(8,128)(2,1)S(1)} collective-permute-done((bf16[320,1024]{1,0:T(8,128)(2,1)S(1)}, bf16[320,1024]{1,0:T(8,128)(2,1)S(1)}, u32[]{:S(2)}, u32[]{:S(2)}) %collective-permute-start.14) | collective-permute-done | bytes 655392 | tf_op jit(solution)/shard_map/ppermute | solution.py:206
  148.7 0.7 collective-permute-done.33.refs_1_
  150.1 1.7 %place.17.refs_0_ = bf16[4096,1024]{1,0:T(8,128)(2,1)} custom-call(s32[1]{0:T(128)} %bitcast.me_ref, bf16[160,1024]{1,0:T(8,128)(2,1)S(1)} %get-tuple-element.31.refs_0_, bf16[160,1024]{1,0:T(8,128)(2,1)S(1)} %get-tuple-element.32.refs_1_, bf16[96,1024]{1,0:T(8,128)(2,1)S(1)} %get-tuple-element.33.refs_2_, bf16[96,1024]{1,0:T(8,128)(2,1)S(1)} %get-tuple-element.34.refs_3_, ...), custom_call_target="tpu_custom_call" | custom-call | flops 1572864 | bytes 6291456 | tf_op jit(solution)/shard_map/place/pallas_call | solution.py:189
  151.8 1.8 %place.18.refs_0_ = bf16[4096,1024]{1,0:T(8,128)(2,1)} custom-call(s32[1]{0:T(128)} %bitcast.me_ref, bf16[4096,1024]{1,0:T(8,128)(2,1)} %place.17.refs_0_, bf16[160,1024]{1,0:T(8,128)(2,1)S(1)} %collective-permute-done.45.refs_1_, bf16[160,1024]{1,0:T(8,128)(2,1)S(1)} %collective-permute-done.46.refs_2_, ...), custom_call_target="tpu_custom_call", output_to_operand_aliasing={{}: (1, {})} | custom-call | flops 1572864 | bytes 6291456 | tf_op jit(solution)/shard_map/place/pallas_call | solution.py:189
  153.6 1.1 place.19.refs_0_
  154.7 1.7 %place.11.refs_0_ = bf16[4096,1024]{1,0:T(8,128)(2,1)} custom-call(s32[1]{0:T(128)} %bitcast.me_ref, bf16[320,1024]{1,0:T(8,128)(2,1)S(1)} %get-tuple-element.24.refs_0_, bf16[192,1024]{1,0:T(8,128)(2,1)S(1)} %get-tuple-element.25.refs_1_, bf16[320,1024]{1,0:T(8,128)(2,1)S(1)} %collective-permute-done.4.refs_2_, ...), custom_call_target="tpu_custom_call" | custom-call | flops 1572864 | bytes 6291456 | tf_op jit(solution)/shard_map/place/pallas_call | solution.py:189
  156.4 0.8 place.20.refs_0_
  157.2 1.7 %place.14.refs_0_ = bf16[4096,1024]{1,0:T(8,128)(2,1)} custom-call(s32[1]{0:T(128)} %bitcast.me_ref, bf16[320,1024]{1,0:T(8,128)(2,1)S(1)} %get-tuple-element.28.refs_0_, bf16[192,1024]{1,0:T(8,128)(2,1)S(1)} %get-tuple-element.29.refs_1_, bf16[320,1024]{1,0:T(8,128)(2,1)S(1)} %collective-permute-done.23.refs_2_, ...), custom_call_target="tpu_custom_call" | custom-call | flops 1572864 | bytes 6291456 | tf_op jit(solution)/shard_map/place/pallas_call | solution.py:189
  158.9 0.8 place.21
  159.7 1.7 %place.12.refs_0_ = bf16[4096,1024]{1,0:T(8,128)(2,1)} custom-call(s32[1]{0:T(128)} %bitcast.me_ref, bf16[4096,1024]{1,0:T(8,128)(2,1)} %place.11.refs_0_, bf16[320,1024]{1,0:T(8,128)(2,1)S(1)} %collective-permute-done.8.refs_1_, bf16[192,1024]{1,0:T(8,128)(2,1)S(1)} %collective-permute-done.9.refs_2_, ...), custom_call_target="tpu_custom_call", output_to_operand_aliasing={{}: (1, {})} | custom-call | flops 1572864 | bytes 6291456 | tf_op jit(solution)/shard_map/place/pallas_call | solution.py:189
  161.4 1.7 %place.15.refs_0_ = bf16[4096,1024]{1,0:T(8,128)(2,1)} custom-call(s32[1]{0:T(128)} %bitcast.me_ref, bf16[4096,1024]{1,0:T(8,128)(2,1)} %place.14.refs_0_, bf16[320,1024]{1,0:T(8,128)(2,1)S(1)} %collective-permute-done.27.refs_1_, bf16[192,1024]{1,0:T(8,128)(2,1)S(1)} %collective-permute-done.28.refs_2_, ...), custom_call_target="tpu_custom_call", output_to_operand_aliasing={{}: (1, {})} | custom-call | flops 1572864 | bytes 6291456 | tf_op jit(solution)/shard_map/place/pallas_call | solution.py:189
  163.2 1.3 place.13
  164.5 1.3 place.16
  (89 shorter events, 8.7 us)
Async XLA Ops:
  7.7 1.3 collective-permute-start.18
  9.0 4.4 %collective-permute-start.19 = (f32[2,1024]{1,0:T(2,128)S(1)}, f32[2,1024]{1,0:T(2,128)S(1)}, u32[]{:S(2)}, u32[]{:S(2)}) collective-permute-start(f32[2,1024]{1,0:T(2,128)S(1)} %add.7.refs_0_), channel_id=1, source_target_pairs={{0,8},{4,20},{8,0},{12,28},{16,24},{20,4},{24,16},{28,12},{1,9},{5... | collective-permute-start | bytes 24584 | tf_op jit(solution)/shard_map/ppermute | solution.py:272
  11.9 3.1 %collective-permute-start.21 = (f32[2,1024]{1,0:T(2,128)S(1)}, f32[2,1024]{1,0:T(2,128)S(1)}, u32[]{:S(2)}, u32[]{:S(2)}) collective-permute-start(f32[2,1024]{1,0:T(2,128)S(1)} %add.7.refs_0_), channel_id=1, source_target_pairs={{4,28},{12,20},{20,12},{28,4},{5,29},{13,21},{21,13},{29,5},{6,30}... | collective-permute-start | bytes 24584 | tf_op jit(solution)/shard_map/ppermute | solution.py:273
  13.5 3.6 %collective-permute-start.20 = (f32[2,1024]{1,0:T(2,128)S(1)}, f32[2,1024]{1,0:T(2,128)S(1)}, u32[]{:S(2)}, u32[]{:S(2)}) collective-permute-start(f32[2,1024]{1,0:T(2,128)S(1)} %collective-permute-done.19.refs_1_), channel_id=1, source_target_pairs={{0,4},{4,0},{8,12},{12,8},{16,20},{20,16},{24,28},{28,24},{1,5},{5... | collective-permute-start | bytes 24584 | tf_op jit(solution)/shard_map/ppermute | solution.py:20
  14.9 3.0 %collective-permute-start.22 = (f32[2,1024]{1,0:T(2,128)S(1)}, f32[2,1024]{1,0:T(2,128)S(1)}, u32[]{:S(2)}, u32[]{:S(2)}) collective-permute-start(f32[2,1024]{1,0:T(2,128)S(1)} %collective-permute-done.21.refs_3_), channel_id=1, source_target_pairs={{0,4},{4,0},{8,12},{12,8},{16,20},{20,16},{24,28},{28,24},{1,5},{5... | collective-permute-start | bytes 24584 | tf_op jit(solution)/shard_map/ppermute | solution.py:20
  20.4 12.7 %collective-permute-start.41 = (bf16[96,1024]{1,0:T(8,128)(2,1)S(1)}, bf16[96,1024]{1,0:T(8,128)(2,1)S(1)}, u32[]{:S(2)}, u32[]{:S(2)}) collective-permute-start(bf16[96,1024]{1,0:T(8,128)(2,1)S(1)} %get-tuple-element.33.refs_2_), channel_id=1, source_target_pairs={{0,8},{4,20},{8,0},{12,28},{16,24},{20,4},{24,16},{28,12},{1,9},{5... | collective-permute-start | bytes 589832 | tf_op jit(solution)/shard_map/ppermute | solution.py:206
  26.8 3.6 %collective-permute-start.1 = (f32[1,1024]{1,0:T(1,128)S(1)}, f32[1,1024]{1,0:T(1,128)S(1)}, u32[]{:S(2)}, u32[]{:S(2)}) collective-permute-start(f32[1,1024]{1,0:T(1,128)S(1)} %add.6.refs_0_), channel_id=1, source_target_pairs={{0,8},{4,28},{8,0},{12,20},{16,24},{20,12},{24,16},{28,4},{1,9},{5... | collective-permute-start | bytes 12296 | tf_op jit(solution)/shard_map/ppermute | solution.py:275
  27.4 5.1 %collective-permute-start.3 = (f32[1,1024]{1,0:T(1,128)S(1)}, f32[1,1024]{1,0:T(1,128)S(1)}, u32[]{:S(2)}, u32[]{:S(2)}) collective-permute-start(f32[1,1024]{1,0:T(1,128)S(1)} %add.6.refs_0_), channel_id=1, source_target_pairs={{0,16},{4,20},{8,24},{12,28},{16,0},{20,4},{24,8},{28,12},{1,17},{... | collective-permute-start | bytes 12296 | tf_op jit(solution)/shard_map/ppermute | solution.py:20
  30.4 2.6 %collective-permute-start.2 = (f32[1,1024]{1,0:T(1,128)S(1)}, f32[1,1024]{1,0:T(1,128)S(1)}, u32[]{:S(2)}, u32[]{:S(2)}) collective-permute-start(f32[1,1024]{1,0:T(1,128)S(1)} %collective-permute-done.1.refs_1_), channel_id=1, source_target_pairs={{0,4},{4,0},{8,12},{12,8},{16,20},{20,16},{24,28},{28,24},{1,5},{5... | collective-permute-start | bytes 12296 | tf_op jit(solution)/shard_map/ppermute | solution.py:20
  30.5 6.8 %collective-permute-start.43 = (bf16[96,1024]{1,0:T(8,128)(2,1)S(1)}, bf16[96,1024]{1,0:T(8,128)(2,1)S(1)}, u32[]{:S(2)}, u32[]{:S(2)}) collective-permute-start(bf16[96,1024]{1,0:T(8,128)(2,1)S(1)} %get-tuple-element.34.refs_3_), channel_id=1, source_target_pairs={{0,16},{4,12},{8,24},{12,4},{16,0},{20,28},{24,8},{28,20},{1,17},{... | collective-permute-start | bytes 589832 | tf_op jit(solution)/shard_map/ppermute | solution.py:206
  31.0 10.5 %collective-permute-start.42 = (bf16[96,1024]{1,0:T(8,128)(2,1)S(1)}, bf16[96,1024]{1,0:T(8,128)(2,1)S(1)}, u32[]{:S(2)}, u32[]{:S(2)}) collective-permute-start(bf16[96,1024]{1,0:T(8,128)(2,1)S(1)} %get-tuple-element.33.refs_2_), channel_id=1, source_target_pairs={{0,16},{4,12},{8,24},{12,4},{16,0},{20,28},{24,8},{28,20},{1,17},{... | collective-permute-start | bytes 589832 | tf_op jit(solution)/shard_map/ppermute | solution.py:206
  32.5 9.5 %collective-permute-start.44 = (bf16[96,1024]{1,0:T(8,128)(2,1)S(1)}, bf16[96,1024]{1,0:T(8,128)(2,1)S(1)}, u32[]{:S(2)}, u32[]{:S(2)}) collective-permute-start(bf16[96,1024]{1,0:T(8,128)(2,1)S(1)} %get-tuple-element.34.refs_3_), channel_id=1, source_target_pairs={{0,8},{4,20},{8,0},{12,28},{16,24},{20,4},{24,16},{28,12},{1,9},{5... | collective-permute-start | bytes 589832 | tf_op jit(solution)/shard_map/ppermute | solution.py:206
  33.0 10.4 %collective-permute-start.47 = (bf16[96,1024]{1,0:T(8,128)(2,1)S(1)}, bf16[96,1024]{1,0:T(8,128)(2,1)S(1)}, u32[]{:S(2)}, u32[]{:S(2)}) collective-permute-start(bf16[96,1024]{1,0:T(8,128)(2,1)S(1)} %get-tuple-element.33.refs_2_), channel_id=1, source_target_pairs={{0,4},{4,0},{8,12},{12,8},{16,20},{20,16},{24,28},{28,24},{1,5},{5... | collective-permute-start | bytes 589832 | tf_op jit(solution)/shard_map/ppermute | solution.py:20
  33.1 14.2 %collective-permute-start.37 = (bf16[160,1024]{1,0:T(8,128)(2,1)S(1)}, bf16[160,1024]{1,0:T(8,128)(2,1)S(1)}, u32[]{:S(2)}, u32[]{:S(2)}) collective-permute-start(bf16[160,1024]{1,0:T(8,128)(2,1)S(1)} %get-tuple-element.31.refs_0_), channel_id=1, source_target_pairs={{0,8},{4,20},{8,0},{12,28},{16,24},{20,4},{24,16},{28,12},{1,9},{5... | collective-permute-start | bytes 983048 | tf_op jit(solution)/shard_map/ppermute | solution.py:206
  37.2 11.2 %collective-permute-start.39 = (bf16[160,1024]{1,0:T(8,128)(2,1)S(1)}, bf16[160,1024]{1,0:T(8,128)(2,1)S(1)}, u32[]{:S(2)}, u32[]{:S(2)}) collective-permute-start(bf16[160,1024]{1,0:T(8,128)(2,1)S(1)} %get-tuple-element.32.refs_1_), channel_id=1, source_target_pairs={{0,16},{4,12},{8,24},{12,4},{16,0},{20,28},{24,8},{28,20},{1,17},{... | collective-permute-start | bytes 983048 | tf_op jit(solution)/shard_map/ppermute | solution.py:206
  41.4 14.0 %collective-permute-start.38 = (bf16[160,1024]{1,0:T(8,128)(2,1)S(1)}, bf16[160,1024]{1,0:T(8,128)(2,1)S(1)}, u32[]{:S(2)}, u32[]{:S(2)}) collective-permute-start(bf16[160,1024]{1,0:T(8,128)(2,1)S(1)} %get-tuple-element.31.refs_0_), channel_id=1, source_target_pairs={{0,16},{4,12},{8,24},{12,4},{16,0},{20,28},{24,8},{28,20},{1,17},{... | collective-permute-start | bytes 983048 | tf_op jit(solution)/shard_map/ppermute | solution.py:206
  41.9 13.5 %collective-permute-start.40 = (bf16[160,1024]{1,0:T(8,128)(2,1)S(1)}, bf16[160,1024]{1,0:T(8,128)(2,1)S(1)}, u32[]{:S(2)}, u32[]{:S(2)}) collective-permute-start(bf16[160,1024]{1,0:T(8,128)(2,1)S(1)} %get-tuple-element.32.refs_1_), channel_id=1, source_target_pairs={{0,8},{4,20},{8,0},{12,28},{16,24},{20,4},{24,16},{28,12},{1,9},{5... | collective-permute-start | bytes 983048 | tf_op jit(solution)/shard_map/ppermute | solution.py:206
  43.4 1.4 collective-permute-start.48
  44.9 11.1 %collective-permute-start.45 = (bf16[160,1024]{1,0:T(8,128)(2,1)S(1)}, bf16[160,1024]{1,0:T(8,128)(2,1)S(1)}, u32[]{:S(2)}, u32[]{:S(2)}) collective-permute-start(bf16[160,1024]{1,0:T(8,128)(2,1)S(1)} %get-tuple-element.31.refs_0_), channel_id=1, source_target_pairs={{0,4},{4,0},{8,12},{12,8},{16,20},{20,16},{24,28},{28,24},{1,5},{5... | collective-permute-start | bytes 983048 | tf_op jit(solution)/shard_map/ppermute | solution.py:20
  47.3 15.5 %collective-permute-start.6 = (bf16[192,1024]{1,0:T(8,128)(2,1)S(1)}, bf16[192,1024]{1,0:T(8,128)(2,1)S(1)}, u32[]{:S(2)}, u32[]{:S(2)}) collective-permute-start(bf16[192,1024]{1,0:T(8,128)(2,1)S(1)} %get-tuple-element.25.refs_1_), channel_id=1, source_target_pairs={{0,16},{4,12},{8,24},{12,4},{16,0},{20,28},{24,8},{28,20},{1,17},{... | collective-permute-start | bytes 1179656 | tf_op jit(solution)/shard_map/ppermute | solution.py:206
  48.5 14.4 %collective-permute-start.7 = (bf16[192,1024]{1,0:T(8,128)(2,1)S(1)}, bf16[192,1024]{1,0:T(8,128)(2,1)S(1)}, u32[]{:S(2)}, u32[]{:S(2)}) collective-permute-start(bf16[192,1024]{1,0:T(8,128)(2,1)S(1)} %get-tuple-element.25.refs_1_), channel_id=1, source_target_pairs={{0,8},{4,20},{8,0},{12,28},{16,24},{20,4},{24,16},{28,12},{1,9},{5... | collective-permute-start | bytes 1179656 | tf_op jit(solution)/shard_map/ppermute | solution.py:206
  55.5 7.8 %collective-permute-start.9 = (bf16[192,1024]{1,0:T(8,128)(2,1)S(1)}, bf16[192,1024]{1,0:T(8,128)(2,1)S(1)}, u32[]{:S(2)}, u32[]{:S(2)}) collective-permute-start(bf16[192,1024]{1,0:T(8,128)(2,1)S(1)} %get-tuple-element.25.refs_1_), channel_id=1, source_target_pairs={{0,4},{4,0},{8,12},{12,8},{16,20},{20,16},{24,28},{28,24},{1,5},{5... | collective-permute-start | bytes 1179656 | tf_op jit(solution)/shard_map/ppermute | solution.py:20
  55.5 2.2 %collective-permute-start.46 = (bf16[160,1024]{1,0:T(8,128)(2,1)S(1)}, bf16[160,1024]{1,0:T(8,128)(2,1)S(1)}, u32[]{:S(2)}, u32[]{:S(2)}) collective-permute-start(bf16[160,1024]{1,0:T(8,128)(2,1)S(1)} %get-tuple-element.32.refs_1_), channel_id=1, source_target_pairs={{0,4},{4,0},{8,12},{12,8},{16,20},{20,16},{24,28},{28,24},{1,5},{5... | collective-permute-start | bytes 983048 | tf_op jit(solution)/shard_map/ppermute | solution.py:20
  56.0 8.5 %collective-permute-start.53 = (bf16[96,1024]{1,0:T(8,128)(2,1)S(1)}, bf16[96,1024]{1,0:T(8,128)(2,1)S(1)}, u32[]{:S(2)}, u32[]{:S(2)}) collective-permute-start(bf16[96,1024]{1,0:T(8,128)(2,1)S(1)} %collective-permute-done.41.refs_8_), channel_id=1, source_target_pairs={{0,4},{4,0},{8,12},{12,8},{16,20},{20,16},{24,28},{28,24},{1,5},{5... | collective-permute-start | bytes 589832 | tf_op jit(solution)/shard_map/ppermute | solution.py:20
  57.7 9.1 %collective-permute-start.55 = (bf16[96,1024]{1,0:T(8,128)(2,1)S(1)}, bf16[96,1024]{1,0:T(8,128)(2,1)S(1)}, u32[]{:S(2)}, u32[]{:S(2)}) collective-permute-start(bf16[96,1024]{1,0:T(8,128)(2,1)S(1)} %collective-permute-done.43.refs_10_), channel_id=1, source_target_pairs={{0,4},{4,0},{8,12},{12,8},{16,20},{20,16},{24,28},{28,24},{1,5},{5... | collective-permute-start | bytes 589832 | tf_op jit(solution)/shard_map/ppermute | solution.py:20
  62.8 4.5 %collective-permute-start.54 = (bf16[96,1024]{1,0:T(8,128)(2,1)S(1)}, bf16[96,1024]{1,0:T(8,128)(2,1)S(1)}, u32[]{:S(2)}, u32[]{:S(2)}) collective-permute-start(bf16[96,1024]{1,0:T(8,128)(2,1)S(1)} %collective-permute-done.42.refs_9_), channel_id=1, source_target_pairs={{0,4},{4,0},{8,12},{12,8},{16,20},{20,16},{24,28},{28,24},{1,5},{5... | collective-permute-start | bytes 589832 | tf_op jit(solution)/shard_map/ppermute | solution.py:20
  62.8 6.8 %collective-permute-start.61 = (bf16[96,1024]{1,0:T(8,128)(2,1)S(1)}, bf16[96,1024]{1,0:T(8,128)(2,1)S(1)}, u32[]{:S(2)}, u32[]{:S(2)}) collective-permute-start(bf16[96,1024]{1,0:T(8,128)(2,1)S(1)} %collective-permute-done.41.refs_8_), channel_id=1, source_target_pairs={{0,16},{4,12},{8,24},{12,4},{16,0},{20,28},{24,8},{28,20},{1,17},{... | collective-permute-start | bytes 589832 | tf_op jit(solution)/shard_map/ppermute | solution.py:206
  63.3 5.3 %collective-permute-start.56 = (bf16[96,1024]{1,0:T(8,128)(2,1)S(1)}, bf16[96,1024]{1,0:T(8,128)(2,1)S(1)}, u32[]{:S(2)}, u32[]{:S(2)}) collective-permute-start(bf16[96,1024]{1,0:T(8,128)(2,1)S(1)} %collective-permute-done.44.refs_11_), channel_id=1, source_target_pairs={{0,4},{4,0},{8,12},{12,8},{16,20},{20,16},{24,28},{28,24},{1,5},{5... | collective-permute-start | bytes 589832 | tf_op jit(solution)/shard_map/ppermute | solution.py:20
  64.5 22.4 %collective-permute-start.25 = (bf16[192,1024]{1,0:T(8,128)(2,1)S(1)}, bf16[192,1024]{1,0:T(8,128)(2,1)S(1)}, u32[]{:S(2)}, u32[]{:S(2)}) collective-permute-start(bf16[192,1024]{1,0:T(8,128)(2,1)S(1)} %get-tuple-element.29.refs_1_), channel_id=1, source_target_pairs={{0,8},{4,20},{8,0},{12,28},{16,24},{20,4},{24,16},{28,12},{1,9},{5... | collective-permute-start | bytes 1179656 | tf_op jit(solution)/shard_map/ppermute | solution.py:206
  66.7 23.1 %collective-permute-start.4 = (bf16[320,1024]{1,0:T(8,128)(2,1)S(1)}, bf16[320,1024]{1,0:T(8,128)(2,1)S(1)}, u32[]{:S(2)}, u32[]{:S(2)}) collective-permute-start(bf16[320,1024]{1,0:T(8,128)(2,1)S(1)} %get-tuple-element.24.refs_0_), channel_id=1, source_target_pairs={{0,8},{4,20},{8,0},{12,28},{16,24},{20,4},{24,16},{28,12},{1,9},{5... | collective-permute-start | bytes 1966088 | tf_op jit(solution)/shard_map/ppermute | solution.py:206
  67.3 19.6 %collective-permute-start.26 = (bf16[192,1024]{1,0:T(8,128)(2,1)S(1)}, bf16[192,1024]{1,0:T(8,128)(2,1)S(1)}, u32[]{:S(2)}, u32[]{:S(2)}) collective-permute-start(bf16[192,1024]{1,0:T(8,128)(2,1)S(1)} %get-tuple-element.29.refs_1_), channel_id=1, source_target_pairs={{0,16},{4,12},{8,24},{12,4},{16,0},{20,28},{24,8},{28,20},{1,17},{... | collective-permute-start | bytes 1179656 | tf_op jit(solution)/shard_map/ppermute | solution.py:206
  68.6 18.8 %collective-permute-start.28 = (bf16[192,1024]{1,0:T(8,128)(2,1)S(1)}, bf16[192,1024]{1,0:T(8,128)(2,1)S(1)}, u32[]{:S(2)}, u32[]{:S(2)}) collective-permute-start(bf16[192,1024]{1,0:T(8,128)(2,1)S(1)} %get-tuple-element.29.refs_1_), channel_id=1, source_target_pairs={{0,4},{4,0},{8,12},{12,8},{16,20},{20,16},{24,28},{28,24},{1,5},{5... | collective-permute-start | bytes 1179656 | tf_op jit(solution)/shard_map/ppermute | solution.py:20
  69.7 15.9 %collective-permute-start.62 = (bf16[96,1024]{1,0:T(8,128)(2,1)S(1)}, bf16[96,1024]{1,0:T(8,128)(2,1)S(1)}, u32[]{:S(2)}, u32[]{:S(2)}) collective-permute-start(bf16[96,1024]{1,0:T(8,128)(2,1)S(1)} %collective-permute-done.43.refs_10_), channel_id=1, source_target_pairs={{0,8},{4,20},{8,0},{12,28},{16,24},{20,4},{24,16},{28,12},{1,9},{5... | collective-permute-start | bytes 589832 | tf_op jit(solution)/shard_map/ppermute | solution.py:206
  85.6 10.6 %collective-permute-start.5 = (bf16[320,1024]{1,0:T(8,128)(2,1)S(1)}, bf16[320,1024]{1,0:T(8,128)(2,1)S(1)}, u32[]{:S(2)}, u32[]{:S(2)}) collective-permute-start(bf16[320,1024]{1,0:T(8,128)(2,1)S(1)} %get-tuple-element.24.refs_0_), channel_id=1, source_target_pairs={{0,16},{4,12},{8,24},{12,4},{16,0},{20,28},{24,8},{28,20},{1,17},{... | collective-permute-start | bytes 1966088 | tf_op jit(solution)/shard_map/ppermute | solution.py:206
  86.9 9.3 %collective-permute-start.8 = (bf16[320,1024]{1,0:T(8,128)(2,1)S(1)}, bf16[320,1024]{1,0:T(8,128)(2,1)S(1)}, u32[]{:S(2)}, u32[]{:S(2)}) collective-permute-start(bf16[320,1024]{1,0:T(8,128)(2,1)S(1)} %get-tuple-element.24.refs_0_), channel_id=1, source_target_pairs={{0,4},{4,0},{8,12},{12,8},{16,20},{20,16},{24,28},{28,24},{1,5},{5... | collective-permute-start | bytes 1966088 | tf_op jit(solution)/shard_map/ppermute | solution.py:20
  86.9 2.4 %collective-permute-start.63 = (bf16[96,1024]{1,0:T(8,128)(2,1)S(1)}, bf16[96,1024]{1,0:T(8,128)(2,1)S(1)}, u32[]{:S(2)}, u32[]{:S(2)}) collective-permute-start(bf16[96,1024]{1,0:T(8,128)(2,1)S(1)} %collective-permute-done.61.refs_1_), channel_id=1, source_target_pairs={{0,4},{4,0},{8,12},{12,8},{16,20},{20,16},{24,28},{28,24},{1,5},{5... | collective-permute-start | bytes 589832 | tf_op jit(solution)/shard_map/ppermute | solution.py:20
  87.4 2.1 %collective-permute-start.64 = (bf16[96,1024]{1,0:T(8,128)(2,1)S(1)}, bf16[96,1024]{1,0:T(8,128)(2,1)S(1)}, u32[]{:S(2)}, u32[]{:S(2)}) collective-permute-start(bf16[96,1024]{1,0:T(8,128)(2,1)S(1)} %collective-permute-done.62.refs_2_), channel_id=1, source_target_pairs={{0,4},{4,0},{8,12},{12,8},{16,20},{20,16},{24,28},{28,24},{1,5},{5... | collective-permute-start | bytes 589832 | tf_op jit(solution)/shard_map/ppermute | solution.py:20
  89.3 8.2 %collective-permute-start.49 = (bf16[160,1024]{1,0:T(8,128)(2,1)S(1)}, bf16[160,1024]{1,0:T(8,128)(2,1)S(1)}, u32[]{:S(2)}, u32[]{:S(2)}) collective-permute-start(bf16[160,1024]{1,0:T(8,128)(2,1)S(1)} %collective-permute-done.37.refs_4_), channel_id=1, source_target_pairs={{0,4},{4,0},{8,12},{12,8},{16,20},{20,16},{24,28},{28,24},{1,5},{5... | collective-permute-start | bytes 983048 | tf_op jit(solution)/shard_map/ppermute | solution.py:20
  89.6 8.7 %collective-permute-start.51 = (bf16[160,1024]{1,0:T(8,128)(2,1)S(1)}, bf16[160,1024]{1,0:T(8,128)(2,1)S(1)}, u32[]{:S(2)}, u32[]{:S(2)}) collective-permute-start(bf16[160,1024]{1,0:T(8,128)(2,1)S(1)} %collective-permute-done.39.refs_6_), channel_id=1, source_target_pairs={{0,4},{4,0},{8,12},{12,8},{16,20},{20,16},{24,28},{28,24},{1,5},{5... | collective-permute-start | bytes 983048 | tf_op jit(solution)/shard_map/ppermute | solution.py:20
  89.8 9.9 %collective-permute-start.50 = (bf16[160,1024]{1,0:T(8,128)(2,1)S(1)}, bf16[160,1024]{1,0:T(8,128)(2,1)S(1)}, u32[]{:S(2)}, u32[]{:S(2)}) collective-permute-start(bf16[160,1024]{1,0:T(8,128)(2,1)S(1)} %collective-permute-done.38.refs_5_), channel_id=1, source_target_pairs={{0,4},{4,0},{8,12},{12,8},{16,20},{20,16},{24,28},{28,24},{1,5},{5... | collective-permute-start | bytes 983048 | tf_op jit(solution)/shard_map/ppermute | solution.py:20
  96.2 3.5 %collective-permute-start.52 = (bf16[160,1024]{1,0:T(8,128)(2,1)S(1)}, bf16[160,1024]{1,0:T(8,128)(2,1)S(1)}, u32[]{:S(2)}, u32[]{:S(2)}) collective-permute-start(bf16[160,1024]{1,0:T(8,128)(2,1)S(1)} %collective-permute-done.40.refs_7_), channel_id=1, source_target_pairs={{0,4},{4,0},{8,12},{12,8},{16,20},{20,16},{24,28},{28,24},{1,5},{5... | collective-permute-start | bytes 983048 | tf_op jit(solution)/shard_map/ppermute | solution.py:20
  96.2 24.5 %collective-permute-start.23 = (bf16[320,1024]{1,0:T(8,128)(2,1)S(1)}, bf16[320,1024]{1,0:T(8,128)(2,1)S(1)}, u32[]{:S(2)}, u32[]{:S(2)}) collective-permute-start(bf16[320,1024]{1,0:T(8,128)(2,1)S(1)} %get-tuple-element.28.refs_0_), channel_id=1, source_target_pairs={{0,16},{4,12},{8,24},{12,4},{16,0},{20,28},{24,8},{28,20},{1,17},{... | collective-permute-start | bytes 1966088 | tf_op jit(solution)/shard_map/ppermute | solution.py:206
  97.5 22.3 %collective-permute-start.57 = (bf16[160,1024]{1,0:T(8,128)(2,1)S(1)}, bf16[160,1024]{1,0:T(8,128)(2,1)S(1)}, u32[]{:S(2)}, u32[]{:S(2)}) collective-permute-start(bf16[160,1024]{1,0:T(8,128)(2,1)S(1)} %collective-permute-done.37.refs_4_), channel_id=1, source_target_pairs={{0,16},{4,12},{8,24},{12,4},{16,0},{20,28},{24,8},{28,20},{1,17},{... | collective-permute-start | bytes 983048 | tf_op jit(solution)/shard_map/ppermute | solution.py:206
  98.2 23.9 %collective-permute-start.24 = (bf16[320,1024]{1,0:T(8,128)(2,1)S(1)}, bf16[320,1024]{1,0:T(8,128)(2,1)S(1)}, u32[]{:S(2)}, u32[]{:S(2)}) collective-permute-start(bf16[320,1024]{1,0:T(8,128)(2,1)S(1)} %get-tuple-element.28.refs_0_), channel_id=1, source_target_pairs={{0,8},{4,20},{8,0},{12,28},{16,24},{20,4},{24,16},{28,12},{1,9},{5... | collective-permute-start | bytes 1966088 | tf_op jit(solution)/shard_map/ppermute | solution.py:206
  99.7 22.4 %collective-permute-start.27 = (bf16[320,1024]{1,0:T(8,128)(2,1)S(1)}, bf16[320,1024]{1,0:T(8,128)(2,1)S(1)}, u32[]{:S(2)}, u32[]{:S(2)}) collective-permute-start(bf16[320,1024]{1,0:T(8,128)(2,1)S(1)} %get-tuple-element.28.refs_0_), channel_id=1, source_target_pairs={{0,4},{4,0},{8,12},{12,8},{16,20},{20,16},{24,28},{28,24},{1,5},{5... | collective-permute-start | bytes 1966088 | tf_op jit(solution)/shard_map/ppermute | solution.py:20
  99.7 20.7 %collective-permute-start.58 = (bf16[160,1024]{1,0:T(8,128)(2,1)S(1)}, bf16[160,1024]{1,0:T(8,128)(2,1)S(1)}, u32[]{:S(2)}, u32[]{:S(2)}) collective-permute-start(bf16[160,1024]{1,0:T(8,128)(2,1)S(1)} %collective-permute-done.39.refs_6_), channel_id=1, source_target_pairs={{0,8},{4,20},{8,0},{12,28},{16,24},{20,4},{24,16},{28,12},{1,9},{5... | collective-permute-start | bytes 983048 | tf_op jit(solution)/shard_map/ppermute | solution.py:206
  119.8 2.8 %collective-permute-start.12 = (bf16[192,1024]{1,0:T(8,128)(2,1)S(1)}, bf16[192,1024]{1,0:T(8,128)(2,1)S(1)}, u32[]{:S(2)}, u32[]{:S(2)}) collective-permute-start(bf16[192,1024]{1,0:T(8,128)(2,1)S(1)} %collective-permute-done.6.refs_4_), channel_id=1, source_target_pairs={{0,4},{4,0},{8,12},{12,8},{16,20},{20,16},{24,28},{28,24},{1,5},{5... | collective-permute-start | bytes 1179656 | tf_op jit(solution)/shard_map/ppermute | solution.py:20
  120.4 2.8 %collective-permute-start.13 = (bf16[192,1024]{1,0:T(8,128)(2,1)S(1)}, bf16[192,1024]{1,0:T(8,128)(2,1)S(1)}, u32[]{:S(2)}, u32[]{:S(2)}) collective-permute-start(bf16[192,1024]{1,0:T(8,128)(2,1)S(1)} %collective-permute-done.7.refs_5_), channel_id=1, source_target_pairs={{0,4},{4,0},{8,12},{12,8},{16,20},{20,16},{24,28},{28,24},{1,5},{5... | collective-permute-start | bytes 1179656 | tf_op jit(solution)/shard_map/ppermute | solution.py:20
  120.7 10.9 %collective-permute-start.15 = (bf16[192,1024]{1,0:T(8,128)(2,1)S(1)}, bf16[192,1024]{1,0:T(8,128)(2,1)S(1)}, u32[]{:S(2)}, u32[]{:S(2)}) collective-permute-start(bf16[192,1024]{1,0:T(8,128)(2,1)S(1)} %collective-permute-done.6.refs_4_), channel_id=1, source_target_pairs={{0,8},{4,20},{8,0},{12,28},{16,24},{20,4},{24,16},{28,12},{1,9},{5... | collective-permute-start | bytes 1179656 | tf_op jit(solution)/shard_map/ppermute | solution.py:206
  122.1 9.4 %collective-permute-start.31 = (bf16[192,1024]{1,0:T(8,128)(2,1)S(1)}, bf16[192,1024]{1,0:T(8,128)(2,1)S(1)}, u32[]{:S(2)}, u32[]{:S(2)}) collective-permute-start(bf16[192,1024]{1,0:T(8,128)(2,1)S(1)} %collective-permute-done.25.refs_4_), channel_id=1, source_target_pairs={{0,4},{4,0},{8,12},{12,8},{16,20},{20,16},{24,28},{28,24},{1,5},{5... | collective-permute-start | bytes 1179656 | tf_op jit(solution)/shard_map/ppermute | solution.py:20
  122.1 9.9 %collective-permute-start.32 = (bf16[192,1024]{1,0:T(8,128)(2,1)S(1)}, bf16[192,1024]{1,0:T(8,128)(2,1)S(1)}, u32[]{:S(2)}, u32[]{:S(2)}) collective-permute-start(bf16[192,1024]{1,0:T(8,128)(2,1)S(1)} %collective-permute-done.26.refs_5_), channel_id=1, source_target_pairs={{0,4},{4,0},{8,12},{12,8},{16,20},{20,16},{24,28},{28,24},{1,5},{5... | collective-permute-start | bytes 1179656 | tf_op jit(solution)/shard_map/ppermute | solution.py:20
  122.6 11.5 %collective-permute-start.34 = (bf16[192,1024]{1,0:T(8,128)(2,1)S(1)}, bf16[192,1024]{1,0:T(8,128)(2,1)S(1)}, u32[]{:S(2)}, u32[]{:S(2)}) collective-permute-start(bf16[192,1024]{1,0:T(8,128)(2,1)S(1)} %collective-permute-done.25.refs_4_), channel_id=1, source_target_pairs={{0,16},{4,12},{8,24},{12,4},{16,0},{20,28},{24,8},{28,20},{1,17},{... | collective-permute-start | bytes 1179656 | tf_op jit(solution)/shard_map/ppermute | solution.py:206
  123.2 11.4 %collective-permute-start.59 = (bf16[160,1024]{1,0:T(8,128)(2,1)S(1)}, bf16[160,1024]{1,0:T(8,128)(2,1)S(1)}, u32[]{:S(2)}, u32[]{:S(2)}) collective-permute-start(bf16[160,1024]{1,0:T(8,128)(2,1)S(1)} %collective-permute-done.57.refs_1_), channel_id=1, source_target_pairs={{0,4},{4,0},{8,12},{12,8},{16,20},{20,16},{24,28},{28,24},{1,5},{5... | collective-permute-start | bytes 983048 | tf_op jit(solution)/shard_map/ppermute | solution.py:20
  131.6 3.0 %collective-permute-start.60 = (bf16[160,1024]{1,0:T(8,128)(2,1)S(1)}, bf16[160,1024]{1,0:T(8,128)(2,1)S(1)}, u32[]{:S(2)}, u32[]{:S(2)}) collective-permute-start(bf16[160,1024]{1,0:T(8,128)(2,1)S(1)} %collective-permute-done.58.refs_2_), channel_id=1, source_target_pairs={{0,4},{4,0},{8,12},{12,8},{16,20},{20,16},{24,28},{28,24},{1,5},{5... | collective-permute-start | bytes 983048 | tf_op jit(solution)/shard_map/ppermute | solution.py:20
  131.6 3.5 %collective-permute-start.10 = (bf16[320,1024]{1,0:T(8,128)(2,1)S(1)}, bf16[320,1024]{1,0:T(8,128)(2,1)S(1)}, u32[]{:S(2)}, u32[]{:S(2)}) collective-permute-start(bf16[320,1024]{1,0:T(8,128)(2,1)S(1)} %collective-permute-done.4.refs_2_), channel_id=1, source_target_pairs={{0,4},{4,0},{8,12},{12,8},{16,20},{20,16},{24,28},{28,24},{1,5},{5... | collective-permute-start | bytes 1966088 | tf_op jit(solution)/shard_map/ppermute | solution.py:20
  132.1 16.6 %collective-permute-start.14 = (bf16[320,1024]{1,0:T(8,128)(2,1)S(1)}, bf16[320,1024]{1,0:T(8,128)(2,1)S(1)}, u32[]{:S(2)}, u32[]{:S(2)}) collective-permute-start(bf16[320,1024]{1,0:T(8,128)(2,1)S(1)} %collective-permute-done.4.refs_2_), channel_id=1, source_target_pairs={{0,16},{4,12},{8,24},{12,4},{16,0},{20,28},{24,8},{28,20},{1,17},{... | collective-permute-start | bytes 1966088 | tf_op jit(solution)/shard_map/ppermute | solution.py:206
  134.2 15.2 %collective-permute-start.33 = (bf16[320,1024]{1,0:T(8,128)(2,1)S(1)}, bf16[320,1024]{1,0:T(8,128)(2,1)S(1)}, u32[]{:S(2)}, u32[]{:S(2)}) collective-permute-start(bf16[320,1024]{1,0:T(8,128)(2,1)S(1)} %collective-permute-done.23.refs_2_), channel_id=1, source_target_pairs={{0,8},{4,20},{8,0},{12,28},{16,24},{20,4},{24,16},{28,12},{1,9},{5... | collective-permute-start | bytes 1966088 | tf_op jit(solution)/shard_map/ppermute | solution.py:206
  134.5 15.0 %collective-permute-start.11 = (bf16[320,1024]{1,0:T(8,128)(2,1)S(1)}, bf16[320,1024]{1,0:T(8,128)(2,1)S(1)}, u32[]{:S(2)}, u32[]{:S(2)}) collective-permute-start(bf16[320,1024]{1,0:T(8,128)(2,1)S(1)} %collective-permute-done.5.refs_3_), channel_id=1, source_target_pairs={{0,4},{4,0},{8,12},{12,8},{16,20},{20,16},{24,28},{28,24},{1,5},{5... | collective-permute-start | bytes 1966088 | tf_op jit(solution)/shard_map/ppermute | solution.py:20
  134.5 15.4 %collective-permute-start.29 = (bf16[320,1024]{1,0:T(8,128)(2,1)S(1)}, bf16[320,1024]{1,0:T(8,128)(2,1)S(1)}, u32[]{:S(2)}, u32[]{:S(2)}) collective-permute-start(bf16[320,1024]{1,0:T(8,128)(2,1)S(1)} %collective-permute-done.23.refs_2_), channel_id=1, source_target_pairs={{0,4},{4,0},{8,12},{12,8},{16,20},{20,16},{24,28},{28,24},{1,5},{5... | collective-permute-start | bytes 1966088 | tf_op jit(solution)/shard_map/ppermute | solution.py:20
  135.0 26.4 %collective-permute-start.30 = (bf16[320,1024]{1,0:T(8,128)(2,1)S(1)}, bf16[320,1024]{1,0:T(8,128)(2,1)S(1)}, u32[]{:S(2)}, u32[]{:S(2)}) collective-permute-start(bf16[320,1024]{1,0:T(8,128)(2,1)S(1)} %collective-permute-done.24.refs_3_), channel_id=1, source_target_pairs={{0,4},{4,0},{8,12},{12,8},{16,20},{20,16},{24,28},{28,24},{1,5},{5... | collective-permute-start | bytes 1966088 | tf_op jit(solution)/shard_map/ppermute | solution.py:20
  148.7 14.5 %collective-permute-start.16 = (bf16[320,1024]{1,0:T(8,128)(2,1)S(1)}, bf16[320,1024]{1,0:T(8,128)(2,1)S(1)}, u32[]{:S(2)}, u32[]{:S(2)}) collective-permute-start(bf16[320,1024]{1,0:T(8,128)(2,1)S(1)} %collective-permute-done.14.refs_1_), channel_id=1, source_target_pairs={{0,4},{4,0},{8,12},{12,8},{16,20},{20,16},{24,28},{28,24},{1,5},{5... | collective-permute-start | bytes 1966088 | tf_op jit(solution)/shard_map/ppermute | solution.py:20
  149.4 15.1 %collective-permute-start.35 = (bf16[320,1024]{1,0:T(8,128)(2,1)S(1)}, bf16[320,1024]{1,0:T(8,128)(2,1)S(1)}, u32[]{:S(2)}, u32[]{:S(2)}) collective-permute-start(bf16[320,1024]{1,0:T(8,128)(2,1)S(1)} %collective-permute-done.33.refs_1_), channel_id=1, source_target_pairs={{0,4},{4,0},{8,12},{12,8},{16,20},{20,16},{24,28},{28,24},{1,5},{5... | collective-permute-start | bytes 1966088 | tf_op jit(solution)/shard_map/ppermute | solution.py:20
  149.6 13.6 %collective-permute-start.17 = (bf16[192,1024]{1,0:T(8,128)(2,1)S(1)}, bf16[192,1024]{1,0:T(8,128)(2,1)S(1)}, u32[]{:S(2)}, u32[]{:S(2)}) collective-permute-start(bf16[192,1024]{1,0:T(8,128)(2,1)S(1)} %collective-permute-done.15.refs_2_), channel_id=1, source_target_pairs={{0,4},{4,0},{8,12},{12,8},{16,20},{20,16},{24,28},{28,24},{1,5},{5... | collective-permute-start | bytes 1179656 | tf_op jit(solution)/shard_map/ppermute | solution.py:20
  149.9 14.6 %collective-permute-start.36 = (bf16[192,1024]{1,0:T(8,128)(2,1)S(1)}, bf16[192,1024]{1,0:T(8,128)(2,1)S(1)}, u32[]{:S(2)}, u32[]{:S(2)}) collective-permute-start(bf16[192,1024]{1,0:T(8,128)(2,1)S(1)} %collective-permute-done.34.refs_2_), channel_id=1, source_target_pairs={{0,4},{4,0},{8,12},{12,8},{16,20},{20,16},{24,28},{28,24},{1,5},{5... | collective-permute-start | bytes 1179656 | tf_op jit(solution)/shard_map/ppermute | solution.py:20
  (3 other events, 4.1 us)

commit v2 on v1

--- a/solution.py
+++ b/solution.py
@@ -43,9 +43,9 @@
     return [slice(at, at + LANES) for at in range(0, cols, LANES)]
 
 
-def update_kernel(count, chunk, gain_ref, *refs):
+def update_kernel(count, chunk, tails, gain_hbm, *refs):
     ins, kept, sums = refs[: 3 * count], refs[3 * count : 4 * count], refs[4 * count]
-    held, (acc_ref, column_ref, sems) = refs[4 * count + 1 : -3], refs[-3:]
+    held, (acc_ref, column_ref, gain_ref, sems, gain_sem) = refs[4 * count + 1 + tails : -5], refs[-5:]
     rows, cols = kept[0].shape
     chunks = rows // chunk
 
@@ -53,10 +53,13 @@
         at = pl.ds(pl.multiple_of(c * chunk, 8), chunk)
         return pltpu.make_async_copy(ins[j].at[at], held[j].at[at], sems.at[c, j])
 
+    gain_copy = pltpu.make_async_copy(gain_hbm, gain_ref, gain_sem)
+    gain_copy.start()
     for c in range(chunks):
         for j in range(3 * count):
             copy(c, j).start()
     acc_ref[...] = jnp.zeros_like(acc_ref)
+    gain_copy.wait()
     for start in range(0, rows, chunk):
         for i, column in enumerate(gain_columns(gain_ref, start, chunk, 8)):
             column_ref[start + 8 * i : start + 8 * i + 8, :] = jnp.broadcast_to(column, (8, LANES))
@@ -81,36 +84,42 @@
     lax.fori_loop(0, chunks, work, 0)
     for t in range(count):
         sums[t : t + 1, :] = jnp.sum(acc_ref[t], axis=0, keepdims=True)
-
-
-def update(triples, gain_row):
+    if tails:
+        tail = refs[4 * count + 1]
+        tail[...] = kept[0][rows - tail.shape[0] :, :]
+
+
+def update(triples, gain_row, tail=0):
     rows, cols = triples[0][0].shape
     chunk = step_rows(rows)
     count = len(triples)
     size = rows * cols * count
-    *gained, sums = pl.pallas_call(
-        functools.partial(update_kernel, count, chunk),
-        in_specs=[pl.BlockSpec(memory_space=pltpu.VMEM)]
-        + [pl.BlockSpec(memory_space=pltpu.HBM)] * (3 * count),
-        out_specs=[pl.BlockSpec(memory_space=pltpu.VMEM)] * (count + 1),
+    tails = 1 if tail else 0
+    outs = pl.pallas_call(
+        functools.partial(update_kernel, count, chunk, tails),
+        in_specs=[pl.BlockSpec(memory_space=pltpu.HBM)] * (3 * count + 1),
+        out_specs=[pl.BlockSpec(memory_space=pltpu.VMEM)] * (count + 1 + tails),
         out_shape=[jax.ShapeDtypeStruct((rows, cols), jnp.float32)] * count
-        + [jax.ShapeDtypeStruct((count, cols), jnp.float32)],
+        + [jax.ShapeDtypeStruct((count, cols), jnp.float32)]
+        + [jax.ShapeDtypeStruct((tail, cols), jnp.float32)] * tails,
         scratch_shapes=[pltpu.VMEM((rows, cols), jnp.float32)] * (3 * count)
         + [
             pltpu.VMEM((count, 8, cols), jnp.float32),
             pltpu.VMEM((rows, LANES), jnp.float32),
+            pltpu.VMEM((1, rows), jnp.float32),
             pltpu.SemaphoreType.DMA((rows // chunk, 3 * count)),
+            pltpu.SemaphoreType.DMA,
         ],
         compiler_params=pltpu.CompilerParams(vmem_limit_bytes=VMEM_LIMIT),
         cost_estimate=pl.CostEstimate(flops=8 * size, bytes_accessed=12 * size, transcendentals=0),
         name="update",
     )(gain_row, *[hbm(a) for triple in triples for a in triple])
-    return gained, sums
-
-
-def mean_of(index, rows_all, me_ref, totals, roles):
+    return outs[:count], outs[count], *outs[count + 1 :]
+
+
+def mean_of(index, rows_all, totals, roles):
     values = [r[index : index + 1, :] for r in totals]
-    even = (me_ref[0] & 1) == 0
+    even = (lax.axis_index("fsdp") & 1) == 0
     if roles == "fast":
         own, got, other, across = values
         values = [own, jnp.where(even, got, other), across, jnp.where(even, other, got)]
@@ -127,48 +136,68 @@
     return values[0] / rows_all
 
 
-def narrow_kernel(index, count, rows_all, start, roles, me_ref, *refs):
-    totals, block, pieces, factor = refs[:count], refs[count], refs[count + 1 : -1], refs[-1]
-    mean = mean_of(index, rows_all, me_ref, totals, roles)
-    factor[...] = mean
-    scale = 1.0 / mean
+def narrow_kernel(index, count, rows_all, start, roles, *refs):
+    totals, block, pieces = refs[:count], refs[count], refs[count + 1 :]
+    scale = 1.0 / mean_of(index, rows_all, totals, roles)
     for piece in pieces:
         rows, cols = piece.shape
 
-        def work(i, _, piece=piece, start=start, cols=cols):
+        slab = math.gcd(rows, 64)
+
+        def work(i, _, piece=piece, start=start, cols=cols, slab=slab):
             for lanes in lane_groups(cols):
-                x = block[pl.ds(pl.multiple_of(start + i * 16, 16), 16), lanes]
-                piece[pl.ds(pl.multiple_of(i * 16, 16), 16), lanes] = (x * scale[:, lanes]).astype(jnp.bfloat16)
+                by = jnp.broadcast_to(scale[:, lanes], (16, LANES))
+                for r in range(0, slab, 16):
+                    x = block[pl.ds(pl.multiple_of(start + i * slab + r, 16), 16), lanes]
+                    at = pl.ds(pl.multiple_of(i * slab + r, 16), 16)
+                    piece[at, lanes] = (x * by).astype(jnp.bfloat16)
             return _
 
-        lax.fori_loop(0, rows // 16, work, 0, unroll=2 if rows % 32 == 0 else 1)
+        lax.fori_loop(0, rows // slab, work, 0)
         start += rows
 
 
-def narrow(gained, totals, roles, index, me, n, start, sizes):
-    rows, cols = gained.shape
+def narrow(gained, totals, roles, index, rows_all, start, sizes):
+    cols = gained.shape[1]
     size = sum(sizes) * cols
-    *pieces, factor = pl.pallas_call(
-        functools.partial(narrow_kernel, index, len(totals), float(n * rows), start, roles),
-        in_specs=[pl.BlockSpec(memory_space=pltpu.SMEM)]
-        + [pl.BlockSpec(memory_space=pltpu.VMEM)] * (len(totals) + 1),
-        out_specs=[pl.BlockSpec(memory_space=pltpu.VMEM)] * (len(sizes) + 1),
-        out_shape=[jax.ShapeDtypeStruct((s, cols), jnp.bfloat16) for s in sizes]
-        + [jax.ShapeDtypeStruct((1, cols), jnp.float32)],
+    return list(pl.pallas_call(
+        functools.partial(narrow_kernel, index, len(totals), float(rows_all), start, roles),
+        in_specs=[pl.BlockSpec(memory_space=pltpu.VMEM)] * (len(totals) + 1),
+        out_specs=[pl.BlockSpec(memory_space=pltpu.VMEM)] * len(sizes),
+        out_shape=[jax.ShapeDtypeStruct((s, cols), jnp.bfloat16) for s in sizes],
         compiler_params=pltpu.CompilerParams(vmem_limit_bytes=VMEM_LIMIT),
         cost_estimate=pl.CostEstimate(flops=8 * size, bytes_accessed=6 * size, transcendentals=0),
         name="narrow",
-    )(me, *totals, gained)
-    return pieces, factor.reshape(cols)
+    )(*totals, gained))
+
+
+def factors_kernel(rows_all, roles, *refs):
+    totals, outs = refs[: -refs[0].shape[0]], refs[-refs[0].shape[0] :]
+    for index, out in enumerate(outs):
+        out[...] = mean_of(index, rows_all, totals, roles)
+
+
+def factors(totals, roles, rows_all):
+    count, cols = totals[0].shape
+    outs = pl.pallas_call(
+        functools.partial(factors_kernel, float(rows_all), roles),
+        in_specs=[pl.BlockSpec(memory_space=pltpu.VMEM)] * len(totals),
+        out_specs=[pl.BlockSpec(memory_space=pltpu.VMEM)] * count,
+        out_shape=[jax.ShapeDtypeStruct((1, cols), jnp.float32)] * count,
+        compiler_params=pltpu.CompilerParams(vmem_limit_bytes=VMEM_LIMIT),
+        cost_estimate=pl.CostEstimate(flops=cols, bytes_accessed=4 * cols, transcendentals=0),
+        name="factors",
+    )(*totals)
+    return [out.reshape(cols) for out in outs]
 
 
 def mask_of(link, core, links):
     return 2 << ((link + core) % links)
 
 
-def place_kernel(spots, rows, held, me_ref, *refs):
+def place_kernel(spots, rows, held, *refs):
     pieces, out, sems = refs[held : held + len(spots)], refs[-2], refs[-1]
-    me = me_ref[0]
+    me = lax.axis_index("fsdp")
     copies = []
     for i, (even, odd, start) in enumerate(spots):
         device = me ^ jnp.where((me & 1) == 0, even, odd)
@@ -181,24 +210,23 @@
         copy.wait()
 
 
-def place(out, me, n, rows, items):
+def place(out, n, rows, items):
     spots = tuple(item[:3] for item in items)
     pieces = [item[3] for item in items]
     size = sum(piece.size for piece in pieces)
     held = [] if out is None else [out]
     return pl.pallas_call(
         functools.partial(place_kernel, spots, rows, len(held)),
-        in_specs=[pl.BlockSpec(memory_space=pltpu.SMEM)]
-        + [pl.BlockSpec(memory_space=pltpu.HBM)] * len(held)
+        in_specs=[pl.BlockSpec(memory_space=pltpu.HBM)] * len(held)
         + [pl.BlockSpec(memory_space=pltpu.VMEM)] * len(pieces),
         out_specs=pl.BlockSpec(memory_space=pltpu.HBM),
         out_shape=jax.ShapeDtypeStruct((n * rows, pieces[0].shape[1]), pieces[0].dtype),
-        input_output_aliases={1: 0} if held else {},
+        input_output_aliases={0: 0} if held else {},
         scratch_shapes=[pltpu.SemaphoreType.DMA((len(pieces),))],
         compiler_params=pltpu.CompilerParams(vmem_limit_bytes=VMEM_LIMIT),
         cost_estimate=pl.CostEstimate(flops=size, bytes_accessed=4 * size, transcendentals=0),
         name="place",
-    )(me, *held, *pieces)
+    )(*held, *pieces)
 
 
 def over_link(link, piece, n, links):
@@ -210,12 +238,13 @@
     return swap(piece, 1, n)
 
 
-def send_first(pieces, plan, n, links):
+def send_first(pieces, plan, n, links, arrived):
     sent = []
     for p, (_, turn) in enumerate(plan):
         for s in range(links):
             link = (turn + s) % links
-            sent.append(((link,), p, s, over_link(link, pieces[p], n, links)))
+            got = arrived[p][link] if p in arrived else over_link(link, pieces[p], n, links)
+            sent.append(((link,), p, s, got))
     return sent
 
 
@@ -233,7 +262,7 @@
     return later
 
 
-def assemble(pieces, first, later, plan, me, n, links, last):
+def assemble(pieces, first, later, plan, n, links, last):
     starts = [sum(size for size, _ in plan[:p]) for p in range(len(plan) + 1)]
 
     def own(crossed, p, piece):
@@ -250,7 +279,7 @@
         + [near(c, p, x) for c, p, _, x in first],
     ]
     batches = [later]
-    if len(plan) > links:
+    if last and len(plan) > links:
         split = len(plan) - links
         batches = [[x for x in later if x[1] < split], [x for x in later if x[1] >= split]]
     for b, batch in enumerate(batches):
@@ -260,7 +289,7 @@
     out = None
     for items in stages:
         if items:
-            out = place(out, me, n, starts[-1], items)
+            out = place(out, n, starts[-1], items)
     return out
 
 
@@ -284,11 +313,11 @@
     if links == 2 and count == 3 and rows % 256 == 0:
         unit = rows // 16
         return [
-            [(10 * unit, 0), (6 * unit, 1)],
+            [(10 * unit, 0), (5 * unit, 1), (unit, 1)],
             [(10 * unit, 1), (6 * unit, 0)],
             [(5 * unit, 0), (5 * unit, 1), (3 * unit, 0), (3 * unit, 1)],
-        ]
-    return [[(rows // links, p) for p in range(links)]] * count
+        ], True
+    return [[(rows // links, p) for p in range(links)]] * count, False
 
 
 def solution(mesh):
@@ -296,26 +325,33 @@
     links = n.bit_length() - 2
 
     def on_device(wq, fq, sq, wk, fk, sk, wv, fv, sv, norm_gain):
-        me = lax.axis_index("fsdp").astype(jnp.int32).reshape(1)
+        rows = wq.shape[0]
         gain_row = hbm(norm_gain[None, :])
-        plans = plans_for(wq.shape[0], links, 3)
+        plans, early = plans_for(rows, links, 3)
         sizes = [[size for size, _ in plan] for plan in plans]
-        gained, sums = update([(wq, fq, sq)], gain_row)
+        arrived = {}
+        gained, sums, *tail = update([(wq, fq, sq)], gain_row, sizes[0][-1] if early else 0)
         totals, roles = chip_totals(sums, n, False)
-        head, factor = narrow(gained[0], totals, roles, 0, me, n, 0, sizes[0][:1])
-        rest, _ = narrow(gained[0], totals, roles, 0, me, n, sizes[0][0], sizes[0][1:])
+        if early:
+            raw = [over_link(link, tail[0], n, links) for link in range(links)]
+        head = narrow(gained[0], totals, roles, 0, n * rows, 0, sizes[0][:1])
+        rest = narrow(gained[0], totals, roles, 0, n * rows, sizes[0][0], sizes[0][1:])
+        if early:
+            arrived[len(plans[0]) - 1] = [narrow(x, totals, roles, 0, n * rows, 0, sizes[0][-1:])[0] for x in raw]
+        mean = factors(totals, roles, n * rows)
         gained, sums = update([(wk, fk, sk), (wv, fv, sv)], gain_row)
         totals, roles = chip_totals(sums, n, True)
         narrowed = [
-            narrow(g, totals, roles, t, me, n, 0, sizes[t + 1]) for t, g in enumerate(gained)
+            narrow(g, totals, roles, t, n * rows, 0, sizes[t + 1]) for t, g in enumerate(gained)
         ]
-        pieces = [head + rest, narrowed[0][0], narrowed[1][0]]
+        mean += factors(totals, roles, n * rows)
+        pieces = [head + rest, *narrowed]
         outs = []
         for t, plan in enumerate(plans):
-            first = send_first(pieces[t], plan, n, links)
+            first = send_first(pieces[t], plan, n, links, arrived if t == 0 else {})
             later = send_onward(first, plan, n, links)
-            outs.append(assemble(pieces[t], first, later, plan, me, n, links, t == 2))
-        return (*outs, factor, narrowed[0][1], narrowed[1][1])
+            outs.append(assemble(pieces[t], first, later, plan, n, links, t == 2))
+        return (*outs, *mean)
 
     return jax.shard_map(
         on_device,

time: 166 us -> 164 us (0.988)
  starting transfers between devices: 37.2 us -> 47.8 us
  waiting for transfers between devices: 96.5 us -> 87.7 us
  local copies, waits for them, and re-layouts: 2.9 us -> 0 us
    ppermute x24 -> x27, starting transfers between devices: 23 us -> 31.8 us  [over_link(): return lax.ppermute(piece, 'fsdp', pairs)]
    ppermute x24 -> x27, waiting for transfers between devices: 85.8 us -> 81.1 us  [over_link(): return lax.ppermute(piece, 'fsdp', pairs)]
    ppermute x38 -> x42, waiting for transfers between devices: 7.87 us -> 4.5 us  [swap(): return lax.ppermute(value, 'fsdp', [(i, i ^ mask) for i in range(n)])]
    ppermute x38 -> x42, starting transfers between devices: 10.3 us -> 13.2 us  [swap(): return lax.ppermute(value, 'fsdp', [(i, i ^ mask) for i in range(n)])]
    unnamed x4 -> x0, local copies, waits for them, and re-layouts: 2.9 us -> none
    pallas_call x4 -> x6, Pallas kernels: 3.22 us -> 0.77 us  [narrow(): pl.pallas_call(functools.partial(narrow_kernel, index, len(totals), float...]
    ppermute x1, starting transfers between devices: 2.82 us -> 0.53 us  [chip_totals(): lax.ppermute(chip, 'fsdp', [(i, i ^ (4 if i & 1 else 2)) for i in range(n)])]
    pallas_call x2 -> x4, Pallas kernels: 9.49 us -> 10.9 us  [the longest x2 9.68 us: update(): pl.pallas_call(functools.partial(update_kernel, count, chunk, tails), in_...]
  transfers between devices with their start and end apart: 65 -> 72, of which waited for: 23 -> 20; matrix products, arithmetic and copies ran while one was open for 0% -> 0% of each run, Pallas kernels for 12% -> 14%
where the time goes in v2:
time: 164 us
  waiting for transfers between devices  87.7 us (53%)
  starting transfers between devices  47.8 us (29%)
  Pallas kernels  27.4 us (17%)
    ppermute x27, waiting for transfers between devices, over_link(): return lax.ppermute(piece, 'fsdp', pairs)  81.1 us
    ppermute x27, starting transfers between devices, over_link(): return lax.ppermute(piece, 'fsdp', pairs)  31.8 us
    pallas_call x11, Pallas kernels, place(): pl.pallas_call(functools.partial(place_kernel, spots, rows, len(held)), i...  15.8 us
    ppermute x42, starting transfers between devices, swap(): return lax.ppermute(value, 'fsdp', [(i, i ^ mask) for i in range(n)])  13.2 us
    pallas_call x2, Pallas kernels, update(): pl.pallas_call(functools.partial(update_kernel, count, chunk, tails), in_...  9.68 us
    ppermute x42, waiting for transfers between devices, swap(): return lax.ppermute(value, 'fsdp', [(i, i ^ mask) for i in range(n)])  4.5 us
  transfers between devices with their start and end apart: 72, of which 20 were waited for; matrix products, arithmetic and copies ran while one was open for 0% of the time, Pallas kernels for 14%

profile of v2, /device:TPU:0, one launch (start us, length us, event | category | flops | bytes accessed | tf_op | source)
XLA Modules:
  0.0 163.8 jit_solution(7886812283499007168)
XLA Ops:
  0.6 3.5 %update.2 = (f32[512,1024]{1,0:T(8,128)S(1)}, f32[1,1024]{1,0:T(1,128)S(1)}, f32[32,1024]{1,0:T(8,128)S(1)}) custom-call(f32[1,512]{1,0:T(1,128)} %bitcast.4, f32[512,1024]{1,0:T(8,128)} %refs_0_.2, f32[512,1024]{1,0:T(8,128)} %refs_1_.2, f32[512,1024]{1,0:T(8,128)} %refs_2_.2), custom_call_target="tpu_custom_call" | custom-call | flops 4194304 | bytes 6291456 | tf_op jit(solution)/shard_map/update/pallas_call | solution.py:98
  4.2 3.1 %collective-permute-start.8 = (f32[32,1024]{1,0:T(8,128)S(1)}, f32[32,1024]{1,0:T(8,128)S(1)}, u32[]{:S(2)}, u32[]{:S(2)}) collective-permute-start(f32[32,1024]{1,0:T(8,128)S(1)} %get-tuple-element.26), channel_id=1, source_target_pairs={{0,16},{4,12},{8,24},{12,4},{16,0},{20,28},{24,8},{28,20},{1,17},{... | collective-permute-start | bytes 393224 | tf_op jit(solution)/shard_map/ppermute | solution.py:234
  7.2 1.5 collective-permute-start.9
  8.7 6.2 %update.3 = (f32[512,1024]{1,0:T(8,128)S(1)}, f32[512,1024]{1,0:T(8,128)S(1)}, f32[2,1024]{1,0:T(2,128)S(1)}) custom-call(f32[1,512]{1,0:T(1,128)} %bitcast.5, f32[512,1024]{1,0:T(8,128)} %refs_0_.3, f32[512,1024]{1,0:T(8,128)} %refs_1_.3, f32[512,1024]{1,0:T(8,128)} %refs_2_.3, f32[512,1024]{1,0:T(8,128)} %refs_3_.1, f32[512,1024]{1,0:T(8,128)} %refs_4_.1, ...), custom_call_target="tpu_custom_call" | custom-call | flops 8388608 | bytes 12582912 | tf_op jit(solution)/shard_map/update/pallas_call | solution.py:98
  15.5 0.7 collective-permute-done.25
  16.1 0.5 collective-permute-start.26
  16.7 0.6 collective-permute-start.28
  17.3 1.6 collective-permute-start.1
  18.9 2.1 %collective-permute-done.1.refs_1_ = f32[1,1024]{1,0:T(1,128)S(1)} collective-permute-done((f32[1,1024]{1,0:T(1,128)S(1)}, f32[1,1024]{1,0:T(1,128)S(1)}, u32[]{:S(2)}, u32[]{:S(2)}) %collective-permute-start.1) | collective-permute-done | bytes 4128 | tf_op jit(solution)/shard_map/ppermute | solution.py:304
  21.1 2.0 %collective-permute-start.27 = (f32[2,1024]{1,0:T(2,128)S(1)}, f32[2,1024]{1,0:T(2,128)S(1)}, u32[]{:S(2)}, u32[]{:S(2)}) collective-permute-start(f32[2,1024]{1,0:T(2,128)S(1)} %collective-permute-done.26.refs_1_), channel_id=1, source_target_pairs={{0,4},{4,0},{8,12},{12,8},{16,20},{20,16},{24,28},{28,24},{1,5},{5... | collective-permute-start | bytes 24584 | tf_op jit(solution)/shard_map/ppermute | solution.py:20
  23.2 1.4 collective-permute-done.3.refs_3_
  24.6 0.9 collective-permute-start.2
  25.5 0.8 collective-permute-done.2.refs_2_
  27.9 1.6 collective-permute-start.48
  29.4 0.5 collective-permute-start.21
  30.3 1.7 %collective-permute-start.49 = (bf16[96,1024]{1,0:T(8,128)(2,1)S(1)}, bf16[96,1024]{1,0:T(8,128)(2,1)S(1)}, u32[]{:S(2)}, u32[]{:S(2)}) collective-permute-start(bf16[96,1024]{1,0:T(8,128)(2,1)S(1)} %get-tuple-element.34.refs_2_), channel_id=1, source_target_pairs={{0,16},{4,12},{8,24},{12,4},{16,0},{20,28},{24,8},{28,20},{1,17},{... | collective-permute-start | bytes 589832 | tf_op jit(solution)/shard_map/ppermute | solution.py:234
  32.0 1.5 collective-permute-start.51
  33.5 3.0 %collective-permute-done.21.refs_3_ = bf16[32,1024]{1,0:T(8,128)(2,1)S(1)} collective-permute-done((bf16[32,1024]{1,0:T(8,128)(2,1)S(1)}, bf16[32,1024]{1,0:T(8,128)(2,1)S(1)}, u32[]{:S(2)}, u32[]{:S(2)}) %collective-permute-start.21) | collective-permute-done | bytes 65568 | tf_op jit(solution)/shard_map/ppermute | solution.py:234
  36.7 0.9 collective-permute-done.50.refs_10_
  37.6 1.5 collective-permute-start.7
  39.1 0.7 collective-permute-done.49.refs_9_
  39.8 0.9 collective-permute-start.11
  40.7 1.6 collective-permute-start.44
  42.8 3.5 %collective-permute-done.6.refs_5_ = bf16[160,1024]{1,0:T(8,128)(2,1)S(1)} collective-permute-done((bf16[160,1024]{1,0:T(8,128)(2,1)S(1)}, bf16[160,1024]{1,0:T(8,128)(2,1)S(1)}, u32[]{:S(2)}, u32[]{:S(2)}) %collective-permute-start.6) | collective-permute-done | bytes 327712 | tf_op jit(solution)/shard_map/ppermute | solution.py:234
  46.3 1.9 %collective-permute-done.7.refs_6_ = bf16[160,1024]{1,0:T(8,128)(2,1)S(1)} collective-permute-done((bf16[160,1024]{1,0:T(8,128)(2,1)S(1)}, bf16[160,1024]{1,0:T(8,128)(2,1)S(1)}, u32[]{:S(2)}, u32[]{:S(2)}) %collective-permute-start.7) | collective-permute-done | bytes 327712 | tf_op jit(solution)/shard_map/ppermute | solution.py:234
  48.2 1.5 collective-permute-start.47
  49.7 5.5 %collective-permute-done.44.refs_4_ = bf16[160,1024]{1,0:T(8,128)(2,1)S(1)} collective-permute-done((bf16[160,1024]{1,0:T(8,128)(2,1)S(1)}, bf16[160,1024]{1,0:T(8,128)(2,1)S(1)}, u32[]{:S(2)}, u32[]{:S(2)}) %collective-permute-start.44) | collective-permute-done | bytes 327712 | tf_op jit(solution)/shard_map/ppermute | solution.py:234
  55.2 0.5 collective-permute-start.60
  55.7 4.6 %collective-permute-done.45.refs_5_ = bf16[160,1024]{1,0:T(8,128)(2,1)S(1)} collective-permute-done((bf16[160,1024]{1,0:T(8,128)(2,1)S(1)}, bf16[160,1024]{1,0:T(8,128)(2,1)S(1)}, u32[]{:S(2)}, u32[]{:S(2)}) %collective-permute-start.45) | collective-permute-done | bytes 327712 | tf_op jit(solution)/shard_map/ppermute | solution.py:234
  60.3 0.9 collective-permute-start.62
  62.8 1.7 %collective-permute-start.32 = (bf16[192,1024]{1,0:T(8,128)(2,1)S(1)}, bf16[192,1024]{1,0:T(8,128)(2,1)S(1)}, u32[]{:S(2)}, u32[]{:S(2)}) collective-permute-start(bf16[192,1024]{1,0:T(8,128)(2,1)S(1)} %get-tuple-element.30.refs_1_), channel_id=1, source_target_pairs={{0,8},{4,20},{8,0},{12,28},{16,24},{20,4},{24,16},{28,12},{1,9},{5... | collective-permute-start | bytes 1179656 | tf_op jit(solution)/shard_map/ppermute | solution.py:234
  65.1 1.7 %collective-permute-start.33 = (bf16[192,1024]{1,0:T(8,128)(2,1)S(1)}, bf16[192,1024]{1,0:T(8,128)(2,1)S(1)}, u32[]{:S(2)}, u32[]{:S(2)}) collective-permute-start(bf16[192,1024]{1,0:T(8,128)(2,1)S(1)} %get-tuple-element.30.refs_1_), channel_id=1, source_target_pairs={{0,16},{4,12},{8,24},{12,4},{16,0},{20,28},{24,8},{28,20},{1,17},{... | collective-permute-start | bytes 1179656 | tf_op jit(solution)/shard_map/ppermute | solution.py:234
  66.8 2.6 %collective-permute-done.68.refs_1_ = bf16[96,1024]{1,0:T(8,128)(2,1)S(1)} collective-permute-done((bf16[96,1024]{1,0:T(8,128)(2,1)S(1)}, bf16[96,1024]{1,0:T(8,128)(2,1)S(1)}, u32[]{:S(2)}, u32[]{:S(2)}) %collective-permute-start.68) | collective-permute-done | bytes 196640 | tf_op jit(solution)/shard_map/ppermute | solution.py:234
  69.4 2.1 %collective-permute-start.69 = (bf16[96,1024]{1,0:T(8,128)(2,1)S(1)}, bf16[96,1024]{1,0:T(8,128)(2,1)S(1)}, u32[]{:S(2)}, u32[]{:S(2)}) collective-permute-start(bf16[96,1024]{1,0:T(8,128)(2,1)S(1)} %collective-permute-done.50.refs_10_), channel_id=1, source_target_pairs={{0,8},{4,20},{8,0},{12,28},{16,24},{20,4},{24,16},{28,12},{1,9},{5... | collective-permute-start | bytes 589832 | tf_op jit(solution)/shard_map/ppermute | solution.py:234
  71.5 13.1 %collective-permute-done.69.refs_2_ = bf16[96,1024]{1,0:T(8,128)(2,1)S(1)} collective-permute-done((bf16[96,1024]{1,0:T(8,128)(2,1)S(1)}, bf16[96,1024]{1,0:T(8,128)(2,1)S(1)}, u32[]{:S(2)}, u32[]{:S(2)}) %collective-permute-start.69) | collective-permute-done | bytes 196640 | tf_op jit(solution)/shard_map/ppermute | solution.py:234
  84.5 1.1 collective-permute-start.5
  86.6 1.5 collective-permute-done.70.refs_1_
  88.8 0.9 collective-permute-start.20
  89.7 8.9 %collective-permute-done.5.refs_4_ = bf16[320,1024]{1,0:T(8,128)(2,1)S(1)} collective-permute-done((bf16[320,1024]{1,0:T(8,128)(2,1)S(1)}, bf16[320,1024]{1,0:T(8,128)(2,1)S(1)}, u32[]{:S(2)}, u32[]{:S(2)}) %collective-permute-start.5) | collective-permute-done | bytes 655392 | tf_op jit(solution)/shard_map/ppermute | solution.py:234
  99.7 1.1 collective-permute-start.30
  100.8 1.0 collective-permute-start.31
  101.8 1.4 collective-permute-start.64
  103.2 0.5 collective-permute-start.65
  103.7 20.2 %collective-permute-done.64.refs_1_ = bf16[160,1024]{1,0:T(8,128)(2,1)S(1)} collective-permute-done((bf16[160,1024]{1,0:T(8,128)(2,1)S(1)}, bf16[160,1024]{1,0:T(8,128)(2,1)S(1)}, u32[]{:S(2)}, u32[]{:S(2)}) %collective-permute-start.64) | collective-permute-done | bytes 327712 | tf_op jit(solution)/shard_map/ppermute | solution.py:234
  124.5 1.2 collective-permute-start.41
  126.4 1.1 collective-permute-start.19
  127.5 4.8 %collective-permute-done.41.refs_2_ = bf16[192,1024]{1,0:T(8,128)(2,1)S(1)} collective-permute-done((bf16[192,1024]{1,0:T(8,128)(2,1)S(1)}, bf16[192,1024]{1,0:T(8,128)(2,1)S(1)}, u32[]{:S(2)}, u32[]{:S(2)}) %collective-permute-start.41) | collective-permute-done | bytes 393248 | tf_op jit(solution)/shard_map/ppermute | solution.py:234
  132.3 1.6 collective-permute-start.40
  134.4 10.0 %collective-permute-done.19.refs_1_ = bf16[320,1024]{1,0:T(8,128)(2,1)S(1)} collective-permute-done((bf16[320,1024]{1,0:T(8,128)(2,1)S(1)}, bf16[320,1024]{1,0:T(8,128)(2,1)S(1)}, u32[]{:S(2)}, u32[]{:S(2)}) %collective-permute-start.19) | collective-permute-done | bytes 655392 | tf_op jit(solution)/shard_map/ppermute | solution.py:234
  144.5 0.9 collective-permute-done.40.refs_1_
  145.4 0.7 collective-permute-start.42
  146.7 0.6 factors.2
  147.3 0.6 factors.3
  147.9 1.7 %place.17.refs_0_ = bf16[4096,1024]{1,0:T(8,128)(2,1)} custom-call(bf16[160,1024]{1,0:T(8,128)(2,1)S(1)} %get-tuple-element.32.refs_0_, bf16[160,1024]{1,0:T(8,128)(2,1)S(1)} %get-tuple-element.33.refs_1_, bf16[96,1024]{1,0:T(8,128)(2,1)S(1)} %get-tuple-element.34.refs_2_, bf16[96,1024]{1,0:T(8,128)(2,1)S(1)} %get-tuple-element.35.refs_3_, ...), custom_call_target="tpu_custom_call" | custom-call | flops 1572864 | bytes 6291456 | tf_op jit(solution)/shard_map/place/pallas_call | solution.py:218
  149.7 1.8 %place.18.refs_0_ = bf16[4096,1024]{1,0:T(8,128)(2,1)} custom-call(bf16[4096,1024]{1,0:T(8,128)(2,1)} %place.17.refs_0_, bf16[160,1024]{1,0:T(8,128)(2,1)S(1)} %collective-permute-done.52.refs_1_, bf16[160,1024]{1,0:T(8,128)(2,1)S(1)} %collective-permute-done.53.refs_2_, ...), custom_call_target="tpu_custom_call", output_to_operand_aliasing={{}: (0, {})} | custom-call | flops 1572864 | bytes 6291456 | tf_op jit(solution)/shard_map/place/pallas_call | solution.py:218
  151.4 1.1 place.19.refs_0_
  152.6 1.7 %place.11.refs_0_ = bf16[4096,1024]{1,0:T(8,128)(2,1)} custom-call(bf16[320,1024]{1,0:T(8,128)(2,1)S(1)} %narrow.6.refs_0_, bf16[160,1024]{1,0:T(8,128)(2,1)S(1)} %get-tuple-element.24.refs_1_, bf16[32,1024]{1,0:T(8,128)(2,1)S(1)} %get-tuple-element.25.refs_2_, bf16[320,1024]{1,0:T(8,128)(2,1)S(1)} %collective-permute-done.4.refs_3_, ...), custom_call_target="tpu_custom_call" | custom-call | flops 1572864 | bytes 6291456 | tf_op jit(solution)/shard_map/place/pallas_call | solution.py:218
  154.3 0.8 place.20.refs_0_
  155.1 1.7 %place.14.refs_0_ = bf16[4096,1024]{1,0:T(8,128)(2,1)} custom-call(bf16[320,1024]{1,0:T(8,128)(2,1)S(1)} %get-tuple-element.29.refs_0_, bf16[192,1024]{1,0:T(8,128)(2,1)S(1)} %get-tuple-element.30.refs_1_, bf16[320,1024]{1,0:T(8,128)(2,1)S(1)} %collective-permute-done.30.refs_2_, bf16[320,1024]{1,0:T(8,128)(2,1)S(1)} %collective-permute-done.31.refs_3_, ...), custom_call_target="tpu_custom_call" | custom-call | flops 1572864 | bytes 6291456 | tf_op jit(solution)/shard_map/place/pallas_call | solution.py:218
  156.8 0.8 place.21
  157.6 1.7 %place.12.refs_0_ = bf16[4096,1024]{1,0:T(8,128)(2,1)} custom-call(bf16[4096,1024]{1,0:T(8,128)(2,1)} %place.11.refs_0_, bf16[320,1024]{1,0:T(8,128)(2,1)S(1)} %collective-permute-done.10.refs_1_, bf16[160,1024]{1,0:T(8,128)(2,1)S(1)} %collective-permute-done.11.refs_2_, ...), custom_call_target="tpu_custom_call", output_to_operand_aliasing={{}: (0, {})} | custom-call | flops 1572864 | bytes 6291456 | tf_op jit(solution)/shard_map/place/pallas_call | solution.py:218
  159.3 1.7 %place.15.refs_0_ = bf16[4096,1024]{1,0:T(8,128)(2,1)} custom-call(bf16[4096,1024]{1,0:T(8,128)(2,1)} %place.14.refs_0_, bf16[320,1024]{1,0:T(8,128)(2,1)S(1)} %collective-permute-done.34.refs_1_, bf16[192,1024]{1,0:T(8,128)(2,1)S(1)} %collective-permute-done.35.refs_2_, ...), custom_call_target="tpu_custom_call", output_to_operand_aliasing={{}: (0, {})} | custom-call | flops 1572864 | bytes 6291456 | tf_op jit(solution)/shard_map/place/pallas_call | solution.py:218
  161.1 1.4 place.13
  162.5 1.4 place.16
  (103 shorter events, 10.6 us)
Async XLA Ops:
  4.2 22.7 %collective-permute-start.8 = (f32[32,1024]{1,0:T(8,128)S(1)}, f32[32,1024]{1,0:T(8,128)S(1)}, u32[]{:S(2)}, u32[]{:S(2)}) collective-permute-start(f32[32,1024]{1,0:T(8,128)S(1)} %get-tuple-element.26), channel_id=1, source_target_pairs={{0,16},{4,12},{8,24},{12,4},{16,0},{20,28},{24,8},{28,20},{1,17},{... | collective-permute-start | bytes 393224 | tf_op jit(solution)/shard_map/ppermute | solution.py:234
  7.2 19.9 %collective-permute-start.9 = (f32[32,1024]{1,0:T(8,128)S(1)}, f32[32,1024]{1,0:T(8,128)S(1)}, u32[]{:S(2)}, u32[]{:S(2)}) collective-permute-start(f32[32,1024]{1,0:T(8,128)S(1)} %get-tuple-element.26), channel_id=1, source_target_pairs={{0,8},{4,20},{8,0},{12,28},{16,24},{20,4},{24,16},{28,12},{1,9},{5... | collective-permute-start | bytes 393224 | tf_op jit(solution)/shard_map/ppermute | solution.py:234
  16.1 5.0 %collective-permute-start.26 = (f32[2,1024]{1,0:T(2,128)S(1)}, f32[2,1024]{1,0:T(2,128)S(1)}, u32[]{:S(2)}, u32[]{:S(2)}) collective-permute-start(f32[2,1024]{1,0:T(2,128)S(1)} %add.7.refs_0_), channel_id=1, source_target_pairs={{0,8},{4,20},{8,0},{12,28},{16,24},{20,4},{24,16},{28,12},{1,9},{5... | collective-permute-start | bytes 24584 | tf_op jit(solution)/shard_map/ppermute | solution.py:301
  16.7 6.5 %collective-permute-start.28 = (f32[2,1024]{1,0:T(2,128)S(1)}, f32[2,1024]{1,0:T(2,128)S(1)}, u32[]{:S(2)}, u32[]{:S(2)}) collective-permute-start(f32[2,1024]{1,0:T(2,128)S(1)} %add.7.refs_0_), channel_id=1, source_target_pairs={{4,28},{12,20},{20,12},{28,4},{5,29},{13,21},{21,13},{29,5},{6,30}... | collective-permute-start | bytes 24584 | tf_op jit(solution)/shard_map/ppermute | solution.py:302
  17.3 3.7 %collective-permute-start.1 = (f32[1,1024]{1,0:T(1,128)S(1)}, f32[1,1024]{1,0:T(1,128)S(1)}, u32[]{:S(2)}, u32[]{:S(2)}) collective-permute-start(f32[1,1024]{1,0:T(1,128)S(1)} %add.6.refs_0_), channel_id=1, source_target_pairs={{0,8},{4,28},{8,0},{12,20},{16,24},{20,12},{24,16},{28,4},{1,9},{5... | collective-permute-start | bytes 12296 | tf_op jit(solution)/shard_map/ppermute | solution.py:304
  21.0 3.6 %collective-permute-start.3 = (f32[1,1024]{1,0:T(1,128)S(1)}, f32[1,1024]{1,0:T(1,128)S(1)}, u32[]{:S(2)}, u32[]{:S(2)}) collective-permute-start(f32[1,1024]{1,0:T(1,128)S(1)} %add.6.refs_0_), channel_id=1, source_target_pairs={{0,16},{4,20},{8,24},{12,28},{16,0},{20,4},{24,8},{28,12},{1,17},{... | collective-permute-start | bytes 12296 | tf_op jit(solution)/shard_map/ppermute | solution.py:20
  21.1 6.5 %collective-permute-start.27 = (f32[2,1024]{1,0:T(2,128)S(1)}, f32[2,1024]{1,0:T(2,128)S(1)}, u32[]{:S(2)}, u32[]{:S(2)}) collective-permute-start(f32[2,1024]{1,0:T(2,128)S(1)} %collective-permute-done.26.refs_1_), channel_id=1, source_target_pairs={{0,4},{4,0},{8,12},{12,8},{16,20},{20,16},{24,28},{28,24},{1,5},{5... | collective-permute-start | bytes 24584 | tf_op jit(solution)/shard_map/ppermute | solution.py:20
  23.1 4.5 %collective-permute-start.29 = (f32[2,1024]{1,0:T(2,128)S(1)}, f32[2,1024]{1,0:T(2,128)S(1)}, u32[]{:S(2)}, u32[]{:S(2)}) collective-permute-start(f32[2,1024]{1,0:T(2,128)S(1)} %collective-permute-done.28.refs_3_), channel_id=1, source_target_pairs={{0,4},{4,0},{8,12},{12,8},{16,20},{20,16},{24,28},{28,24},{1,5},{5... | collective-permute-start | bytes 24584 | tf_op jit(solution)/shard_map/ppermute | solution.py:20
  26.5 3.5 %collective-permute-start.12 = (bf16[32,1024]{1,0:T(8,128)(2,1)S(1)}, bf16[32,1024]{1,0:T(8,128)(2,1)S(1)}, u32[]{:S(2)}, u32[]{:S(2)}) collective-permute-start(bf16[32,1024]{1,0:T(8,128)(2,1)S(1)} %get-tuple-element.25.refs_2_), channel_id=1, source_target_pairs={{0,4},{4,0},{8,12},{12,8},{16,20},{20,16},{24,28},{28,24},{1,5},{5... | collective-permute-start | bytes 196616 | tf_op jit(solution)/shard_map/ppermute | solution.py:20
  26.9 3.4 %collective-permute-start.17 = (bf16[32,1024]{1,0:T(8,128)(2,1)S(1)}, bf16[32,1024]{1,0:T(8,128)(2,1)S(1)}, u32[]{:S(2)}, u32[]{:S(2)}) collective-permute-start(bf16[32,1024]{1,0:T(8,128)(2,1)S(1)} %narrow.8.refs_7_), channel_id=1, source_target_pairs={{0,4},{4,0},{8,12},{12,8},{16,20},{20,16},{24,28},{28,24},{1,5},{5... | collective-permute-start | bytes 196616 | tf_op jit(solution)/shard_map/ppermute | solution.py:20
  27.2 4.8 %collective-permute-start.18 = (bf16[32,1024]{1,0:T(8,128)(2,1)S(1)}, bf16[32,1024]{1,0:T(8,128)(2,1)S(1)}, u32[]{:S(2)}, u32[]{:S(2)}) collective-permute-start(bf16[32,1024]{1,0:T(8,128)(2,1)S(1)} %narrow.9.refs_8_), channel_id=1, source_target_pairs={{0,4},{4,0},{8,12},{12,8},{16,20},{20,16},{24,28},{28,24},{1,5},{5... | collective-permute-start | bytes 196616 | tf_op jit(solution)/shard_map/ppermute | solution.py:20
  27.9 8.6 %collective-permute-start.48 = (bf16[96,1024]{1,0:T(8,128)(2,1)S(1)}, bf16[96,1024]{1,0:T(8,128)(2,1)S(1)}, u32[]{:S(2)}, u32[]{:S(2)}) collective-permute-start(bf16[96,1024]{1,0:T(8,128)(2,1)S(1)} %get-tuple-element.34.refs_2_), channel_id=1, source_target_pairs={{0,8},{4,20},{8,0},{12,28},{16,24},{20,4},{24,16},{28,12},{1,9},{5... | collective-permute-start | bytes 589832 | tf_op jit(solution)/shard_map/ppermute | solution.py:234
  29.4 7.0 %collective-permute-start.21 = (bf16[32,1024]{1,0:T(8,128)(2,1)S(1)}, bf16[32,1024]{1,0:T(8,128)(2,1)S(1)}, u32[]{:S(2)}, u32[]{:S(2)}) collective-permute-start(bf16[32,1024]{1,0:T(8,128)(2,1)S(1)} %narrow.8.refs_7_), channel_id=1, source_target_pairs={{0,8},{4,20},{8,0},{12,28},{16,24},{20,4},{24,16},{28,12},{1,9},{5... | collective-permute-start | bytes 196616 | tf_op jit(solution)/shard_map/ppermute | solution.py:234
  30.0 7.7 %collective-permute-start.50 = (bf16[96,1024]{1,0:T(8,128)(2,1)S(1)}, bf16[96,1024]{1,0:T(8,128)(2,1)S(1)}, u32[]{:S(2)}, u32[]{:S(2)}) collective-permute-start(bf16[96,1024]{1,0:T(8,128)(2,1)S(1)} %get-tuple-element.35.refs_3_), channel_id=1, source_target_pairs={{0,16},{4,12},{8,24},{12,4},{16,0},{20,28},{24,8},{28,20},{1,17},{... | collective-permute-start | bytes 589832 | tf_op jit(solution)/shard_map/ppermute | solution.py:234
  30.3 9.6 %collective-permute-start.49 = (bf16[96,1024]{1,0:T(8,128)(2,1)S(1)}, bf16[96,1024]{1,0:T(8,128)(2,1)S(1)}, u32[]{:S(2)}, u32[]{:S(2)}) collective-permute-start(bf16[96,1024]{1,0:T(8,128)(2,1)S(1)} %get-tuple-element.34.refs_2_), channel_id=1, source_target_pairs={{0,16},{4,12},{8,24},{12,4},{16,0},{20,28},{24,8},{28,20},{1,17},{... | collective-permute-start | bytes 589832 | tf_op jit(solution)/shard_map/ppermute | solution.py:234
  32.0 8.7 %collective-permute-start.51 = (bf16[96,1024]{1,0:T(8,128)(2,1)S(1)}, bf16[96,1024]{1,0:T(8,128)(2,1)S(1)}, u32[]{:S(2)}, u32[]{:S(2)}) collective-permute-start(bf16[96,1024]{1,0:T(8,128)(2,1)S(1)} %get-tuple-element.35.refs_3_), channel_id=1, source_target_pairs={{0,8},{4,20},{8,0},{12,28},{16,24},{20,4},{24,16},{28,12},{1,9},{5... | collective-permute-start | bytes 589832 | tf_op jit(solution)/shard_map/ppermute | solution.py:234
  36.4 4.3 %collective-permute-start.54 = (bf16[96,1024]{1,0:T(8,128)(2,1)S(1)}, bf16[96,1024]{1,0:T(8,128)(2,1)S(1)}, u32[]{:S(2)}, u32[]{:S(2)}) collective-permute-start(bf16[96,1024]{1,0:T(8,128)(2,1)S(1)} %get-tuple-element.34.refs_2_), channel_id=1, source_target_pairs={{0,4},{4,0},{8,12},{12,8},{16,20},{20,16},{24,28},{28,24},{1,5},{5... | collective-permute-start | bytes 589832 | tf_op jit(solution)/shard_map/ppermute | solution.py:20
  36.5 9.8 %collective-permute-start.6 = (bf16[160,1024]{1,0:T(8,128)(2,1)S(1)}, bf16[160,1024]{1,0:T(8,128)(2,1)S(1)}, u32[]{:S(2)}, u32[]{:S(2)}) collective-permute-start(bf16[160,1024]{1,0:T(8,128)(2,1)S(1)} %get-tuple-element.24.refs_1_), channel_id=1, source_target_pairs={{0,16},{4,12},{8,24},{12,4},{16,0},{20,28},{24,8},{28,20},{1,17},{... | collective-permute-start | bytes 983048 | tf_op jit(solution)/shard_map/ppermute | solution.py:234
  37.6 10.6 %collective-permute-start.7 = (bf16[160,1024]{1,0:T(8,128)(2,1)S(1)}, bf16[160,1024]{1,0:T(8,128)(2,1)S(1)}, u32[]{:S(2)}, u32[]{:S(2)}) collective-permute-start(bf16[160,1024]{1,0:T(8,128)(2,1)S(1)} %get-tuple-element.24.refs_1_), channel_id=1, source_target_pairs={{0,8},{4,20},{8,0},{12,28},{16,24},{20,4},{24,16},{28,12},{1,9},{5... | collective-permute-start | bytes 983048 | tf_op jit(solution)/shard_map/ppermute | solution.py:234
  39.8 9.9 %collective-permute-start.11 = (bf16[160,1024]{1,0:T(8,128)(2,1)S(1)}, bf16[160,1024]{1,0:T(8,128)(2,1)S(1)}, u32[]{:S(2)}, u32[]{:S(2)}) collective-permute-start(bf16[160,1024]{1,0:T(8,128)(2,1)S(1)} %get-tuple-element.24.refs_1_), channel_id=1, source_target_pairs={{0,4},{4,0},{8,12},{12,8},{16,20},{20,16},{24,28},{28,24},{1,5},{5... | collective-permute-start | bytes 983048 | tf_op jit(solution)/shard_map/ppermute | solution.py:20
  40.7 14.5 %collective-permute-start.44 = (bf16[160,1024]{1,0:T(8,128)(2,1)S(1)}, bf16[160,1024]{1,0:T(8,128)(2,1)S(1)}, u32[]{:S(2)}, u32[]{:S(2)}) collective-permute-start(bf16[160,1024]{1,0:T(8,128)(2,1)S(1)} %get-tuple-element.32.refs_0_), channel_id=1, source_target_pairs={{0,8},{4,20},{8,0},{12,28},{16,24},{20,4},{24,16},{28,12},{1,9},{5... | collective-permute-start | bytes 983048 | tf_op jit(solution)/shard_map/ppermute | solution.py:234
  42.3 13.0 %collective-permute-start.46 = (bf16[160,1024]{1,0:T(8,128)(2,1)S(1)}, bf16[160,1024]{1,0:T(8,128)(2,1)S(1)}, u32[]{:S(2)}, u32[]{:S(2)}) collective-permute-start(bf16[160,1024]{1,0:T(8,128)(2,1)S(1)} %get-tuple-element.33.refs_1_), channel_id=1, source_target_pairs={{0,16},{4,12},{8,24},{12,4},{16,0},{20,28},{24,8},{28,20},{1,17},{... | collective-permute-start | bytes 983048 | tf_op jit(solution)/shard_map/ppermute | solution.py:234
  46.3 14.0 %collective-permute-start.45 = (bf16[160,1024]{1,0:T(8,128)(2,1)S(1)}, bf16[160,1024]{1,0:T(8,128)(2,1)S(1)}, u32[]{:S(2)}, u32[]{:S(2)}) collective-permute-start(bf16[160,1024]{1,0:T(8,128)(2,1)S(1)} %get-tuple-element.32.refs_0_), channel_id=1, source_target_pairs={{0,16},{4,12},{8,24},{12,4},{16,0},{20,28},{24,8},{28,20},{1,17},{... | collective-permute-start | bytes 983048 | tf_op jit(solution)/shard_map/ppermute | solution.py:234
  48.2 13.5 %collective-permute-start.47 = (bf16[160,1024]{1,0:T(8,128)(2,1)S(1)}, bf16[160,1024]{1,0:T(8,128)(2,1)S(1)}, u32[]{:S(2)}, u32[]{:S(2)}) collective-permute-start(bf16[160,1024]{1,0:T(8,128)(2,1)S(1)} %get-tuple-element.33.refs_1_), channel_id=1, source_target_pairs={{0,8},{4,20},{8,0},{12,28},{16,24},{20,4},{24,16},{28,12},{1,9},{5... | collective-permute-start | bytes 983048 | tf_op jit(solution)/shard_map/ppermute | solution.py:234
  49.7 12.0 %collective-permute-start.52 = (bf16[160,1024]{1,0:T(8,128)(2,1)S(1)}, bf16[160,1024]{1,0:T(8,128)(2,1)S(1)}, u32[]{:S(2)}, u32[]{:S(2)}) collective-permute-start(bf16[160,1024]{1,0:T(8,128)(2,1)S(1)} %get-tuple-element.32.refs_0_), channel_id=1, source_target_pairs={{0,4},{4,0},{8,12},{12,8},{16,20},{20,16},{24,28},{28,24},{1,5},{5... | collective-permute-start | bytes 983048 | tf_op jit(solution)/shard_map/ppermute | solution.py:20
  55.2 7.0 %collective-permute-start.53 = (bf16[160,1024]{1,0:T(8,128)(2,1)S(1)}, bf16[160,1024]{1,0:T(8,128)(2,1)S(1)}, u32[]{:S(2)}, u32[]{:S(2)}) collective-permute-start(bf16[160,1024]{1,0:T(8,128)(2,1)S(1)} %get-tuple-element.33.refs_1_), channel_id=1, source_target_pairs={{0,4},{4,0},{8,12},{12,8},{16,20},{20,16},{24,28},{28,24},{1,5},{5... | collective-permute-start | bytes 983048 | tf_op jit(solution)/shard_map/ppermute | solution.py:20
  55.2 7.5 %collective-permute-start.60 = (bf16[96,1024]{1,0:T(8,128)(2,1)S(1)}, bf16[96,1024]{1,0:T(8,128)(2,1)S(1)}, u32[]{:S(2)}, u32[]{:S(2)}) collective-permute-start(bf16[96,1024]{1,0:T(8,128)(2,1)S(1)} %collective-permute-done.48.refs_8_), channel_id=1, source_target_pairs={{0,4},{4,0},{8,12},{12,8},{16,20},{20,16},{24,28},{28,24},{1,5},{5... | collective-permute-start | bytes 589832 | tf_op jit(solution)/shard_map/ppermute | solution.py:20
  60.3 4.3 %collective-permute-start.62 = (bf16[96,1024]{1,0:T(8,128)(2,1)S(1)}, bf16[96,1024]{1,0:T(8,128)(2,1)S(1)}, u32[]{:S(2)}, u32[]{:S(2)}) collective-permute-start(bf16[96,1024]{1,0:T(8,128)(2,1)S(1)} %collective-permute-done.50.refs_10_), channel_id=1, source_target_pairs={{0,4},{4,0},{8,12},{12,8},{16,20},{20,16},{24,28},{28,24},{1,5},{5... | collective-permute-start | bytes 589832 | tf_op jit(solution)/shard_map/ppermute | solution.py:20
  61.7 3.4 %collective-permute-start.61 = (bf16[96,1024]{1,0:T(8,128)(2,1)S(1)}, bf16[96,1024]{1,0:T(8,128)(2,1)S(1)}, u32[]{:S(2)}, u32[]{:S(2)}) collective-permute-start(bf16[96,1024]{1,0:T(8,128)(2,1)S(1)} %collective-permute-done.49.refs_9_), channel_id=1, source_target_pairs={{0,4},{4,0},{8,12},{12,8},{16,20},{20,16},{24,28},{28,24},{1,5},{5... | collective-permute-start | bytes 589832 | tf_op jit(solution)/shard_map/ppermute | solution.py:20
  61.7 5.1 %collective-permute-start.63 = (bf16[96,1024]{1,0:T(8,128)(2,1)S(1)}, bf16[96,1024]{1,0:T(8,128)(2,1)S(1)}, u32[]{:S(2)}, u32[]{:S(2)}) collective-permute-start(bf16[96,1024]{1,0:T(8,128)(2,1)S(1)} %collective-permute-done.51.refs_11_), channel_id=1, source_target_pairs={{0,4},{4,0},{8,12},{12,8},{16,20},{20,16},{24,28},{28,24},{1,5},{5... | collective-permute-start | bytes 589832 | tf_op jit(solution)/shard_map/ppermute | solution.py:20
  62.2 7.2 %collective-permute-start.68 = (bf16[96,1024]{1,0:T(8,128)(2,1)S(1)}, bf16[96,1024]{1,0:T(8,128)(2,1)S(1)}, u32[]{:S(2)}, u32[]{:S(2)}) collective-permute-start(bf16[96,1024]{1,0:T(8,128)(2,1)S(1)} %collective-permute-done.48.refs_8_), channel_id=1, source_target_pairs={{0,16},{4,12},{8,24},{12,4},{16,0},{20,28},{24,8},{28,20},{1,17},{... | collective-permute-start | bytes 589832 | tf_op jit(solution)/shard_map/ppermute | solution.py:234
  62.8 22.9 %collective-permute-start.32 = (bf16[192,1024]{1,0:T(8,128)(2,1)S(1)}, bf16[192,1024]{1,0:T(8,128)(2,1)S(1)}, u32[]{:S(2)}, u32[]{:S(2)}) collective-permute-start(bf16[192,1024]{1,0:T(8,128)(2,1)S(1)} %get-tuple-element.30.refs_1_), channel_id=1, source_target_pairs={{0,8},{4,20},{8,0},{12,28},{16,24},{20,4},{24,16},{28,12},{1,9},{5... | collective-permute-start | bytes 1179656 | tf_op jit(solution)/shard_map/ppermute | solution.py:234
  64.7 24.1 %collective-permute-start.4 = (bf16[320,1024]{1,0:T(8,128)(2,1)S(1)}, bf16[320,1024]{1,0:T(8,128)(2,1)S(1)}, u32[]{:S(2)}, u32[]{:S(2)}) collective-permute-start(bf16[320,1024]{1,0:T(8,128)(2,1)S(1)} %narrow.6.refs_0_), channel_id=1, source_target_pairs={{0,8},{4,20},{8,0},{12,28},{16,24},{20,4},{24,16},{28,12},{1,9},{5... | collective-permute-start | bytes 1966088 | tf_op jit(solution)/shard_map/ppermute | solution.py:234
  65.1 21.0 %collective-permute-start.33 = (bf16[192,1024]{1,0:T(8,128)(2,1)S(1)}, bf16[192,1024]{1,0:T(8,128)(2,1)S(1)}, u32[]{:S(2)}, u32[]{:S(2)}) collective-permute-start(bf16[192,1024]{1,0:T(8,128)(2,1)S(1)} %get-tuple-element.30.refs_1_), channel_id=1, source_target_pairs={{0,16},{4,12},{8,24},{12,4},{16,0},{20,28},{24,8},{28,20},{1,17},{... | collective-permute-start | bytes 1179656 | tf_op jit(solution)/shard_map/ppermute | solution.py:234
  66.8 19.4 %collective-permute-start.35 = (bf16[192,1024]{1,0:T(8,128)(2,1)S(1)}, bf16[192,1024]{1,0:T(8,128)(2,1)S(1)}, u32[]{:S(2)}, u32[]{:S(2)}) collective-permute-start(bf16[192,1024]{1,0:T(8,128)(2,1)S(1)} %get-tuple-element.30.refs_1_), channel_id=1, source_target_pairs={{0,4},{4,0},{8,12},{12,8},{16,20},{20,16},{24,28},{28,24},{1,5},{5... | collective-permute-start | bytes 1179656 | tf_op jit(solution)/shard_map/ppermute | solution.py:20
  69.4 15.2 %collective-permute-start.69 = (bf16[96,1024]{1,0:T(8,128)(2,1)S(1)}, bf16[96,1024]{1,0:T(8,128)(2,1)S(1)}, u32[]{:S(2)}, u32[]{:S(2)}) collective-permute-start(bf16[96,1024]{1,0:T(8,128)(2,1)S(1)} %collective-permute-done.50.refs_10_), channel_id=1, source_target_pairs={{0,8},{4,20},{8,0},{12,28},{16,24},{20,4},{24,16},{28,12},{1,9},{5... | collective-permute-start | bytes 589832 | tf_op jit(solution)/shard_map/ppermute | solution.py:234
  84.5 14.1 %collective-permute-start.5 = (bf16[320,1024]{1,0:T(8,128)(2,1)S(1)}, bf16[320,1024]{1,0:T(8,128)(2,1)S(1)}, u32[]{:S(2)}, u32[]{:S(2)}) collective-permute-start(bf16[320,1024]{1,0:T(8,128)(2,1)S(1)} %narrow.6.refs_0_), channel_id=1, source_target_pairs={{0,16},{4,12},{8,24},{12,4},{16,0},{20,28},{24,8},{28,20},{1,17},{... | collective-permute-start | bytes 1966088 | tf_op jit(solution)/shard_map/ppermute | solution.py:234
  85.7 13.6 %collective-permute-start.10 = (bf16[320,1024]{1,0:T(8,128)(2,1)S(1)}, bf16[320,1024]{1,0:T(8,128)(2,1)S(1)}, u32[]{:S(2)}, u32[]{:S(2)}) collective-permute-start(bf16[320,1024]{1,0:T(8,128)(2,1)S(1)} %narrow.6.refs_0_), channel_id=1, source_target_pairs={{0,4},{4,0},{8,12},{12,8},{16,20},{20,16},{24,28},{28,24},{1,5},{5... | collective-permute-start | bytes 1966088 | tf_op jit(solution)/shard_map/ppermute | solution.py:20
  88.1 10.5 %collective-permute-start.15 = (bf16[160,1024]{1,0:T(8,128)(2,1)S(1)}, bf16[160,1024]{1,0:T(8,128)(2,1)S(1)}, u32[]{:S(2)}, u32[]{:S(2)}) collective-permute-start(bf16[160,1024]{1,0:T(8,128)(2,1)S(1)} %collective-permute-done.6.refs_5_), channel_id=1, source_target_pairs={{0,4},{4,0},{8,12},{12,8},{16,20},{20,16},{24,28},{28,24},{1,5},{5... | collective-permute-start | bytes 983048 | tf_op jit(solution)/shard_map/ppermute | solution.py:20
  88.5 10.6 %collective-permute-start.16 = (bf16[160,1024]{1,0:T(8,128)(2,1)S(1)}, bf16[160,1024]{1,0:T(8,128)(2,1)S(1)}, u32[]{:S(2)}, u32[]{:S(2)}) collective-permute-start(bf16[160,1024]{1,0:T(8,128)(2,1)S(1)} %collective-permute-done.7.refs_6_), channel_id=1, source_target_pairs={{0,4},{4,0},{8,12},{12,8},{16,20},{20,16},{24,28},{28,24},{1,5},{5... | collective-permute-start | bytes 983048 | tf_op jit(solution)/shard_map/ppermute | solution.py:20
  88.8 10.9 %collective-permute-start.20 = (bf16[160,1024]{1,0:T(8,128)(2,1)S(1)}, bf16[160,1024]{1,0:T(8,128)(2,1)S(1)}, u32[]{:S(2)}, u32[]{:S(2)}) collective-permute-start(bf16[160,1024]{1,0:T(8,128)(2,1)S(1)} %collective-permute-done.6.refs_5_), channel_id=1, source_target_pairs={{0,8},{4,20},{8,0},{12,28},{16,24},{20,4},{24,16},{28,12},{1,9},{5... | collective-permute-start | bytes 983048 | tf_op jit(solution)/shard_map/ppermute | solution.py:234
  98.6 3.1 %collective-permute-start.58 = (bf16[160,1024]{1,0:T(8,128)(2,1)S(1)}, bf16[160,1024]{1,0:T(8,128)(2,1)S(1)}, u32[]{:S(2)}, u32[]{:S(2)}) collective-permute-start(bf16[160,1024]{1,0:T(8,128)(2,1)S(1)} %collective-permute-done.46.refs_6_), channel_id=1, source_target_pairs={{0,4},{4,0},{8,12},{12,8},{16,20},{20,16},{24,28},{28,24},{1,5},{5... | collective-permute-start | bytes 983048 | tf_op jit(solution)/shard_map/ppermute | solution.py:20
  99.1 4.1 %collective-permute-start.57 = (bf16[160,1024]{1,0:T(8,128)(2,1)S(1)}, bf16[160,1024]{1,0:T(8,128)(2,1)S(1)}, u32[]{:S(2)}, u32[]{:S(2)}) collective-permute-start(bf16[160,1024]{1,0:T(8,128)(2,1)S(1)} %collective-permute-done.45.refs_5_), channel_id=1, source_target_pairs={{0,4},{4,0},{8,12},{12,8},{16,20},{20,16},{24,28},{28,24},{1,5},{5... | collective-permute-start | bytes 983048 | tf_op jit(solution)/shard_map/ppermute | solution.py:20
  99.2 4.5 %collective-permute-start.59 = (bf16[160,1024]{1,0:T(8,128)(2,1)S(1)}, bf16[160,1024]{1,0:T(8,128)(2,1)S(1)}, u32[]{:S(2)}, u32[]{:S(2)}) collective-permute-start(bf16[160,1024]{1,0:T(8,128)(2,1)S(1)} %collective-permute-done.47.refs_7_), channel_id=1, source_target_pairs={{0,4},{4,0},{8,12},{12,8},{16,20},{20,16},{24,28},{28,24},{1,5},{5... | collective-permute-start | bytes 983048 | tf_op jit(solution)/shard_map/ppermute | solution.py:20
  99.7 24.8 %collective-permute-start.30 = (bf16[320,1024]{1,0:T(8,128)(2,1)S(1)}, bf16[320,1024]{1,0:T(8,128)(2,1)S(1)}, u32[]{:S(2)}, u32[]{:S(2)}) collective-permute-start(bf16[320,1024]{1,0:T(8,128)(2,1)S(1)} %get-tuple-element.29.refs_0_), channel_id=1, source_target_pairs={{0,16},{4,12},{8,24},{12,4},{16,0},{20,28},{24,8},{28,20},{1,17},{... | collective-permute-start | bytes 1966088 | tf_op jit(solution)/shard_map/ppermute | solution.py:234
  100.8 24.9 %collective-permute-start.31 = (bf16[320,1024]{1,0:T(8,128)(2,1)S(1)}, bf16[320,1024]{1,0:T(8,128)(2,1)S(1)}, u32[]{:S(2)}, u32[]{:S(2)}) collective-permute-start(bf16[320,1024]{1,0:T(8,128)(2,1)S(1)} %get-tuple-element.29.refs_0_), channel_id=1, source_target_pairs={{0,8},{4,20},{8,0},{12,28},{16,24},{20,4},{24,16},{28,12},{1,9},{5... | collective-permute-start | bytes 1966088 | tf_op jit(solution)/shard_map/ppermute | solution.py:234
  101.8 22.2 %collective-permute-start.64 = (bf16[160,1024]{1,0:T(8,128)(2,1)S(1)}, bf16[160,1024]{1,0:T(8,128)(2,1)S(1)}, u32[]{:S(2)}, u32[]{:S(2)}) collective-permute-start(bf16[160,1024]{1,0:T(8,128)(2,1)S(1)} %collective-permute-done.44.refs_4_), channel_id=1, source_target_pairs={{0,16},{4,12},{8,24},{12,4},{16,0},{20,28},{24,8},{28,20},{1,17},{... | collective-permute-start | bytes 983048 | tf_op jit(solution)/shard_map/ppermute | solution.py:234
  103.2 20.8 %collective-permute-start.65 = (bf16[160,1024]{1,0:T(8,128)(2,1)S(1)}, bf16[160,1024]{1,0:T(8,128)(2,1)S(1)}, u32[]{:S(2)}, u32[]{:S(2)}) collective-permute-start(bf16[160,1024]{1,0:T(8,128)(2,1)S(1)} %collective-permute-done.46.refs_6_), channel_id=1, source_target_pairs={{0,8},{4,20},{8,0},{12,28},{16,24},{20,4},{24,16},{28,12},{1,9},{5... | collective-permute-start | bytes 983048 | tf_op jit(solution)/shard_map/ppermute | solution.py:234
  103.7 22.1 %collective-permute-start.34 = (bf16[320,1024]{1,0:T(8,128)(2,1)S(1)}, bf16[320,1024]{1,0:T(8,128)(2,1)S(1)}, u32[]{:S(2)}, u32[]{:S(2)}) collective-permute-start(bf16[320,1024]{1,0:T(8,128)(2,1)S(1)} %get-tuple-element.29.refs_0_), channel_id=1, source_target_pairs={{0,4},{4,0},{8,12},{12,8},{16,20},{20,16},{24,28},{28,24},{1,5},{5... | collective-permute-start | bytes 1966088 | tf_op jit(solution)/shard_map/ppermute | solution.py:20
  124.0 2.4 %collective-permute-start.39 = (bf16[192,1024]{1,0:T(8,128)(2,1)S(1)}, bf16[192,1024]{1,0:T(8,128)(2,1)S(1)}, u32[]{:S(2)}, u32[]{:S(2)}) collective-permute-start(bf16[192,1024]{1,0:T(8,128)(2,1)S(1)} %collective-permute-done.33.refs_5_), channel_id=1, source_target_pairs={{0,4},{4,0},{8,12},{12,8},{16,20},{20,16},{24,28},{28,24},{1,5},{5... | collective-permute-start | bytes 1179656 | tf_op jit(solution)/shard_map/ppermute | solution.py:20
  124.5 7.8 %collective-permute-start.41 = (bf16[192,1024]{1,0:T(8,128)(2,1)S(1)}, bf16[192,1024]{1,0:T(8,128)(2,1)S(1)}, u32[]{:S(2)}, u32[]{:S(2)}) collective-permute-start(bf16[192,1024]{1,0:T(8,128)(2,1)S(1)} %collective-permute-done.32.refs_4_), channel_id=1, source_target_pairs={{0,16},{4,12},{8,24},{12,4},{16,0},{20,28},{24,8},{28,20},{1,17},{... | collective-permute-start | bytes 1179656 | tf_op jit(solution)/shard_map/ppermute | solution.py:234
  125.7 8.7 %collective-permute-start.13 = (bf16[320,1024]{1,0:T(8,128)(2,1)S(1)}, bf16[320,1024]{1,0:T(8,128)(2,1)S(1)}, u32[]{:S(2)}, u32[]{:S(2)}) collective-permute-start(bf16[320,1024]{1,0:T(8,128)(2,1)S(1)} %collective-permute-done.4.refs_3_), channel_id=1, source_target_pairs={{0,4},{4,0},{8,12},{12,8},{16,20},{20,16},{24,28},{28,24},{1,5},{5... | collective-permute-start | bytes 1966088 | tf_op jit(solution)/shard_map/ppermute | solution.py:20
  125.9 8.0 %collective-permute-start.66 = (bf16[160,1024]{1,0:T(8,128)(2,1)S(1)}, bf16[160,1024]{1,0:T(8,128)(2,1)S(1)}, u32[]{:S(2)}, u32[]{:S(2)}) collective-permute-start(bf16[160,1024]{1,0:T(8,128)(2,1)S(1)} %collective-permute-done.64.refs_1_), channel_id=1, source_target_pairs={{0,4},{4,0},{8,12},{12,8},{16,20},{20,16},{24,28},{28,24},{1,5},{5... | collective-permute-start | bytes 983048 | tf_op jit(solution)/shard_map/ppermute | solution.py:20
  126.2 7.6 %collective-permute-start.67 = (bf16[160,1024]{1,0:T(8,128)(2,1)S(1)}, bf16[160,1024]{1,0:T(8,128)(2,1)S(1)}, u32[]{:S(2)}, u32[]{:S(2)}) collective-permute-start(bf16[160,1024]{1,0:T(8,128)(2,1)S(1)} %collective-permute-done.65.refs_2_), channel_id=1, source_target_pairs={{0,4},{4,0},{8,12},{12,8},{16,20},{20,16},{24,28},{28,24},{1,5},{5... | collective-permute-start | bytes 983048 | tf_op jit(solution)/shard_map/ppermute | solution.py:20
  126.4 18.1 %collective-permute-start.19 = (bf16[320,1024]{1,0:T(8,128)(2,1)S(1)}, bf16[320,1024]{1,0:T(8,128)(2,1)S(1)}, u32[]{:S(2)}, u32[]{:S(2)}) collective-permute-start(bf16[320,1024]{1,0:T(8,128)(2,1)S(1)} %collective-permute-done.4.refs_3_), channel_id=1, source_target_pairs={{0,16},{4,12},{8,24},{12,4},{16,0},{20,28},{24,8},{28,20},{1,17},{... | collective-permute-start | bytes 1966088 | tf_op jit(solution)/shard_map/ppermute | solution.py:234
  132.3 13.1 %collective-permute-start.40 = (bf16[320,1024]{1,0:T(8,128)(2,1)S(1)}, bf16[320,1024]{1,0:T(8,128)(2,1)S(1)}, u32[]{:S(2)}, u32[]{:S(2)}) collective-permute-start(bf16[320,1024]{1,0:T(8,128)(2,1)S(1)} %collective-permute-done.30.refs_2_), channel_id=1, source_target_pairs={{0,8},{4,20},{8,0},{12,28},{16,24},{20,4},{24,16},{28,12},{1,9},{5... | collective-permute-start | bytes 1966088 | tf_op jit(solution)/shard_map/ppermute | solution.py:234
  133.9 12.3 %collective-permute-start.14 = (bf16[320,1024]{1,0:T(8,128)(2,1)S(1)}, bf16[320,1024]{1,0:T(8,128)(2,1)S(1)}, u32[]{:S(2)}, u32[]{:S(2)}) collective-permute-start(bf16[320,1024]{1,0:T(8,128)(2,1)S(1)} %collective-permute-done.5.refs_4_), channel_id=1, source_target_pairs={{0,4},{4,0},{8,12},{12,8},{16,20},{20,16},{24,28},{28,24},{1,5},{5... | collective-permute-start | bytes 1966088 | tf_op jit(solution)/shard_map/ppermute | solution.py:20
  133.9 12.3 %collective-permute-start.36 = (bf16[320,1024]{1,0:T(8,128)(2,1)S(1)}, bf16[320,1024]{1,0:T(8,128)(2,1)S(1)}, u32[]{:S(2)}, u32[]{:S(2)}) collective-permute-start(bf16[320,1024]{1,0:T(8,128)(2,1)S(1)} %collective-permute-done.30.refs_2_), channel_id=1, source_target_pairs={{0,4},{4,0},{8,12},{12,8},{16,20},{20,16},{24,28},{28,24},{1,5},{5... | collective-permute-start | bytes 1966088 | tf_op jit(solution)/shard_map/ppermute | solution.py:20
  134.4 12.3 %collective-permute-start.37 = (bf16[320,1024]{1,0:T(8,128)(2,1)S(1)}, bf16[320,1024]{1,0:T(8,128)(2,1)S(1)}, u32[]{:S(2)}, u32[]{:S(2)}) collective-permute-start(bf16[320,1024]{1,0:T(8,128)(2,1)S(1)} %collective-permute-done.31.refs_3_), channel_id=1, source_target_pairs={{0,4},{4,0},{8,12},{12,8},{16,20},{20,16},{24,28},{28,24},{1,5},{5... | collective-permute-start | bytes 1966088 | tf_op jit(solution)/shard_map/ppermute | solution.py:20
  144.5 16.6 %collective-permute-start.22 = (bf16[320,1024]{1,0:T(8,128)(2,1)S(1)}, bf16[320,1024]{1,0:T(8,128)(2,1)S(1)}, u32[]{:S(2)}, u32[]{:S(2)}) collective-permute-start(bf16[320,1024]{1,0:T(8,128)(2,1)S(1)} %collective-permute-done.19.refs_1_), channel_id=1, source_target_pairs={{0,4},{4,0},{8,12},{12,8},{16,20},{20,16},{24,28},{28,24},{1,5},{5... | collective-permute-start | bytes 1966088 | tf_op jit(solution)/shard_map/ppermute | solution.py:20
  145.4 17.1 %collective-permute-start.42 = (bf16[320,1024]{1,0:T(8,128)(2,1)S(1)}, bf16[320,1024]{1,0:T(8,128)(2,1)S(1)}, u32[]{:S(2)}, u32[]{:S(2)}) collective-permute-start(bf16[320,1024]{1,0:T(8,128)(2,1)S(1)} %collective-permute-done.40.refs_1_), channel_id=1, source_target_pairs={{0,4},{4,0},{8,12},{12,8},{16,20},{20,16},{24,28},{28,24},{1,5},{5... | collective-permute-start | bytes 1966088 | tf_op jit(solution)/shard_map/ppermute | solution.py:20
  146.1 16.3 %collective-permute-start.43 = (bf16[192,1024]{1,0:T(8,128)(2,1)S(1)}, bf16[192,1024]{1,0:T(8,128)(2,1)S(1)}, u32[]{:S(2)}, u32[]{:S(2)}) collective-permute-start(bf16[192,1024]{1,0:T(8,128)(2,1)S(1)} %collective-permute-done.41.refs_2_), channel_id=1, source_target_pairs={{0,4},{4,0},{8,12},{12,8},{16,20},{20,16},{24,28},{28,24},{1,5},{5... | collective-permute-start | bytes 1179656 | tf_op jit(solution)/shard_map/ppermute | solution.py:20
  146.1 14.9 %collective-permute-start.23 = (bf16[160,1024]{1,0:T(8,128)(2,1)S(1)}, bf16[160,1024]{1,0:T(8,128)(2,1)S(1)}, u32[]{:S(2)}, u32[]{:S(2)}) collective-permute-start(bf16[160,1024]{1,0:T(8,128)(2,1)S(1)} %collective-permute-done.20.refs_2_), channel_id=1, source_target_pairs={{0,4},{4,0},{8,12},{12,8},{16,20},{20,16},{24,28},{28,24},{1,5},{5... | collective-permute-start | bytes 983048 | tf_op jit(solution)/shard_map/ppermute | solution.py:20
  146.6 14.4 %collective-permute-start.24 = (bf16[32,1024]{1,0:T(8,128)(2,1)S(1)}, bf16[32,1024]{1,0:T(8,128)(2,1)S(1)}, u32[]{:S(2)}, u32[]{:S(2)}) collective-permute-start(bf16[32,1024]{1,0:T(8,128)(2,1)S(1)} %collective-permute-done.21.refs_3_), channel_id=1, source_target_pairs={{0,4},{4,0},{8,12},{12,8},{16,20},{20,16},{24,28},{28,24},{1,5},{5... | collective-permute-start | bytes 196616 | tf_op jit(solution)/shard_map/ppermute | solution.py:20
  (8 other events, 15.6 us)
